TPU v7x, 32 devices: a 4x4x1 block of a 4x4x8 slice. The times are simulated.
32 devices in a mesh: rep: 1 (over z), mp: 4 (over y), tok: 8 (over x, core).
Axes of the slice: x: 4, y: 4, z: 1, core: 2. Of those that a mesh axis runs over, the one named last changes fastest.
The devices are a block of a 4x4x8 slice.
Arguments:
- x_in: bfloat16 [2, 8192, 2048], P(None, ('rep', 'tok', 'mp'))
- seg_ids: int32 [2, 8192], P(None, ('rep', 'tok', 'mp'))
- g_attn: bfloat16 [2, 2048], replicated
- w_q: bfloat16 [2, 2048, 32, 64], P(None, 'tok', 'mp')
- w_k: bfloat16 [2, 2048, 8, 64], P(None, 'tok', 'mp')
- w_v: bfloat16 [2, 2048, 8, 64], P(None, 'tok', 'mp')
- w_o: bfloat16 [2, 32, 64, 2048], P(None, 'mp', None, 'tok')
- g_mlp: bfloat16 [2, 2048], replicated
- w_gate: bfloat16 [2, 2048, 8192], P(None, 'tok', 'mp')
- w_up: bfloat16 [2, 2048, 8192], P(None, 'tok', 'mp')
- w_down: bfloat16 [2, 8192, 2048], P(None, 'mp', 'tok')
Outputs:
- output: float32 [2, 8192, 2048], P(None, ('rep', 'tok', 'mp'))
All inputs are finite; a program needn't handle non-finite values.
Results may differ from a plain program's by a relative error of at most 0.00825783.
Values are sent between devices in bfloat16 or wider.
A program may use at most 768 MiB of HBM per device.

v0:
```python
import jax
import jax.numpy as jnp
from jax import lax
from jax.sharding import PartitionSpec as P

NORM_EPS = 1e-5
ROPE_BASE = 10000.0
NEG_BIG = -1e30


def rms_norm(resid, gain_vec):
    mean_sq = jnp.mean(resid * resid, axis=-1, keepdims=True)
    return (resid * lax.rsqrt(mean_sq + NORM_EPS) * gain_vec.astype(jnp.float32)).astype(jnp.bfloat16)


def seg_positions(seg_rows):
    positions = jnp.arange(seg_rows.shape[-1], dtype=jnp.int32)
    previous = jnp.concatenate([seg_rows[..., :1] - 1, seg_rows[..., :-1]], axis=-1)
    start_at = jnp.where(seg_rows != previous, positions, 0)
    return positions - lax.cummax(start_at, axis=seg_rows.ndim - 1)


def rope_tables(positions, head_dim):
    half_dim = head_dim // 2
    inv_freq = ROPE_BASE ** (-2.0 * jnp.arange(half_dim, dtype=jnp.float32) / head_dim)
    angles = positions.astype(jnp.float32)[..., None] * inv_freq
    return jnp.cos(angles), jnp.sin(angles)


def apply_rope(values, cos_t, sin_t):
    half_dim = values.shape[-1] // 2
    first_half = values[..., :half_dim]
    second_half = values[..., half_dim:]
    return jnp.concatenate([first_half * cos_t - second_half * sin_t, second_half * cos_t + first_half * sin_t], axis=-1)


def attend(q_rot, k_rot, v_val, allowed):
    scores = jnp.einsum('msngd,mtnd->mnsgt', q_rot, k_rot, preferred_element_type=jnp.float32) * q_rot.shape[-1] ** -0.5
    scores = jnp.where(allowed[:, None, :, None, :], scores, NEG_BIG)
    probs_bf = jax.nn.softmax(scores, axis=-1).astype(jnp.bfloat16)
    return jnp.einsum('mnsgt,mtnd->mnsgd', probs_bf, v_val, preferred_element_type=jnp.float32).astype(jnp.bfloat16)


def solution(mesh):
    act_spec = P(None, ('rep', 'tok', 'mp'), None)
    seg_spec = P(None, ('rep', 'tok', 'mp'))
    gain_spec = P(None, None)
    head_in = P(None, 'tok', 'mp', None)
    head_out = P(None, 'mp', None, 'tok')
    ffn_in = P(None, 'tok', 'mp')
    ffn_out = P(None, 'mp', 'tok')

    def device_fn(x_in, seg_ids, g_attn, w_q, w_k, w_v, w_o, g_mlp, w_gate, w_up, w_down):
        micro_n = x_in.shape[0]
        head_dim = w_q.shape[3]
        kv_heads = w_k.shape[2]
        groups = w_q.shape[2] // kv_heads
        seg_blk = lax.all_gather(seg_ids, 'mp', axis=1, tiled=True)
        blk_len = seg_blk.shape[1]
        tok_order = jnp.arange(blk_len)
        allowed = (seg_blk[:, :, None] == seg_blk[:, None, :]) & (tok_order[None, :] <= tok_order[:, None])
        cos_t, sin_t = rope_tables(seg_positions(seg_blk), head_dim)
        cos_t = cos_t[:, :, None, :]
        sin_t = sin_t[:, :, None, :]
        residual = x_in.astype(jnp.float32)
        for layer_idx in range(w_q.shape[0]):
            wq_full = lax.all_gather(w_q[layer_idx], 'tok', axis=0, tiled=True)
            wk_full = lax.all_gather(w_k[layer_idx], 'tok', axis=0, tiled=True)
            wv_full = lax.all_gather(w_v[layer_idx], 'tok', axis=0, tiled=True)
            wo_full = lax.all_gather(w_o[layer_idx], 'tok', axis=2, tiled=True)
            wg_full = lax.all_gather(w_gate[layer_idx], 'tok', axis=0, tiled=True)
            wu_full = lax.all_gather(w_up[layer_idx], 'tok', axis=0, tiled=True)
            wd_full = lax.all_gather(w_down[layer_idx], 'tok', axis=1, tiled=True)
            embed_dim = wo_full.shape[2]

            hidden = rms_norm(residual, g_attn[layer_idx])
            h_blk = lax.all_gather(hidden, 'mp', axis=1, tiled=True)
            q_lin = jnp.einsum('mse,end->msnd', h_blk, wq_full, preferred_element_type=jnp.float32)
            k_lin = jnp.einsum('mse,end->msnd', h_blk, wk_full, preferred_element_type=jnp.float32)
            v_val = jnp.einsum('mse,end->msnd', h_blk, wv_full, preferred_element_type=jnp.float32).astype(jnp.bfloat16)
            q_rot = apply_rope(q_lin, cos_t, sin_t).astype(jnp.bfloat16).reshape(micro_n, blk_len, kv_heads, groups, head_dim)
            k_rot = apply_rope(k_lin, cos_t, sin_t).astype(jnp.bfloat16)
            attn_out = attend(q_rot, k_rot, v_val, allowed)
            part_sum = jnp.einsum('mnsgd,ngde->mse', attn_out, wo_full.reshape(kv_heads, groups, head_dim, embed_dim), preferred_element_type=jnp.float32)
            residual = residual + lax.psum_scatter(part_sum, 'mp', scatter_dimension=1, tiled=True)

            hidden = rms_norm(residual, g_mlp[layer_idx])
            h_blk = lax.all_gather(hidden, 'mp', axis=1, tiled=True)
            gate_val = jnp.einsum('mse,ef->msf', h_blk, wg_full, preferred_element_type=jnp.float32)
            up_val = jnp.einsum('mse,ef->msf', h_blk, wu_full, preferred_element_type=jnp.float32)
            act_val = (jax.nn.silu(gate_val) * up_val).astype(jnp.bfloat16)
            part_sum = jnp.einsum('msf,fe->mse', act_val, wd_full, preferred_element_type=jnp.float32)
            residual = residual + lax.psum_scatter(part_sum, 'mp', scatter_dimension=1, tiled=True)
        return residual

    return jax.shard_map(
        device_fn,
        mesh=mesh,
        in_specs=(act_spec, seg_spec, gain_spec, head_in, head_in, head_in, head_out, gain_spec, ffn_in, ffn_in, ffn_out),
        out_specs=act_spec,
        check_vma=False,
    )
```

profile of v0, /device:TPU:97, one launch (start us, length us, event | category | flops | bytes accessed | tf_op | source)
XLA Modules:
  0.0 1510.9 jit_solution(17091892007875475765)
XLA Ops:
  6.6 2.0 fusion.100
  8.7 2.1 fusion.46
  10.8 1.4 slice_convert_fusion.1
  12.2 3.4 fusion.48
  15.8 0.8 fusion.101
  17.1 12.4 all_gather.57
  29.6 0.6 reduce-window.6
  30.7 0.6 fusion.103
  31.3 20.4 %all-gather.1 = bf16[1,2048,2,64]{1,3,2,0:T(8,128)(2,1)} all-gather(bf16[1,256,2,64]{1,3,2,0:T(8,128)(2,1)S(1)} %get-tuple-element.30), channel_id=3, replica_groups=mesh['rep'=1,'mp'=4,'tok'=8] {'tok'}, dimensions={1}, use_global_device_ids=true | all-gather | bytes 589824 | tf_op jit(solution)/shard_map/all_gather | solution.py:68
  51.7 1.7 compare_and_fusion
  53.4 0.7 fusion.102
  54.0 24.6 %all-gather.2 = bf16[1,2048,2,64]{1,3,2,0:T(8,128)(2,1)} all-gather(bf16[1,256,2,64]{1,3,2,0:T(8,128)(2,1)S(1)} %get-tuple-element.28), channel_id=4, replica_groups=mesh['rep'=1,'mp'=4,'tok'=8] {'tok'}, dimensions={1}, use_global_device_ids=true | all-gather | bytes 589824 | tf_op jit(solution)/shard_map/all_gather | solution.py:69
  78.6 1.0 multiply_cosine_fusion
  79.7 40.2 %all-gather.29.cloned.1.call-done = bf16[2,1024,2048]{2,1,0:T(8,128)(2,1)} async-done(((bf16[2,256,2048]{2,1,0:T(8,128)(2,1)}), bf16[2,1024,2048]{2,1,0:T(8,128)(2,1)}) %all-gather.29.cloned.1.call-update) | async-done | bytes 8388624 | tf_op jit(solution)/shard_map/all_gather | solution.py:77
  119.9 7.8 fusion.40
  127.6 2.0 subtract_convert_fusion.1
  129.7 2.9 fusion.38
  132.6 0.9 subtract_convert_fusion.3
  133.5 3.7 fusion.68
  137.2 2.4 copy.36
  139.6 34.3 %fusion.104 = (f32[2,2,1024,4]{2,3,1,0:T(4,128)S(1)}, f32[2,2,1024,4,1024]{2,4,3,1,0:T(8,128)}) fusion(pred[2,1024,1024]{1,2,0:T(8,128)(4,1)S(1)} %compare_and_fusion, bf16[2,1024,2,4,32]{1,4,3,2,0:T(8,128)(2,1)} %bitcast.156, bf16[2,1024,2,4,32]{1,4,3,2,0:T(8,128)(2,1)} %bitcast.155, bf16[2,1024,2,32]{1,3,2,0:T(8,128)(2,1)} %get-tuple-element.22, ...), kind=kOutput, calls=%fused_computation.129 | convolution fusion | flops 2219836416 | bytes 71892992 | tf_op jit(solution)/shard_map/sub | solution.py:40
  173.9 30.3 %convolution_bitcast_fusion.1 = f32[2,1024,2048]{2,1,0:T(8,128)} fusion(bf16[2,4,64,2048,1]{3,2,1,0,4:T(8,128)(2,1)} %bitcast.164, bf16[2,1024,2,64,1]{3,2,1,0,4:T(2,128)(2,1)S(1)} %bitcast.152, f32[2,2,1024,4,1024]{2,4,3,1,0:T(8,128)} %get-tuple-element.38, f32[2,2,1024,4]{2,3,1,0:T(4,128)S(1)} %get-tuple-element.37), kind=kOutput, calls=%fused_computation.50 | convolution fusion | flops 6477053952 | bytes 86573056 | tf_op jit(solution)/shard_map/mnsgd,ngde->mse/dot_general | solution.py:84
  204.3 3.3 fusion.99
  207.7 0.6 slice_convert_fusion
  208.3 142.4 %reduce-scatter.5.cloned.1.call-done = f32[2,256,2048]{2,1,0:T(8,128)} async-done(((f32[2,1024,2048]{2,1,0:T(8,128)}), f32[2,256,2048]{2,1,0:T(8,128)}) %reduce-scatter.5.cloned.1.call-update) | async-done | bytes 4194320 | tf_op jit(solution)/shard_map/reduce_scatter | solution.py:85
  350.7 3.0 multiply_reduce_fusion.2
  354.2 2.0 multiply_convert_fusion.4
  356.3 3.1 fusion.98
  359.6 3.0 fusion.97
  362.8 36.7 %all-gather.41.cloned.1.call-done = bf16[1,2048,2048]{2,1,0:T(8,128)(2,1)} async-done(((bf16[1,256,2048]{2,1,0:T(8,128)(2,1)}), bf16[1,2048,2048]{2,1,0:T(8,128)(2,1)}) %all-gather.41.cloned.1.call-update) | async-done | bytes 8388624 | tf_op jit(solution)/shard_map/all_gather | solution.py:71
  399.5 81.9 %all-gather.31.cloned.1.call-done = bf16[2,1024,2048]{2,1,0:T(8,128)(2,1)} async-done(((bf16[2,256,2048]{2,1,0:T(8,128)(2,1)}), bf16[2,1024,2048]{2,1,0:T(8,128)(2,1)}) %all-gather.31.cloned.1.call-update) | async-done | bytes 8388624 | tf_op jit(solution)/shard_map/all_gather | solution.py:88
  481.3 24.5 %fusion.34 = f32[2,1024,2048]{2,1,0:T(8,128)} fusion(bf16[2,1024,2048]{2,1,0:T(8,128)(2,1)} %all-gather.31.cloned.1.call-done, bf16[1,2048,2048]{2,1,0:T(8,128)(2,1)} %all-gather.41.cloned.1.call-done), kind=kOutput, calls=%fused_computation.38 | convolution fusion | flops 17179869184 | bytes 33554432 | tf_op jit(solution)/shard_map/mse,ef->msf/dot_general | solution.py:89
  505.9 25.6 %all-gather.43.cloned.1.call-done = bf16[1,2048,2048]{2,1,0:T(8,128)(2,1)} async-done(((bf16[1,256,2048]{2,1,0:T(8,128)(2,1)}), bf16[1,2048,2048]{2,1,0:T(8,128)(2,1)}) %all-gather.43.cloned.1.call-update) | async-done | bytes 8388624 | tf_op jit(solution)/shard_map/all_gather | solution.py:72
  531.5 26.1 %multiply_convert_fusion.1 = bf16[2,1024,2048]{2,1,0:T(8,128)(2,1)} fusion(f32[2,1024,2048]{2,1,0:T(8,128)} %fusion.34, bf16[2,1024,2048]{2,1,0:T(8,128)(2,1)} %all-gather.31.cloned.1.call-done, bf16[1,2048,2048]{2,1,0:T(8,128)(2,1)} %all-gather.43.cloned.1.call-done), kind=kOutput, calls=%fused_computation.21 | convolution fusion | flops 17205035008 | bytes 41943040 | tf_op jit(solution)/shard_map/mse,ef->msf/dot_general | solution.py:90
  557.6 26.1 %all-gather.45.cloned.1.call-done = bf16[1,2048,2048]{2,1,0:T(8,128)(2,1)} async-done(((bf16[1,2048,256]{2,1,0:T(8,128)(2,1)}), bf16[1,2048,2048]{2,1,0:T(8,128)(2,1)}) %all-gather.45.cloned.1.call-update) | async-done | bytes 8388624 | tf_op jit(solution)/shard_map/all_gather | solution.py:73
  583.6 24.3 %fusion.28 = f32[2,1024,2048]{2,1,0:T(8,128)} fusion(bf16[2,1024,2048]{2,1,0:T(8,128)(2,1)} %multiply_convert_fusion.1, bf16[1,2048,2048]{2,1,0:T(8,128)(2,1)} %all-gather.45.cloned.1.call-done), kind=kOutput, calls=%fused_computation.34 | convolution fusion | flops 17179869184 | bytes 33554432 | tf_op jit(solution)/shard_map/msf,fe->mse/dot_general | solution.py:92
  608.7 145.1 %reduce-scatter.7.cloned.1.call-done = f32[2,256,2048]{2,1,0:T(8,128)} async-done(((f32[2,1024,2048]{2,1,0:T(8,128)}), f32[2,256,2048]{2,1,0:T(8,128)}) %reduce-scatter.7.cloned.1.call-update) | async-done | bytes 4194320 | tf_op jit(solution)/shard_map/reduce_scatter | solution.py:93
  753.9 4.2 multiply_reduce_fusion.1
  758.1 2.0 copy-done.3
  760.1 1.7 multiply_convert_fusion.3
  762.6 19.4 %all-gather.8 = bf16[1,2048,2,64]{1,3,2,0:T(8,128)(2,1)S(1)} all-gather(bf16[1,256,2,64]{1,3,2,0:T(8,128)(2,1)S(1)} %copy-done.13), channel_id=10, replica_groups=mesh['rep'=1,'mp'=4,'tok'=8] {'tok'}, dimensions={1}, use_global_device_ids=true | all-gather | bytes 589824 | tf_op jit(solution)/shard_map/all_gather | solution.py:68
  782.0 22.8 %all-gather.9 = bf16[1,2048,2,64]{1,3,2,0:T(8,128)(2,1)S(1)} all-gather(bf16[1,256,2,64]{1,3,2,0:T(8,128)(2,1)S(1)} %copy-done.14), channel_id=11, replica_groups=mesh['rep'=1,'mp'=4,'tok'=8] {'tok'}, dimensions={1}, use_global_device_ids=true | all-gather | bytes 589824 | tf_op jit(solution)/shard_map/all_gather | solution.py:69
  804.9 58.6 %all-gather.33.cloned.1.call-done = bf16[2,1024,2048]{2,1,0:T(8,128)(2,1)} async-done(((bf16[2,256,2048]{2,1,0:T(8,128)(2,1)}), bf16[2,1024,2048]{2,1,0:T(8,128)(2,1)}) %all-gather.33.cloned.1.call-update) | async-done | bytes 8388624 | tf_op jit(solution)/shard_map/all_gather | solution.py:77
  863.5 7.8 fusion.26
  871.3 2.1 subtract_convert_fusion
  873.4 2.9 fusion.24
  876.3 0.9 subtract_convert_fusion.2
  877.1 3.7 fusion.71
  880.8 2.4 copy.37
  883.2 34.3 %fusion.105 = (f32[2,2,1024,4]{2,3,1,0:T(4,128)S(1)}, f32[2,2,1024,4,1024]{2,4,3,1,0:T(8,128)}) fusion(pred[2,1024,1024]{1,2,0:T(8,128)(4,1)S(1)} %copy-done.9, bf16[2,1024,2,4,32]{1,4,3,2,0:T(8,128)(2,1)} %bitcast.154, bf16[2,1024,2,4,32]{1,4,3,2,0:T(8,128)(2,1)} %bitcast.153, bf16[2,1024,2,32]{1,3,2,0:T(8,128)(2,1)} %get-tuple-element.20, ...), kind=kOutput, calls=%fused_computation.130 | convolution fusion | flops 2219836416 | bytes 71892992 | tf_op jit(solution)/shard_map/sub | solution.py:40
  917.5 30.3 %convolution_bitcast_fusion = f32[2,1024,2048]{2,1,0:T(8,128)} fusion(bf16[2,4,64,2048,1]{3,2,1,0,4:T(8,128)(2,1)} %bitcast.165, bf16[2,1024,2,64,1]{3,2,1,0,4:T(2,128)(2,1)S(1)} %bitcast.151, f32[2,2,1024,4,1024]{2,4,3,1,0:T(8,128)} %get-tuple-element.40, f32[2,2,1024,4]{2,3,1,0:T(4,128)S(1)} %get-tuple-element.39), kind=kOutput, calls=%fused_computation.49 | convolution fusion | flops 6477053952 | bytes 86573056 | tf_op jit(solution)/shard_map/mnsgd,ngde->mse/dot_general | solution.py:84
  948.5 145.8 %reduce-scatter.9.cloned.1.call-done = f32[2,256,2048]{2,1,0:T(8,128)} async-done(((f32[2,1024,2048]{2,1,0:T(8,128)}), f32[2,256,2048]{2,1,0:T(8,128)}) %reduce-scatter.9.cloned.1.call-update) | async-done | bytes 4194320 | tf_op jit(solution)/shard_map/reduce_scatter | solution.py:85
  1094.3 4.0 multiply_reduce_fusion
  1098.3 2.0 copy-done.1
  1100.3 1.8 multiply_convert_fusion.2
  1103.5 39.5 %all-gather.51.cloned.1.call-done = bf16[1,2048,2048]{2,1,0:T(8,128)(2,1)} async-done(((bf16[1,256,2048]{2,1,0:T(8,128)(2,1)}), bf16[1,2048,2048]{2,1,0:T(8,128)(2,1)}) %all-gather.51.cloned.1.call-update) | async-done | bytes 8388624 | tf_op jit(solution)/shard_map/all_gather | solution.py:71
  1143.0 81.9 %all-gather.35.cloned.1.call-done = bf16[2,1024,2048]{2,1,0:T(8,128)(2,1)} async-done(((bf16[2,256,2048]{2,1,0:T(8,128)(2,1)}), bf16[2,1024,2048]{2,1,0:T(8,128)(2,1)}) %all-gather.35.cloned.1.call-update) | async-done | bytes 8388624 | tf_op jit(solution)/shard_map/all_gather | solution.py:88
  1224.9 24.4 %fusion.20 = f32[2,1024,2048]{2,1,0:T(8,128)} fusion(bf16[2,1024,2048]{2,1,0:T(8,128)(2,1)} %all-gather.35.cloned.1.call-done, bf16[1,2048,2048]{2,1,0:T(8,128)(2,1)} %all-gather.51.cloned.1.call-done), kind=kOutput, calls=%fused_computation.26 | convolution fusion | flops 17179869184 | bytes 33554432 | tf_op jit(solution)/shard_map/mse,ef->msf/dot_general | solution.py:89
  1249.3 25.6 %all-gather.53.cloned.1.call-done = bf16[1,2048,2048]{2,1,0:T(8,128)(2,1)} async-done(((bf16[1,256,2048]{2,1,0:T(8,128)(2,1)}), bf16[1,2048,2048]{2,1,0:T(8,128)(2,1)}) %all-gather.53.cloned.1.call-update) | async-done | bytes 8388624 | tf_op jit(solution)/shard_map/all_gather | solution.py:72
  1274.9 26.1 %multiply_convert_fusion = bf16[2,1024,2048]{2,1,0:T(8,128)(2,1)} fusion(f32[2,1024,2048]{2,1,0:T(8,128)} %fusion.20, bf16[2,1024,2048]{2,1,0:T(8,128)(2,1)} %all-gather.35.cloned.1.call-done, bf16[1,2048,2048]{2,1,0:T(8,128)(2,1)} %all-gather.53.cloned.1.call-done), kind=kOutput, calls=%fused_computation.20 | convolution fusion | flops 17205035008 | bytes 41943040 | tf_op jit(solution)/shard_map/mse,ef->msf/dot_general | solution.py:90
  1301.0 25.9 %all-gather.55.cloned.1.call-done = bf16[1,2048,2048]{2,1,0:T(8,128)(2,1)} async-done(((bf16[1,2048,256]{2,1,0:T(8,128)(2,1)}), bf16[1,2048,2048]{2,1,0:T(8,128)(2,1)}) %all-gather.55.cloned.1.call-update) | async-done | bytes 8388624 | tf_op jit(solution)/shard_map/all_gather | solution.py:73
  1326.9 24.1 %fusion.14 = f32[2,1024,2048]{2,1,0:T(8,128)} fusion(bf16[2,1024,2048]{2,1,0:T(8,128)(2,1)} %multiply_convert_fusion, bf16[1,2048,2048]{2,1,0:T(8,128)(2,1)} %all-gather.55.cloned.1.call-done), kind=kOutput, calls=%fused_computation.22 | convolution fusion | flops 17179869184 | bytes 33554432 | tf_op jit(solution)/shard_map/msf,fe->mse/dot_general | solution.py:92
  1351.1 145.9 %reduce-scatter.11.cloned.1.call-done = f32[2,256,2048]{2,1,0:T(8,128)} async-done(((f32[2,1024,2048]{2,1,0:T(8,128)}), f32[2,256,2048]{2,1,0:T(8,128)}) %reduce-scatter.11.cloned.1.call-update) | async-done | bytes 4194320 | tf_op jit(solution)/shard_map/reduce_scatter | solution.py:93
  1497.0 6.6 add.85
  (97 shorter events, 6.2 us)
Async XLA Ops:
  6.5 9.2 copy-start.12
  6.5 10.5 copy-start.20
  6.6 24.1 %copy-start.15 = (bf16[2,256,2,64]{1,3,2,0:T(8,128)(2,1)S(1)}, bf16[2,256,2,64]{1,3,2,0:T(8,128)(2,1)}, u32[]{:S(2)}) copy-start(bf16[2,256,2,64]{1,3,2,0:T(8,128)(2,1)} %param.15) | copy-start | bytes 393220
  6.6 46.8 %copy-start.16 = (bf16[2,256,2,64]{1,3,2,0:T(8,128)(2,1)S(1)}, bf16[2,256,2,64]{1,3,2,0:T(8,128)(2,1)}, u32[]{:S(2)}) copy-start(bf16[2,256,2,64]{1,3,2,0:T(8,128)(2,1)} %param.16) | copy-start | bytes 393220
  6.6 73.1 %all-gather.37.cloned.1.call-start = ((), (), s32[]{:S(2)}) async-start(), calls=%async_computation.12 | async-start | bytes 2359296 | tf_op jit(solution)/shard_map/all_gather | solution.py:67
  8.6 111.2 %all-gather.29.cloned.1.call-start = ((), (), s32[]{:S(2)}) async-start(), calls=%async_computation.4 | async-start | bytes 10485760 | tf_op jit(solution)/shard_map/all_gather | solution.py:77
  15.7 158.2 %all-gather.39.cloned.1.call-start = ((), (), s32[]{:S(2)}) async-start(), calls=%async_computation.13 | async-start | bytes 2359296 | tf_op jit(solution)/shard_map/all_gather | solution.py:70
  16.7 334.0 %reduce-scatter.5.cloned.1.call-start = ((), (), s32[]{:S(2)}) async-start(), calls=%async_computation.5 | async-start | bytes 20971520 | tf_op jit(solution)/shard_map/reduce_scatter | solution.py:85
  53.4 86.2 %copy-start.8 = (pred[2,1024,1024]{1,2,0:T(8,128)(4,1)}, pred[2,1024,1024]{1,2,0:T(8,128)(4,1)S(1)}, u32[]{:S(2)}) copy-start(pred[2,1024,1024]{1,2,0:T(8,128)(4,1)S(1)} %compare_and_fusion) | copy-start | bytes 6291460
  79.6 52.9 %copy-start.4 = (f32[2,1024,32]{1,2,0:T(8,128)}, f32[2,1024,32]{1,2,0:T(8,128)S(1)}, u32[]{:S(2)}) copy-start(f32[2,1024,32]{1,2,0:T(8,128)S(1)} %get-tuple-element.31) | copy-start | bytes 786436
  79.6 52.9 %copy-start.6 = (f32[2,1024,32]{1,2,0:T(8,128)}, f32[2,1024,32]{1,2,0:T(8,128)S(1)}, u32[]{:S(2)}) copy-start(f32[2,1024,32]{1,2,0:T(8,128)S(1)} %get-tuple-element.32) | copy-start | bytes 786436
  79.6 50.0 %copy-start.10 = (bf16[1,2048,2,64]{1,3,2,0:T(8,128)(2,1)S(1)}, bf16[1,2048,2,64]{1,3,2,0:T(8,128)(2,1)}, u32[]{:S(2)}) copy-start(bf16[1,2048,2,64]{1,3,2,0:T(8,128)(2,1)} %all-gather.1) | copy-start | bytes 1572868
  119.9 9.8 copy-start.21
  129.7 3.8 copy-start.11
  204.1 3.6 copy-start.19
  204.1 146.6 %copy-start = (bf16[2,256,2048]{2,1,0:T(8,128)(2,1)S(1)}, bf16[2,256,2048]{2,1,0:T(8,128)(2,1)}, u32[]{:S(2)}) copy-start(bf16[2,256,2048]{2,1,0:T(8,128)(2,1)} %param.11) | copy-start | bytes 6291460
  204.2 195.3 %all-gather.41.cloned.1.call-start = ((), (), s32[]{:S(2)}) async-start(), calls=%async_computation.14 | async-start | bytes 9437184 | tf_op jit(solution)/shard_map/all_gather | solution.py:71
  207.6 273.7 %all-gather.31.cloned.1.call-start = ((), (), s32[]{:S(2)}) async-start(), calls=%async_computation.6 | async-start | bytes 10485760 | tf_op jit(solution)/shard_map/all_gather | solution.py:88
  350.7 3.4 copy-start.2
  356.3 175.2 %all-gather.43.cloned.1.call-start = ((), (), s32[]{:S(2)}) async-start(), calls=%async_computation.15 | async-start | bytes 9437184 | tf_op jit(solution)/shard_map/all_gather | solution.py:72
  359.5 224.1 %all-gather.45.cloned.1.call-start = ((), (), s32[]{:S(2)}) async-start(), calls=%async_computation.16 | async-start | bytes 9437184 | tf_op jit(solution)/shard_map/all_gather | solution.py:73
  362.7 391.2 %reduce-scatter.7.cloned.1.call-start = ((), (), s32[]{:S(2)}) async-start(), calls=%async_computation.7 | async-start | bytes 20971520 | tf_op jit(solution)/shard_map/reduce_scatter | solution.py:93
  608.0 152.1 %copy-start.17 = (f32[1,2048]{1,0:T(1,128)S(1)}, f32[1,2048]{1,0:T(1,128)}, u32[]{:S(2)}) copy-start(f32[1,2048]{1,0:T(1,128)} %get-tuple-element.35) | copy-start | bytes 24580
  608.0 196.9 %all-gather.47.cloned.1.call-start = ((), (), s32[]{:S(2)}) async-start(), calls=%async_computation.17 | async-start | bytes 2359296 | tf_op jit(solution)/shard_map/all_gather | solution.py:67
  608.7 154.0 %copy-start.13 = (bf16[1,256,2,64]{1,3,2,0:T(8,128)(2,1)S(1)}, bf16[1,256,2,64]{1,3,2,0:T(8,128)(2,1)}, u32[]{:S(2)}) copy-start(bf16[1,256,2,64]{1,3,2,0:T(8,128)(2,1)} %get-tuple-element.29) | copy-start | bytes 196612
  608.7 173.4 %copy-start.14 = (bf16[1,256,2,64]{1,3,2,0:T(8,128)(2,1)S(1)}, bf16[1,256,2,64]{1,3,2,0:T(8,128)(2,1)}, u32[]{:S(2)}) copy-start(bf16[1,256,2,64]{1,3,2,0:T(8,128)(2,1)} %get-tuple-element.27) | copy-start | bytes 196612
  608.7 254.8 %all-gather.33.cloned.1.call-start = ((), (), s32[]{:S(2)}) async-start(), calls=%async_computation.8 | async-start | bytes 10485760 | tf_op jit(solution)/shard_map/all_gather | solution.py:77
  758.1 2.0 copy-start.3
  761.9 155.5 %all-gather.49.cloned.1.call-start = ((), (), s32[]{:S(2)}) async-start(), calls=%async_computation.18 | async-start | bytes 2359296 | tf_op jit(solution)/shard_map/all_gather | solution.py:70
  762.6 331.7 %reduce-scatter.9.cloned.1.call-start = ((), (), s32[]{:S(2)}) async-start(), calls=%async_computation.9 | async-start | bytes 20971520 | tf_op jit(solution)/shard_map/reduce_scatter | solution.py:85
  804.9 66.4 %copy-start.5 = (f32[2,1024,32]{1,2,0:T(8,128)S(1)}, f32[2,1024,32]{1,2,0:T(8,128)}, u32[]{:S(2)}) copy-start(f32[2,1024,32]{1,2,0:T(8,128)} %copy-done.4) | copy-start | bytes 786436
  804.9 66.4 %copy-start.7 = (f32[2,1024,32]{1,2,0:T(8,128)S(1)}, f32[2,1024,32]{1,2,0:T(8,128)}, u32[]{:S(2)}) copy-start(f32[2,1024,32]{1,2,0:T(8,128)} %copy-done.6) | copy-start | bytes 786436
  863.5 9.9 copy-start.22
  877.1 6.0 copy-start.9
  947.8 152.5 %copy-start.18 = (f32[1,2048]{1,0:T(1,128)S(1)}, f32[1,2048]{1,0:T(1,128)}, u32[]{:S(2)}) copy-start(f32[1,2048]{1,0:T(1,128)} %get-tuple-element.33) | copy-start | bytes 24580
  947.8 195.3 %all-gather.51.cloned.1.call-start = ((), (), s32[]{:S(2)}) async-start(), calls=%async_computation.19 | async-start | bytes 9437184 | tf_op jit(solution)/shard_map/all_gather | solution.py:71
  948.4 276.5 %all-gather.35.cloned.1.call-start = ((), (), s32[]{:S(2)}) async-start(), calls=%async_computation.10 | async-start | bytes 10485760 | tf_op jit(solution)/shard_map/all_gather | solution.py:88
  1098.3 2.0 copy-start.1
  1102.1 172.8 %all-gather.53.cloned.1.call-start = ((), (), s32[]{:S(2)}) async-start(), calls=%async_computation.20 | async-start | bytes 9437184 | tf_op jit(solution)/shard_map/all_gather | solution.py:72
  1102.8 224.1 %all-gather.55.cloned.1.call-start = ((), (), s32[]{:S(2)}) async-start(), calls=%async_computation.21 | async-start | bytes 9437184 | tf_op jit(solution)/shard_map/all_gather | solution.py:73
  1103.4 393.6 %reduce-scatter.11.cloned.1.call-start = ((), (), s32[]{:S(2)}) async-start(), calls=%async_computation.11 | async-start | bytes 20971520 | tf_op jit(solution)/shard_map/reduce_scatter | solution.py:93
Sparse Core Ops, SparseCore 0:
  9.0 28.1 all-gather.36
  38.7 81.0 all-gather.28
  121.5 25.3 all-gather.38
  204.3 146.3 reduce-scatter.4
  352.2 47.2 all-gather.40
  400.9 80.4 all-gather.30
  483.0 48.4 all-gather.42
  533.1 50.5 all-gather.44
  608.1 145.7 reduce-scatter.6
  755.3 25.2 all-gather.46
  782.2 81.2 all-gather.32
  865.0 25.3 all-gather.48
  947.9 146.3 reduce-scatter.8
  1095.8 47.2 all-gather.50
  1144.5 80.4 all-gather.34
  1226.4 48.4 all-gather.52
  1276.3 50.5 all-gather.54
  1351.2 145.7 reduce-scatter.10
where the time goes:
time: 1520 us; the launch traced here: 1510 us
  waiting for transfers between devices  1020 us (67%)
  matrix products  307 us (20%)
  blocking collectives  99.6 us (7%)
  other arithmetic  40.6 us (3%)
  local copies, waits for them, and re-layouts  23 us (2%)
    reduce_scatter x4, waiting for transfers between devices, device_fn(): lax.psum_scatter(part_sum, 'mp', scatter_dimension=1, tiled=True)  579 us
    all_gather x4, waiting for transfers between devices, device_fn(): h_blk = lax.all_gather(hidden, 'mp', axis=1, tiled=True)  263 us
    all_gather x2, waiting for transfers between devices, device_fn(): wg_full = lax.all_gather(w_gate[layer_idx], 'tok', axis=0, tiled=True)  76.3 us
    sub x2, matrix products, attend(): probs_bf = jax.nn.softmax(scores, axis=-1).astype(jnp.bfloat16)  68.5 us
    dot_general x2, matrix products, device_fn(): jnp.einsum('mnsgd,ngde->mse', attn_out, wo_full.reshape(kv_heads, groups,...  60.5 us
    dot_general x2, matrix products, device_fn(): jnp.einsum('mse,ef->msf', h_blk, wu_full, preferred_element_type=jnp.floa...  52.2 us
    all_gather x2, waiting for transfers between devices, device_fn(): wd_full = lax.all_gather(w_down[layer_idx], 'tok', axis=1, tiled=True)  52 us
    all_gather x2, waiting for transfers between devices, device_fn(): wu_full = lax.all_gather(w_up[layer_idx], 'tok', axis=0, tiled=True)  51.2 us
  transfers between devices with their start and end apart: 18, of which 14 were waited for; matrix products, arithmetic and copies ran while one was open for 16% of the time, Pallas kernels for 0%

commit v1 on v0

v1 whole, which is shorter than its diff:
```python
import functools

import jax
import jax.numpy as jnp
from jax import lax
from jax.experimental import pallas as pl
from jax.experimental.pallas import tpu as pltpu
from jax.sharding import PartitionSpec as P


NORM_EPS = 1e-5
ROPE_BASE = 10000.0
LOG2_E = 1.4426950408889634


def rope_tables(positions, head_dim):
    half_dim = head_dim // 2
    inv_freq = ROPE_BASE ** (-2.0 * jnp.arange(half_dim, dtype=jnp.float32) / head_dim)
    angles = positions.astype(jnp.float32)[..., None] * inv_freq
    cos_t, sin_t = jnp.cos(angles), jnp.sin(angles)
    cos_w = jnp.concatenate([cos_t] * 4, axis=-1)
    sin_w = jnp.concatenate([-sin_t, sin_t] * 2, axis=-1)
    return cos_w, sin_w


def norm_rows(resid, gain):
    mean_sq = jnp.mean(resid * resid, axis=-1, keepdims=True)
    return (resid * lax.rsqrt(mean_sq + NORM_EPS) * gain.astype(jnp.float32)).astype(jnp.bfloat16)


def rotate_pair(x, cos_w, sin_w, low):
    width = x.shape[-1]
    quarter = width // 4
    up = pltpu.roll(x, quarter, 1)
    down = pltpu.roll(x, width - quarter, 1)
    return (x * cos_w + jnp.where(low, down, up) * sin_w).astype(jnp.bfloat16)


def qkv_kernel(q_w, kv_w, resid_ref, gain_ref, cos_ref, sin_ref, w_ref, q_ref, kv_ref, hid):
    @pl.when(pl.program_id(0) == 0)
    def _():
        hid[...] = norm_rows(resid_ref[...].astype(jnp.float32), gain_ref[...])

    acc = jnp.dot(hid[...], w_ref[0], preferred_element_type=jnp.float32)
    cos_w, sin_w = cos_ref[...], sin_ref[...]
    pair = cos_w.shape[-1]
    lane = lax.broadcasted_iota(jnp.int32, cos_w.shape, 1)
    low = lax.rem(lane, pair // 2) < pair // 4
    for p in range(q_w // pair):
        q_ref[0, :, p * pair:(p + 1) * pair] = rotate_pair(acc[:, p * pair:(p + 1) * pair], cos_w, sin_w, low)
    for p in range(kv_w // pair):
        kv_ref[0, :, p * pair:(p + 1) * pair] = rotate_pair(
            acc[:, q_w + p * pair:q_w + (p + 1) * pair], cos_w, sin_w, low)
    kv_ref[0, :, kv_w:] = acc[:, q_w + kv_w:].astype(jnp.bfloat16)


def qkv_call(resid, gain, cos_w, sin_w, w_all):
    rows, embed = resid.shape
    shares, _, cols = w_all.shape
    kv_w = 128
    q_w = cols - 2 * kv_w
    pair = cos_w.shape[-1]
    return pl.pallas_call(
        functools.partial(qkv_kernel, q_w, kv_w),
        name="qkv",
        grid=(shares,),
        in_specs=[
            pl.BlockSpec((rows, embed), lambda m: (0, 0)),
            pl.BlockSpec((1, embed), lambda m: (0, 0)),
            pl.BlockSpec((rows, pair), lambda m: (0, 0)),
            pl.BlockSpec((rows, pair), lambda m: (0, 0)),
            pl.BlockSpec((1, embed, cols), lambda m: (m, 0, 0)),
        ],
        out_specs=[
            pl.BlockSpec((1, rows, q_w), lambda m: (m, 0, 0)),
            pl.BlockSpec((1, rows, 2 * kv_w), lambda m: (m, 0, 0)),
        ],
        out_shape=[
            jax.ShapeDtypeStruct((shares, rows, q_w), jnp.bfloat16),
            jax.ShapeDtypeStruct((shares, rows, 2 * kv_w), jnp.bfloat16),
        ],
        scratch_shapes=[pltpu.VMEM((rows, embed), jnp.bfloat16)],
        compiler_params=pltpu.CompilerParams(dimension_semantics=("arbitrary",), vmem_limit_bytes=40 * 1024 * 1024),
        cost_estimate=pl.CostEstimate(
            flops=2 * rows * embed * cols * shares, bytes_accessed=2 * embed * cols * shares, transcendentals=0),
    )(resid, gain, cos_w, sin_w, w_all)


def attn_kernel(score_c, q_ref, own_ref, left_ref, right_ref, opp_lo_ref, opp_hi_ref, bound_ref, wo_ref, resid_ref, gain_ref,
                out_ref, hid_ref, k_scr, v_scr, o_scr):
    step = pl.program_id(0)
    rows = q_ref.shape[1]
    pair = k_scr.shape[-1]
    half = pair // 2
    n_pairs = q_ref.shape[2] // pair
    lane = lax.broadcasted_iota(jnp.int32, (rows, pair), 1)
    low = lane < half
    zero = jnp.zeros((rows, pair), jnp.float32)

    def spread(c, kv_ref):
        at = slice(c * rows, (c + 1) * rows)
        for scr, lo in ((k_scr, 0), (v_scr, pair)):
            both = kv_ref[0, :, lo:lo + pair].astype(jnp.float32)
            swap = pltpu.roll(both, half, 1)
            scr[0, 0, at] = jnp.where(low, both, zero).astype(jnp.bfloat16)
            scr[0, 1, at] = jnp.where(low, zero, swap).astype(jnp.bfloat16)
            scr[1, 0, at] = jnp.where(low, swap, zero).astype(jnp.bfloat16)
            scr[1, 1, at] = jnp.where(low, zero, both).astype(jnp.bfloat16)

    spread(0, own_ref)
    spread(1, left_ref)
    spread(2, right_ref)
    first_half = step < pl.num_programs(0) // 2

    @pl.when(first_half)
    def _():
        spread(3, opp_lo_ref)

    @pl.when(jnp.logical_not(first_half))
    def _():
        spread(3, opp_hi_ref)

    def one_pair(p, carry):
        cols = pl.ds(pl.multiple_of(p * pair, pair), pair)
        q_pair = q_ref[0, :, cols]
        group = p // (n_pairs // 2)
        out = None
        for side in range(2):
            s = lax.dot_general(q_pair, k_scr[group, side], (((1,), (1,)), ((), ())),
                                preferred_element_type=jnp.float32)
            s = jnp.minimum(s, bound_ref[...]) * score_c
            e = jnp.exp2(s - jnp.max(s, axis=-1, keepdims=True))
            probs = (e * (1.0 / jnp.sum(e, axis=-1, keepdims=True))).astype(jnp.bfloat16)
            part = jnp.dot(probs, v_scr[group, side], preferred_element_type=jnp.float32)
            out = part if out is None else out + part
        o_scr[:, cols] = out.astype(jnp.bfloat16)
        return carry

    lax.fori_loop(0, n_pairs, one_pair, 0, unroll=2)

    @pl.when(step == 0)
    def _():
        out_ref[...] = resid_ref[...].astype(jnp.float32)

    tok_n, width = wo_ref.shape[1], wo_ref.shape[3]
    for t in range(tok_n):
        at = slice(t * width, (t + 1) * width)
        out_ref[:, at] += jnp.dot(o_scr[...], wo_ref[0, t], preferred_element_type=jnp.float32)

    @pl.when(step == pl.num_programs(0) - 1)
    def _():
        hid_ref[...] = norm_rows(out_ref[...], gain_ref[...])


def attn_call(q, kvs, bound, wo_all, resid, gain, head_dim):
    shares, rows, q_w = q.shape
    kv2 = kvs[0].shape[2]
    embed = resid.shape[1]
    pair = kv2 // 2
    keys = bound.shape[1]
    heads = shares * q_w // head_dim
    part = shares // 2
    whole = pl.BlockSpec((1, rows, kv2), lambda m: (m, 0, 0))
    return pl.pallas_call(
        functools.partial(attn_kernel, LOG2_E * head_dim ** -0.5),
        name="attn",
        grid=(shares,),
        in_specs=[
            pl.BlockSpec((1, rows, q_w), lambda m: (m, 0, 0)),
            whole, whole, whole,
            pl.BlockSpec((1, rows, kv2), lambda m: (jnp.minimum(m, part - 1), 0, 0)),
            pl.BlockSpec((1, rows, kv2), lambda m: (jnp.maximum(m - part, 0), 0, 0)),
            pl.BlockSpec((rows, keys), lambda m: (0, 0)),
            pl.BlockSpec((1,) + wo_all.shape[1:], lambda m: (m, 0, 0, 0)),
            pl.BlockSpec((rows, embed), lambda m: (0, 0)),
            pl.BlockSpec((1, embed), lambda m: (0, 0)),
        ],
        out_specs=[
            pl.BlockSpec((rows, embed), lambda m: (0, 0)),
            pl.BlockSpec((rows, embed), lambda m: (0, 0)),
        ],
        out_shape=[
            jax.ShapeDtypeStruct((rows, embed), jnp.float32),
            jax.ShapeDtypeStruct((rows, embed), jnp.bfloat16),
        ],
        scratch_shapes=[
            pltpu.VMEM((2, 2, keys, pair), jnp.bfloat16),
            pltpu.VMEM((2, 2, keys, pair), jnp.bfloat16),
            pltpu.VMEM((rows, q_w), jnp.bfloat16),
        ],
        compiler_params=pltpu.CompilerParams(dimension_semantics=("arbitrary",), vmem_limit_bytes=40 * 1024 * 1024),
        cost_estimate=pl.CostEstimate(
            flops=2 * rows * q_w * embed * shares + 16 * heads * rows * keys * head_dim,
            bytes_accessed=2 * q_w * embed * shares, transcendentals=heads * rows * keys),
    )(q, *kvs, bound, wo_all, resid, gain)


def mlp_kernel(n_in, n_out, n_act, *refs):
    ins = refs[:n_in]
    wg_ref, wu_ref, wd_ref = refs[n_in:n_in + 3]
    outs = refs[n_in + 3:n_in + 3 + n_out]
    x_scr, act_scr = refs[-2:]
    step = pl.program_id(0)

    @pl.when(step == 0)
    def _():
        at = 0
        for ref in ins:
            x_scr[at:at + ref.shape[0]] = ref[...]
            at += ref.shape[0]

    @pl.when(step < n_act)
    def _():
        gate = jnp.dot(x_scr[...], wg_ref[...], preferred_element_type=jnp.float32)
        up = jnp.dot(x_scr[...], wu_ref[...], preferred_element_type=jnp.float32)
        act_scr[step] = (jax.nn.silu(gate) * up).astype(jnp.bfloat16)

    @pl.when(step >= n_act)
    def _():
        rows = outs[0].shape[0]
        blk = act_scr.shape[2]
        part = None
        for i in range(n_act):
            term = jnp.dot(act_scr[i], wd_ref[i * blk:(i + 1) * blk], preferred_element_type=jnp.float32)
            part = term if part is None else part + term
        for i, ref in enumerate(outs):
            ref[...] = part[i * rows:(i + 1) * rows]


def mlp_call(pieces, n_out, w_g, w_u, w_d, blk=512, blk2=512):
    embed, ffn = w_g.shape
    total = sum(p.shape[0] for p in pieces)
    rows = total // n_out
    n_act = ffn // blk
    return pl.pallas_call(
        functools.partial(mlp_kernel, len(pieces), n_out, n_act),
        name="mlp",
        grid=(n_act + embed // blk2,),
        in_specs=[pl.BlockSpec(p.shape, lambda f: (0, 0)) for p in pieces]
        + [
            pl.BlockSpec((embed, blk), lambda f: (0, jnp.minimum(f, n_act - 1))),
            pl.BlockSpec((embed, blk), lambda f: (0, jnp.minimum(f, n_act - 1))),
            pl.BlockSpec((ffn, blk2), lambda f: (0, jnp.maximum(f - n_act, 0))),
        ],
        out_specs=[pl.BlockSpec((rows, blk2), lambda f: (0, jnp.maximum(f - n_act, 0)))] * n_out,
        out_shape=[jax.ShapeDtypeStruct((rows, embed), jnp.float32)] * n_out,
        scratch_shapes=[pltpu.VMEM((total, embed), jnp.bfloat16), pltpu.VMEM((n_act, total, blk), jnp.bfloat16)],
        compiler_params=pltpu.CompilerParams(dimension_semantics=("arbitrary",), vmem_limit_bytes=48 * 1024 * 1024),
        cost_estimate=pl.CostEstimate(
            flops=6 * total * embed * ffn, bytes_accessed=6 * embed * ffn, transcendentals=total * ffn),
    )(*pieces, w_g, w_u, w_d)


def gather_kernel(mp_n, x_n, n_pieces, *refs):
    pieces, outs = refs[:n_pieces], refs[n_pieces:2 * n_pieces]
    local_sems, send_sems, x_full, x_half, y_full, y_half, side_sems = refs[2 * n_pieces:]
    j, t = lax.axis_index('mp'), lax.axis_index('tok')
    x, core = t // 2, t % 2
    x_near = {1: {'tok': lax.rem(x + 1, x_n) * 2 + core}, -1: {'tok': lax.rem(x + x_n - 1, x_n) * 2 + core}}
    y_near = {1: {'mp': lax.rem(j + 1, mp_n)}, -1: {'mp': lax.rem(j + mp_n - 1, mp_n)}}
    other = {'tok': x * 2 + 1 - core}

    barrier = pltpu.get_barrier_semaphore()
    partners = [x_near[1], x_near[-1], y_near[1], y_near[-1], other]
    for who in partners:
        pl.semaphore_signal(barrier, inc=1, device_id=who, device_id_type=pl.DeviceIdType.MESH)
    pl.semaphore_wait(barrier, len(partners))

    order = (0, -1, 1, 2)
    place = {d: i for i, d in enumerate(order)}
    near = tuple(enumerate((-1, 1)))
    sent = []

    def unit(n, dx, dj, c=None):
        at_t = lax.rem(x + dx + x_n, x_n) * 2 + (core if c is None else c)
        return outs[n].at[lax.rem(j + dj + mp_n, mp_n), at_t]

    def part(n, i, ref):
        half = pieces[n].shape[0] // 2
        return ref.at[i * half:(i + 1) * half]

    def send(src, dst, sem, who):
        copy = pltpu.make_async_remote_copy(
            src_ref=src, dst_ref=dst, send_sem=send_sems.at[len(sent)], recv_sem=sem,
            device_id=who, device_id_type=pl.DeviceIdType.MESH)
        copy.start()
        sent.append(copy)

    def arrived(dst, sem, who):
        pltpu.make_async_remote_copy(
            src_ref=dst, dst_ref=dst, send_sem=send_sems.at[0], recv_sem=sem,
            device_id=who, device_id_type=pl.DeviceIdType.MESH).wait_recv()

    def side_sem(n, dx, dj):
        return side_sems.at[n * 16 + place[dx] * 4 + place[dj]]

    def to_side(n, dx, dj, src):
        send(src, unit(n, dx, dj), side_sem(n, dx, dj), other)

    def to_rows(n, dx, src):
        send(src, unit(n, dx, 0), y_full.at[n * 8 + place[dx] * 2], y_near[1])
        send(src, unit(n, dx, 0), y_full.at[n * 8 + place[dx] * 2 + 1], y_near[-1])

    every = range(n_pieces)
    kept = []
    for n in every:
        own = pieces[n]
        keep = pltpu.make_async_copy(own, unit(n, 0, 0), local_sems.at[n])
        keep.start()
        kept.append(keep)
        for i, d in near:
            send(own, unit(n, 0, 0), x_full.at[n * 2 + i], x_near[-d])
        to_rows(n, 0, own)
        to_side(n, 0, 0, own)
    for n in every:
        for i, d in near:
            got = unit(n, d, 0)
            arrived(got, x_full.at[n * 2 + i], x_near[d])
            send(part(n, i, got), part(n, i, got), x_half.at[n * 2 + i], x_near[-d])
            to_rows(n, d, got)
            to_side(n, d, 0, got)
    for n in every:
        got = unit(n, 2, 0)
        for i, d in near:
            arrived(part(n, i, got), x_half.at[n * 2 + i], x_near[d])
        to_rows(n, 2, got)
        to_side(n, 2, 0, got)
    for n in every:
        for dx in order:
            for i, d in near:
                got = unit(n, dx, d)
                at = n * 8 + place[dx] * 2 + i
                arrived(got, y_full.at[at], y_near[d])
                send(part(n, i, got), part(n, i, got), y_half.at[at], y_near[-d])
                to_side(n, dx, d, got)
    for n in every:
        for dx in order:
            got = unit(n, dx, 2)
            for i, d in near:
                arrived(part(n, i, got), y_half.at[n * 8 + place[dx] * 2 + i], y_near[d])
            to_side(n, dx, 2, got)
    for n in every:
        for dx in order:
            for dj in order:
                arrived(unit(n, dx, dj, 1 - core), side_sem(n, dx, dj), other)
    for copy in sent:
        copy.wait_send()
    for keep in kept:
        keep.wait()


def gather_call(pieces, mp_n, tok_n):
    n = len(pieces)
    n_sends = 5 + 2 * 4 + 3 + 8 * 2 + 4
    dma = pltpu.SemaphoreType.DMA
    return pl.pallas_call(
        functools.partial(gather_kernel, mp_n, tok_n // 2, n),
        name="gather_weights",
        in_specs=[pl.BlockSpec(memory_space=pltpu.VMEM)] * n,
        out_specs=[pl.BlockSpec(memory_space=pl.ANY)] * n,
        out_shape=[jax.ShapeDtypeStruct((mp_n, tok_n) + p.shape, p.dtype) for p in pieces],
        scratch_shapes=[dma((n,)), dma((n * n_sends,)), dma((2 * n,)), dma((2 * n,)), dma((8 * n,)), dma((8 * n,)), dma((16 * n,))],
        compiler_params=pltpu.CompilerParams(collective_id=1, has_side_effects=True),
        cost_estimate=pl.CostEstimate(
            flops=10 ** 11, bytes_accessed=sum(p.size for p in pieces) * 2 * mp_n * tok_n, transcendentals=0),
    )(*pieces)


def solution(mesh):
    act_spec = P(None, ('rep', 'tok', 'mp'), None)
    seg_spec = P(None, ('rep', 'tok', 'mp'))
    gain_spec = P(None, None)
    head_in = P(None, 'tok', 'mp', None)
    head_out = P(None, 'mp', None, 'tok')
    ffn_in = P(None, 'tok', 'mp')
    ffn_out = P(None, 'mp', 'tok')
    mp_n, tok_n = mesh.shape['mp'], mesh.shape['tok']
    fwd = [(i, (i + 1) % mp_n) for i in range(mp_n)]
    bwd = [(i, (i - 1) % mp_n) for i in range(mp_n)]

    def to_right(value):
        return lax.ppermute(value, 'mp', fwd)

    def to_left(value):
        return lax.ppermute(value, 'mp', bwd)

    def spread_ring(value):
        half = value.shape[0] // 2
        from_left, from_right = to_right(value), to_left(value)
        return [value, from_left, from_right,
                to_right(from_left[:half]), to_left(from_right[half:])]

    def device_fn(x_in, seg_ids, g_attn, w_q, w_k, w_v, w_o, g_mlp, w_gate, w_up, w_down):
        micro_n, rows, _ = x_in.shape
        layers = w_q.shape[0]
        head_dim = w_q.shape[3]
        e_part = w_q.shape[1]

        seg_parts = [seg_ids, to_right(seg_ids), to_left(seg_ids)]
        seg_parts.append(to_right(seg_parts[1]))
        weights = []
        for l in range(layers):
            w_qkv = jnp.concatenate([w[l].reshape(e_part, -1) for w in (w_q, w_k, w_v)], axis=1)
            w_o_l = w_o[l].reshape(-1, w_o.shape[3])
            if l == 0:
                w_qkv_all, w_o_all = gather_call([w_qkv, w_o_l], mp_n, tok_n)
            else:
                w_qkv_all = lax.all_gather(w_qkv, ('mp', 'tok'), axis=0)
                w_o_all = lax.all_gather(w_o_l, ('mp', 'tok'), axis=0).reshape((mp_n, tok_n) + w_o_l.shape)
            weights.append((
                w_qkv_all.reshape(mp_n, tok_n * e_part, -1), w_o_all,
                lax.all_gather(w_gate[l], 'tok', axis=0, tiled=True),
                lax.all_gather(w_up[l], 'tok', axis=0, tiled=True),
                lax.all_gather(w_down[l], 'tok', axis=1, tiled=True),
            ))

        me = lax.axis_index('mp')
        seg_ring = jnp.concatenate(seg_parts, axis=1)
        ring_at = [lax.rem(me + c + mp_n, mp_n) * rows for c in (0, -1, 1, 2)]
        key_at = jnp.concatenate([at + jnp.arange(rows, dtype=jnp.int32) for at in ring_at])
        own_at = key_at[:rows]
        streams = []
        for b in range(micro_n):
            same = seg_ring[b][None, :] == seg_ids[b][:, None]
            first = jnp.min(jnp.where(same, key_at[None, :], rows * mp_n), axis=1)
            cos_w, sin_w = rope_tables(own_at - first, head_dim)
            ok = same & (key_at[None, :] <= own_at[:, None])
            streams.append(dict(name='ab'[b], cos=cos_w, sin=sin_w, bound=jnp.where(ok, jnp.inf, -jnp.inf),
                                resid=x_in[b].astype(jnp.float32)))

        half = rows // 2
        last = [None]

        def in_turn(value, *more):
            held = [v for v in (last[0],) + more if v is not None]
            return lax.optimization_barrier((value, *held))[0] if held else value

        def qkv_step(st, l):
            resid = in_turn(st['resid'])
            q, kv = qkv_call(resid, g_attn[l:l + 1], st['cos'], st['sin'], weights[l][0])
            st['q'], st['kvs'] = q, spread_ring(kv)
            last[0] = kv

        def attn_step(st, l, *more):
            q = in_turn(st['q'], *more)
            st['resid'], hid = attn_call(q, st['kvs'], st['bound'], weights[l][1], st['resid'],
                                         g_mlp[l:l + 1], head_dim)
            st['hid'] = last[0] = hid

        def share_step(st, *more):
            hid = lax.optimization_barrier((st['hid'], *more))[0] if more else st['hid']
            st['hids'] = spread_ring(hid)

        def opp_step(st, l):
            lo, hi = st['hids'][3:]
            lo = in_turn(lo)
            (p_opp,) = mlp_call([lo, hi], 1, *weights[l][2:])
            st['opp_in'] = to_right(p_opp[:half]), to_left(p_opp[half:])
            last[0] = p_opp

        def near_step(st, l):
            own, left, right = st['hids'][:3]
            left = in_turn(left)
            p_own, p_left, p_right = mlp_call([own, left, right], 3, *weights[l][2:])
            last[0] = p_own
            lo_in, hi_in = st['opp_in']
            p_right = jnp.concatenate([p_right[:half] + lo_in, p_right[half:]], axis=0)
            p_left = jnp.concatenate([p_left[:half], p_left[half:] + hi_in], axis=0)
            st['relay'] = p_right
            st['resid'] = st['resid'] + p_own + to_right(p_right) + to_left(p_left)

        a, b = streams
        for l in range(layers):
            qkv_step(a, l)
            if l == 0:
                qkv_step(b, l)
                attn_step(a, l)
                share_step(a)
                attn_step(b, l)
                share_step(b, *a['hids'][1:3])
                opp_step(a, l)
                near_step(a, l)
            else:
                attn_step(a, l, b['relay'])
                share_step(a)
                qkv_step(b, l)
                opp_step(a, l)
                attn_step(b, l)
                share_step(b)
                near_step(a, l)
            opp_step(b, l)
            near_step(b, l)
        return jnp.stack([st['resid'] for st in streams])


    return jax.shard_map(
        device_fn,
        mesh=mesh,
        in_specs=(act_spec, seg_spec, gain_spec, head_in, head_in, head_in, head_out, gain_spec, ffn_in, ffn_in, ffn_out),
        out_specs=act_spec,
        check_vma=False,
    )
```

time: 1520 us -> 805 us (0.53)
  the two profiles are of different devices: /device:TPU:97 before, /device:TPU:98 now
where the time goes in v1:
time: 805 us; the launch traced here: 796 us
  Pallas kernels  396 us (49%)
  waiting for transfers between devices  220 us (27%)
  starting transfers between devices  82.9 us (10%)
  local copies, waits for them, and re-layouts  45 us (6%)
  other arithmetic  37 us (5%)
  between operations  15 us (2%)
    ppermute x26, waiting for transfers between devices, to_right(): return lax.ppermute(value, 'mp', fwd)  216 us
    pallas_call x8, Pallas kernels, mlp_call(): pl.pallas_call(functools.partial(mlp_kernel, len(pieces), n_out, n_act),...  161 us
    pallas_call x4, Pallas kernels, attn_call(): pl.pallas_call(functools.partial(attn_kernel, LOG2_E * head_dim ** (-0.5)...  105 us
    pallas_call x1, Pallas kernels, gather_call(): pl.pallas_call(functools.partial(gather_kernel, mp_n, tok_n // 2, n), nam...  97.6 us
    ppermute x25, starting transfers between devices, to_left(): return lax.ppermute(value, 'mp', bwd)  75.1 us
    pallas_call x4, Pallas kernels, qkv_call(): pl.pallas_call(functools.partial(qkv_kernel, q_w, kv_w), name='qkv', grid...  32.4 us
    unnamed x117, local copies, waits for them, and re-layouts  21.2 us
  transfers between devices with their start and end apart: 59, of which 16 were waited for; matrix products, arithmetic and copies ran while one was open for 7% of the time, Pallas kernels for 46%

profile of v1, /device:TPU:98, one launch (start us, length us, event | category | flops | bytes accessed | tf_op | source)
XLA Modules:
  0.0 795.9 jit_solution(12973998499782749914)
XLA Ops:
  6.6 3.3 fusion.12
  11.6 3.0 fusion.10
  18.4 2.2 collective-permute-start
  20.6 2.6 collective-permute-start.1
  24.7 3.4 bitcast_convert_fusion
  28.1 97.6 %gather_weights.1 = (bf16[4,8,256,768]{3,2,1,0:T(8,128)(2,1)}, bf16[4,8,512,256]{3,2,1,0:T(8,128)(2,1)}) custom-call(bf16[256,768]{1,0:T(8,128)(2,1)} %pad_maximum_fusion.9.refs_0_, bf16[512,256]{1,0:T(8,128)(2,1)} %bitcast.66), custom_call_target="tpu_custom_call" | custom-call | flops 99999997952 | bytes 20971520 | tf_op jit(solution)/shard_map/gather_weights/pallas_call | solution.py:356
  126.1 4.5 collective-permute-done.2
  133.9 8.3 %qkv.4 = (bf16[4,256,512]{2,1,0:T(8,128)(2,1)S(1)}, bf16[4,256,256]{2,1,0:T(8,128)(2,1)S(1)}) custom-call(f32[256,2048]{1,0:T(8,128)S(1)} %copy-done, bf16[1,2048]{1,0:T(2,128)(2,1)S(1)} %get-tuple-element.142.gain_ref, f32[256,128]{1,0:T(8,128)S(1)} %pad_maximum_fusion.11.cos_ref, f32[256,128]{1,0:T(8,128)S(1)} %pad_maximum_fusion.12.sin_ref, ...), custom_call_target="tpu_custom_call" | custom-call | flops 3221225472 | bytes 12582912 | tf_op jit(solution)/shard_map/qkv/pallas_call | solution.py:63
  142.3 3.2 collective-permute-start.4
  145.9 7.9 qkv.5
  154.8 3.2 collective-permute-start.10
  158.3 3.3 collective-permute-start.6
  163.0 7.8 collective-permute-done.9.left_ref
  173.1 3.4 collective-permute-start.12
  176.5 27.0 %attn.4 = (f32[256,2048]{1,0:T(8,128)S(1)}, bf16[256,2048]{1,0:T(8,128)(2,1)}) custom-call(bf16[4,256,512]{2,1,0:T(8,128)(2,1)S(1)} %get-tuple-element.56.q_ref, bf16[4,256,256]{2,1,0:T(8,128)(2,1)S(1)} %get-tuple-element.53.own_ref, bf16[4,256,256]{2,1,0:T(8,128)(2,1)S(1)} %collective-permute-done.3.left_ref, ...), custom_call_target="tpu_custom_call" | custom-call | flops 10737418240 | bytes 8388608 | tf_op jit(solution)/shard_map/attn/pallas_call | solution.py:164
  204.9 3.2 collective-permute-start.13
  212.8 25.5 %attn.5 = (f32[256,2048]{1,0:T(8,128)S(1)}, bf16[256,2048]{1,0:T(8,128)(2,1)S(1)}) custom-call(bf16[4,256,512]{2,1,0:T(8,128)(2,1)S(1)} %copy-done.33, bf16[4,256,256]{2,1,0:T(8,128)(2,1)S(1)} %copy-done.39, bf16[4,256,256]{2,1,0:T(8,128)(2,1)S(1)} %collective-permute-done.9.left_ref, bf16[4,256,256]{2,1,0:T(8,128)(2,1)S(1)} %copy-done.23, ...), custom_call_target="tpu_custom_call" | custom-call | flops 10737418240 | bytes 8388608 | tf_op jit(solution)/shard_map/attn/pallas_call | solution.py:164
  238.3 7.9 collective-permute-done.7.refs_1_
  246.2 1.8 collective-permute-done.13.refs_2_
  248.0 3.7 collective-permute-start.21
  254.9 3.4 collective-permute-start.14
  258.3 35.2 %collective-permute-done.8.refs_0_ = bf16[128,2048]{1,0:T(8,128)(2,1)S(1)} collective-permute-done((bf16[128,2048]{1,0:T(8,128)(2,1)S(1)}, bf16[128,2048]{1,0:T(8,128)(2,1)S(1)}, u32[]{:S(2)}, u32[]{:S(2)}) %collective-permute-start.8) | collective-permute-done | bytes 524320 | tf_op jit(solution)/shard_map/ppermute | solution.py:382
  294.7 3.0 collective-permute-start.22
  297.8 14.4 %mlp.8 = f32[256,2048]{1,0:T(8,128)S(1)} custom-call(bf16[128,2048]{1,0:T(8,128)(2,1)S(1)} %collective-permute-done.8.refs_0_, bf16[128,2048]{1,0:T(8,128)(2,1)S(1)} %collective-permute-done.14.refs_1_, bf16[2048,2048]{1,0:T(8,128)(2,1)} %bitcast.43, bf16[2048,2048]{1,0:T(8,128)(2,1)} %bitcast.47, bf16[2048,2048]{1,0:T(8,128)(2,1)} %bitcast.51), custom_call_target="tpu_custom_call" | custom-call | flops 6442450944 | bytes 25165824 | tf_op jit(solution)/shard_map/mlp/pallas_call | solution.py:235
  313.4 3.6 collective-permute-start.17
  317.0 27.7 %mlp.9 = (f32[256,2048]{1,0:T(8,128)S(1)}, f32[256,2048]{1,0:T(8,128)}, f32[256,2048]{1,0:T(8,128)}) custom-call(bf16[256,2048]{1,0:T(8,128)(2,1)} %get-tuple-element.59.refs_0_, bf16[256,2048]{1,0:T(8,128)(2,1)} %collective-permute-done.7.refs_1_, bf16[256,2048]{1,0:T(8,128)(2,1)} %collective-permute-done.13.refs_2_, bf16[2048,2048]{1,0:T(8,128)(2,1)} %bitcast.44, ...), custom_call_target="tpu_custom_call" | custom-call | flops 19327352832 | bytes 25165824 | tf_op jit(solution)/shard_map/mlp/pallas_call | solution.py:235
  344.7 14.4 %mlp.10 = f32[256,2048]{1,0:T(8,128)S(1)} custom-call(bf16[128,2048]{1,0:T(8,128)(2,1)S(1)} %collective-permute-done.20.refs_0_, bf16[128,2048]{1,0:T(8,128)(2,1)S(1)} %collective-permute-done.22.refs_1_, bf16[2048,2048]{1,0:T(8,128)(2,1)} %bitcast.45, bf16[2048,2048]{1,0:T(8,128)(2,1)} %bitcast.49, bf16[2048,2048]{1,0:T(8,128)(2,1)} %bitcast.53), custom_call_target="tpu_custom_call" | custom-call | flops 6442450944 | bytes 25165824 | tf_op jit(solution)/shard_map/mlp/pallas_call | solution.py:235
  360.8 3.2 collective-permute-start.30
  369.0 2.0 collective-permute-start.18
  371.0 25.6 %mlp.11 = (f32[256,2048]{1,0:T(8,128)S(1)}, f32[256,2048]{1,0:T(8,128)}, f32[256,2048]{1,0:T(8,128)}) custom-call(bf16[256,2048]{1,0:T(8,128)(2,1)S(1)} %copy-done.29, bf16[256,2048]{1,0:T(8,128)(2,1)S(1)} %copy-done.15, bf16[256,2048]{1,0:T(8,128)(2,1)S(1)} %copy-done.17, bf16[2048,2048]{1,0:T(8,128)(2,1)} %bitcast.46, bf16[2048,2048]{1,0:T(8,128)(2,1)} %bitcast.50, ...), custom_call_target="tpu_custom_call" | custom-call | flops 19327352832 | bytes 25165824 | tf_op jit(solution)/shard_map/mlp/pallas_call | solution.py:235
  396.6 2.9 slice_add_fusion.5
  403.7 2.7 collective-permute-start.31
  406.3 26.9 %collective-permute-done.16 = f32[256,2048]{1,0:T(8,128)S(1)} collective-permute-done((f32[256,2048]{1,0:T(8,128)S(1)}, f32[256,2048]{1,0:T(8,128)S(1)}, u32[]{:S(2)}, u32[]{:S(2)}) %collective-permute-start.16) | collective-permute-done | bytes 2097184 | tf_op jit(solution)/shard_map/ppermute | solution.py:382
  433.2 2.4 add_add_fusion.1.resid_ref
  435.6 8.3 %qkv.6 = (bf16[4,256,512]{2,1,0:T(8,128)(2,1)S(1)}, bf16[4,256,256]{2,1,0:T(8,128)(2,1)S(1)}) custom-call(f32[256,2048]{1,0:T(8,128)S(1)} %add_add_fusion.1.resid_ref, bf16[1,2048]{1,0:T(2,128)(2,1)S(1)} %get-tuple-element.141.gain_ref, f32[256,128]{1,0:T(8,128)S(1)} %pad_maximum_fusion.11.cos_ref, f32[256,128]{1,0:T(8,128)S(1)} %pad_maximum_fusion.12.sin_ref, ...), custom_call_target="tpu_custom_call" | custom-call | flops 3221225472 | bytes 12582912 | tf_op jit(solution)/shard_map/qkv/pallas_call | solution.py:63
  445.0 3.5 collective-permute-start.25
  448.5 35.0 %collective-permute-done.24.left_ref = bf16[4,256,256]{2,1,0:T(8,128)(2,1)S(1)} collective-permute-done((bf16[4,256,256]{2,1,0:T(8,128)(2,1)S(1)}, bf16[4,256,256]{2,1,0:T(8,128)(2,1)S(1)}, u32[]{:S(2)}, u32[]{:S(2)}) %collective-permute-start.24) | collective-permute-done | bytes 524320 | tf_op jit(solution)/shard_map/ppermute | solution.py:382
  484.9 3.2 collective-permute-start.27
  488.2 3.9 collective-permute-done.26.opp_lo_ref
  495.9 26.3 %attn.6 = (f32[256,2048]{1,0:T(8,128)S(1)}, bf16[256,2048]{1,0:T(8,128)(2,1)S(1)}) custom-call(bf16[4,256,512]{2,1,0:T(8,128)(2,1)S(1)} %copy-done.37, bf16[4,256,256]{2,1,0:T(8,128)(2,1)S(1)} %copy-done.43, bf16[4,256,256]{2,1,0:T(8,128)(2,1)S(1)} %collective-permute-done.24.left_ref, bf16[4,256,256]{2,1,0:T(8,128)(2,1)S(1)} %collective-permute-done.25.right_ref, ...), custom_call_target="tpu_custom_call" | custom-call | flops 10737418240 | bytes 8388608 | tf_op jit(solution)/shard_map/attn/pallas_call | solution.py:164
  522.3 3.8 collective-permute-start.33
  526.1 3.0 add_add_fusion.resid_ref
  529.2 7.9 qkv.7
  538.1 3.2 collective-permute-start.36
  542.1 5.3 collective-permute-done.28.refs_1_
  548.6 3.1 collective-permute-start.34
  551.7 7.0 collective-permute-done.35.left_ref
  560.2 3.4 collective-permute-start.38
  564.9 14.0 %mlp.12 = f32[256,2048]{1,0:T(8,128)S(1)} custom-call(bf16[128,2048]{1,0:T(8,128)(2,1)S(1)} %collective-permute-done.32.refs_0_, bf16[128,2048]{1,0:T(8,128)(2,1)S(1)} %collective-permute-done.34.refs_1_, bf16[2048,2048]{1,0:T(8,128)(2,1)} %bitcast.35, bf16[2048,2048]{1,0:T(8,128)(2,1)} %bitcast.39, bf16[2048,2048]{1,0:T(8,128)(2,1)} %bitcast.55), custom_call_target="tpu_custom_call" | custom-call | flops 6442450944 | bytes 25165824 | tf_op jit(solution)/shard_map/mlp/pallas_call | solution.py:235
  581.7 26.1 %attn.7 = (f32[256,2048]{1,0:T(8,128)S(1)}, bf16[256,2048]{1,0:T(8,128)(2,1)S(1)}) custom-call(bf16[4,256,512]{2,1,0:T(8,128)(2,1)S(1)} %copy-done.35, bf16[4,256,256]{2,1,0:T(8,128)(2,1)S(1)} %copy-done.41, bf16[4,256,256]{2,1,0:T(8,128)(2,1)S(1)} %copy-done.25, bf16[4,256,256]{2,1,0:T(8,128)(2,1)S(1)} %copy-done.27, ...), custom_call_target="tpu_custom_call" | custom-call | flops 10737418240 | bytes 8388608 | tf_op jit(solution)/shard_map/attn/pallas_call | solution.py:164
  609.0 2.1 collective-permute-start.45
  611.1 3.2 collective-permute-start.41
  614.4 25.5 %mlp.13 = (f32[256,2048]{1,0:T(8,128)S(1)}, f32[256,2048]{1,0:T(8,128)}, f32[256,2048]{1,0:T(8,128)}) custom-call(bf16[256,2048]{1,0:T(8,128)(2,1)S(1)} %copy-done.31, bf16[256,2048]{1,0:T(8,128)(2,1)S(1)} %copy-done.19, bf16[256,2048]{1,0:T(8,128)(2,1)S(1)} %copy-done.21, bf16[2048,2048]{1,0:T(8,128)(2,1)} %bitcast.36, bf16[2048,2048]{1,0:T(8,128)(2,1)} %bitcast.40, ...), custom_call_target="tpu_custom_call" | custom-call | flops 19327352832 | bytes 25165824 | tf_op jit(solution)/shard_map/mlp/pallas_call | solution.py:235
  639.9 10.4 %collective-permute-done.39 = f32[128,2048]{1,0:T(8,128)S(1)} collective-permute-done((f32[128,2048]{1,0:T(8,128)}, f32[128,2048]{1,0:T(8,128)S(1)}, u32[]{:S(2)}, u32[]{:S(2)}) %collective-permute-start.39) | collective-permute-done | bytes 1048608 | tf_op jit(solution)/shard_map/ppermute | solution.py:382
  653.5 2.1 collective-permute-start.44
  658.9 2.0 collective-permute-start.42
  660.9 41.5 %collective-permute-done.44.refs_0_ = bf16[128,2048]{1,0:T(8,128)(2,1)S(1)} collective-permute-done((bf16[128,2048]{1,0:T(8,128)(2,1)S(1)}, bf16[128,2048]{1,0:T(8,128)(2,1)S(1)}, u32[]{:S(2)}, u32[]{:S(2)}) %collective-permute-start.44) | collective-permute-done | bytes 524320 | tf_op jit(solution)/shard_map/ppermute | solution.py:382
  702.4 14.0 %mlp.14 = f32[256,2048]{1,0:T(8,128)S(1)} custom-call(bf16[128,2048]{1,0:T(8,128)(2,1)S(1)} %collective-permute-done.44.refs_0_, bf16[128,2048]{1,0:T(8,128)(2,1)S(1)} %collective-permute-done.46.refs_1_, bf16[2048,2048]{1,0:T(8,128)(2,1)} %bitcast.37, bf16[2048,2048]{1,0:T(8,128)(2,1)} %bitcast.41, bf16[2048,2048]{1,0:T(8,128)(2,1)} %bitcast.57), custom_call_target="tpu_custom_call" | custom-call | flops 6442450944 | bytes 25165824 | tf_op jit(solution)/shard_map/mlp/pallas_call | solution.py:235
  717.6 3.5 collective-permute-start.49
  721.1 25.5 %mlp.15 = (f32[256,2048]{1,0:T(8,128)S(1)}, f32[256,2048]{1,0:T(8,128)}, f32[256,2048]{1,0:T(8,128)}) custom-call(bf16[256,2048]{1,0:T(8,128)(2,1)S(1)} %get-tuple-element.86.refs_0_, bf16[256,2048]{1,0:T(8,128)(2,1)S(1)} %collective-permute-done.43.refs_1_, bf16[256,2048]{1,0:T(8,128)(2,1)S(1)} %collective-permute-done.45.refs_2_, ...), custom_call_target="tpu_custom_call" | custom-call | flops 19327352832 | bytes 25165824 | tf_op jit(solution)/shard_map/mlp/pallas_call | solution.py:235
  750.4 2.1 collective-permute-start.50
  752.5 2.4 add_bitcast_fusion.1
  754.9 29.8 %collective-permute-done.48 = f32[256,2048]{1,0:T(8,128)S(1)} collective-permute-done((f32[256,2048]{1,0:T(8,128)S(1)}, f32[256,2048]{1,0:T(8,128)S(1)}, u32[]{:S(2)}, u32[]{:S(2)}) %collective-permute-start.48) | collective-permute-done | bytes 2097184 | tf_op jit(solution)/shard_map/ppermute | solution.py:382
  786.1 2.5 pad_maximum_fusion
  (272 shorter events, 67.0 us)
Async XLA Ops:
  6.5 291.2 %all-gather.18.cloned.1.call-start = ((), (), s32[]{:S(2)}) async-start(), calls=%async_computation.1 | async-start | bytes 9437184 | tf_op jit(solution)/shard_map/all_gather | solution.py:412
  9.9 287.8 %all-gather.20.cloned.1.call-start = ((), (), s32[]{:S(2)}) async-start(), calls=%async_computation.2 | async-start | bytes 9437184 | tf_op jit(solution)/shard_map/all_gather | solution.py:413
  11.5 286.2 %all-gather.22.cloned.1.call-start = ((), (), s32[]{:S(2)}) async-start(), calls=%async_computation.3 | async-start | bytes 9437184 | tf_op jit(solution)/shard_map/all_gather | solution.py:414
  14.7 420.9 %all-gather.24.cloned.1.call-start = ((), (), s32[]{:S(2)}) async-start(), calls=%async_computation.4 | async-start | bytes 12976128 | tf_op jit(solution)/shard_map/all_gather | solution.py:408
  16.7 471.5 %all-gather.16.cloned.1.call-start = ((), (), s32[]{:S(2)}) async-start(), calls=%async_computation | async-start | bytes 8650752 | tf_op jit(solution)/shard_map/all_gather | solution.py:409
  17.7 547.2 %all-gather.26.cloned.1.call-start = ((), (), s32[]{:S(2)}) async-start(), calls=%async_computation.5 | async-start | bytes 9437184 | tf_op jit(solution)/shard_map/all_gather | solution.py:412
  18.3 546.6 %all-gather.28.cloned.1.call-start = ((), (), s32[]{:S(2)}) async-start(), calls=%async_computation.6 | async-start | bytes 9437184 | tf_op jit(solution)/shard_map/all_gather | solution.py:413
  18.4 107.3 %collective-permute-start = (s32[2,256]{1,0:T(2,128)S(1)}, s32[2,256]{1,0:T(2,128)S(1)}, u32[]{:S(2)}, u32[]{:S(2)}) collective-permute-start(s32[2,256]{1,0:T(2,128)S(1)} %copy-done.56), channel_id=1, source_target_pairs={{0,8},{8,16},{16,24},{24,0},{1,9},{9,17},{17,25},{25,1},{2,10},{10... | collective-permute-start | bytes 6152 | tf_op jit(solution)/shard_map/ppermute | solution.py:382
  20.6 105.5 %collective-permute-start.1 = (s32[2,256]{1,0:T(2,128)S(1)}, s32[2,256]{1,0:T(2,128)S(1)}, u32[]{:S(2)}, u32[]{:S(2)}) collective-permute-start(s32[2,256]{1,0:T(2,128)S(1)} %copy-done.56), channel_id=1, source_target_pairs={{0,24},{8,0},{16,8},{24,16},{1,25},{9,1},{17,9},{25,17},{2,26},{10... | collective-permute-start | bytes 6152 | tf_op jit(solution)/shard_map/ppermute | solution.py:385
  23.3 541.6 %all-gather.30.cloned.1.call-start = ((), (), s32[]{:S(2)}) async-start(), calls=%async_computation.7 | async-start | bytes 9437184 | tf_op jit(solution)/shard_map/all_gather | solution.py:414
  125.7 4.9 collective-permute-start.2
  142.2 15.8 %collective-permute-start.3 = (bf16[4,256,256]{2,1,0:T(8,128)(2,1)S(1)}, bf16[4,256,256]{2,1,0:T(8,128)(2,1)S(1)}, u32[]{:S(2)}, u32[]{:S(2)}) collective-permute-start(bf16[4,256,256]{2,1,0:T(8,128)(2,1)S(1)} %get-tuple-element.53.own_ref), channel_id=1, source_target_pairs={{0,8},{8,16},{16,24},{24,0},{1,9},{9,17},{17,25},{25,1},{2,10},{10... | collective-permute-start | bytes 1572872 | tf_op jit(solution)/shard_map/ppermute | solution.py:382
  142.3 15.9 %collective-permute-start.4 = (bf16[4,256,256]{2,1,0:T(8,128)(2,1)S(1)}, bf16[4,256,256]{2,1,0:T(8,128)(2,1)S(1)}, u32[]{:S(2)}, u32[]{:S(2)}) collective-permute-start(bf16[4,256,256]{2,1,0:T(8,128)(2,1)S(1)} %get-tuple-element.53.own_ref), channel_id=1, source_target_pairs={{0,24},{8,0},{16,8},{24,16},{1,25},{9,1},{17,9},{25,17},{2,26},{10... | collective-permute-start | bytes 1572872 | tf_op jit(solution)/shard_map/ppermute | solution.py:385
  154.8 16.0 %collective-permute-start.9 = (bf16[4,256,256]{2,1,0:T(8,128)(2,1)S(1)}, bf16[4,256,256]{2,1,0:T(8,128)(2,1)S(1)}, u32[]{:S(2)}, u32[]{:S(2)}) collective-permute-start(bf16[4,256,256]{2,1,0:T(8,128)(2,1)S(1)} %get-tuple-element.55.own_ref), channel_id=1, source_target_pairs={{0,8},{8,16},{16,24},{24,0},{1,9},{9,17},{17,25},{25,1},{2,10},{10... | collective-permute-start | bytes 1572872 | tf_op jit(solution)/shard_map/ppermute | solution.py:382
  154.8 16.7 %collective-permute-start.10 = (bf16[4,256,256]{2,1,0:T(8,128)(2,1)S(1)}, bf16[4,256,256]{2,1,0:T(8,128)(2,1)S(1)}, u32[]{:S(2)}, u32[]{:S(2)}) collective-permute-start(bf16[4,256,256]{2,1,0:T(8,128)(2,1)S(1)} %get-tuple-element.55.own_ref), channel_id=1, source_target_pairs={{0,24},{8,0},{16,8},{24,16},{1,25},{9,1},{17,9},{25,17},{2,26},{10... | collective-permute-start | bytes 1572872 | tf_op jit(solution)/shard_map/ppermute | solution.py:385
  158.1 18.4 %collective-permute-start.5 = (bf16[2,256,256]{2,1,0:T(8,128)(2,1)S(1)}, bf16[2,256,256]{2,1,0:T(8,128)(2,1)S(1)}, u32[]{:S(2)}, u32[]{:S(2)}) collective-permute-start(bf16[2,256,256]{2,1,0:T(8,128)(2,1)S(1)} %slice.262), channel_id=1, source_target_pairs={{0,8},{8,16},{16,24},{24,0},{1,9},{9,17},{17,25},{25,1},{2,10},{10... | collective-permute-start | bytes 786440 | tf_op jit(solution)/shard_map/ppermute | solution.py:382
  158.3 18.3 %collective-permute-start.6 = (bf16[2,256,256]{2,1,0:T(8,128)(2,1)S(1)}, bf16[2,256,256]{2,1,0:T(8,128)(2,1)S(1)}, u32[]{:S(2)}, u32[]{:S(2)}) collective-permute-start(bf16[2,256,256]{2,1,0:T(8,128)(2,1)S(1)} %slice.263), channel_id=1, source_target_pairs={{0,24},{8,0},{16,8},{24,16},{1,25},{9,1},{17,9},{25,17},{2,26},{10... | collective-permute-start | bytes 786440 | tf_op jit(solution)/shard_map/ppermute | solution.py:385
  163.0 40.5 %copy-start.12 = (f32[256,1024]{1,0:T(8,128)}, f32[256,1024]{1,0:T(8,128)S(1)}, u32[]{:S(2)}) copy-start(f32[256,1024]{1,0:T(8,128)S(1)} %get-tuple-element.146.bound_ref) | copy-start | bytes 3145732
  171.5 36.7 %collective-permute-start.11 = (bf16[2,256,256]{2,1,0:T(8,128)(2,1)}, bf16[2,256,256]{2,1,0:T(8,128)(2,1)S(1)}, u32[]{:S(2)}, u32[]{:S(2)}) collective-permute-start(bf16[2,256,256]{2,1,0:T(8,128)(2,1)} %slice.265), channel_id=1, source_target_pairs={{0,8},{8,16},{16,24},{24,0},{1,9},{9,17},{17,25},{25,1},{2,10},{10... | collective-permute-start | bytes 786440 | tf_op jit(solution)/shard_map/ppermute | solution.py:382
  173.1 35.1 %collective-permute-start.12 = (bf16[2,256,256]{2,1,0:T(8,128)(2,1)}, bf16[2,256,256]{2,1,0:T(8,128)(2,1)}, u32[]{:S(2)}, u32[]{:S(2)}) collective-permute-start(bf16[2,256,256]{2,1,0:T(8,128)(2,1)} %slice.266), channel_id=1, source_target_pairs={{0,24},{8,0},{16,8},{24,16},{1,25},{9,1},{17,9},{25,17},{2,26},{10... | collective-permute-start | bytes 786440 | tf_op jit(solution)/shard_map/ppermute | solution.py:385
  204.9 41.3 %collective-permute-start.7 = (bf16[256,2048]{1,0:T(8,128)(2,1)}, bf16[256,2048]{1,0:T(8,128)(2,1)}, u32[]{:S(2)}, u32[]{:S(2)}) collective-permute-start(bf16[256,2048]{1,0:T(8,128)(2,1)} %get-tuple-element.59.refs_0_), channel_id=1, source_target_pairs={{0,8},{8,16},{16,24},{24,0},{1,9},{9,17},{17,25},{25,1},{2,10},{10... | collective-permute-start | bytes 3145736 | tf_op jit(solution)/shard_map/ppermute | solution.py:382
  204.9 43.0 %collective-permute-start.13 = (bf16[256,2048]{1,0:T(8,128)(2,1)}, bf16[256,2048]{1,0:T(8,128)(2,1)}, u32[]{:S(2)}, u32[]{:S(2)}) collective-permute-start(bf16[256,2048]{1,0:T(8,128)(2,1)} %get-tuple-element.59.refs_0_), channel_id=1, source_target_pairs={{0,24},{8,0},{16,8},{24,16},{1,25},{9,1},{17,9},{25,17},{2,26},{10... | collective-permute-start | bytes 3145736 | tf_op jit(solution)/shard_map/ppermute | solution.py:385
  238.2 56.4 %copy-start.2 = (f32[256,2048]{1,0:T(8,128)}, f32[256,2048]{1,0:T(8,128)S(1)}, u32[]{:S(2)}) copy-start(f32[256,2048]{1,0:T(8,128)S(1)} %get-tuple-element.79) | copy-start | bytes 6291460
  248.0 45.5 %collective-permute-start.19 = (bf16[256,2048]{1,0:T(8,128)(2,1)S(1)}, bf16[256,2048]{1,0:T(8,128)(2,1)S(1)}, u32[]{:S(2)}, u32[]{:S(2)}) collective-permute-start(bf16[256,2048]{1,0:T(8,128)(2,1)S(1)} %get-tuple-element.68.refs_0_), channel_id=1, source_target_pairs={{0,8},{8,16},{16,24},{24,0},{1,9},{9,17},{17,25},{25,1},{2,10},{10... | collective-permute-start | bytes 3145736 | tf_op jit(solution)/shard_map/ppermute | solution.py:382
  248.0 45.8 %collective-permute-start.21 = (bf16[256,2048]{1,0:T(8,128)(2,1)S(1)}, bf16[256,2048]{1,0:T(8,128)(2,1)S(1)}, u32[]{:S(2)}, u32[]{:S(2)}) collective-permute-start(bf16[256,2048]{1,0:T(8,128)(2,1)S(1)} %get-tuple-element.68.refs_0_), channel_id=1, source_target_pairs={{0,24},{8,0},{16,8},{24,16},{1,25},{9,1},{17,9},{25,17},{2,26},{10... | collective-permute-start | bytes 3145736 | tf_op jit(solution)/shard_map/ppermute | solution.py:385
  253.7 39.7 %collective-permute-start.8 = (bf16[128,2048]{1,0:T(8,128)(2,1)S(1)}, bf16[128,2048]{1,0:T(8,128)(2,1)S(1)}, u32[]{:S(2)}, u32[]{:S(2)}) collective-permute-start(bf16[128,2048]{1,0:T(8,128)(2,1)S(1)} %slice.264), channel_id=1, source_target_pairs={{0,8},{8,16},{16,24},{24,0},{1,9},{9,17},{17,25},{25,1},{2,10},{10... | collective-permute-start | bytes 1572872 | tf_op jit(solution)/shard_map/ppermute | solution.py:382
  254.9 42.8 %collective-permute-start.14 = (bf16[128,2048]{1,0:T(8,128)(2,1)S(1)}, bf16[128,2048]{1,0:T(8,128)(2,1)S(1)}, u32[]{:S(2)}, u32[]{:S(2)}) collective-permute-start(bf16[128,2048]{1,0:T(8,128)(2,1)S(1)} %slice.267), channel_id=1, source_target_pairs={{0,24},{8,0},{16,8},{24,16},{1,25},{9,1},{17,9},{25,17},{2,26},{10... | collective-permute-start | bytes 1572872 | tf_op jit(solution)/shard_map/ppermute | solution.py:385
  293.5 51.2 %collective-permute-start.20 = (bf16[128,2048]{1,0:T(8,128)(2,1)S(1)}, bf16[128,2048]{1,0:T(8,128)(2,1)S(1)}, u32[]{:S(2)}, u32[]{:S(2)}) collective-permute-start(bf16[128,2048]{1,0:T(8,128)(2,1)S(1)} %slice.270), channel_id=1, source_target_pairs={{0,8},{8,16},{16,24},{24,0},{1,9},{9,17},{17,25},{25,1},{2,10},{10... | collective-permute-start | bytes 1572872 | tf_op jit(solution)/shard_map/ppermute | solution.py:382
  294.7 50.0 %collective-permute-start.22 = (bf16[128,2048]{1,0:T(8,128)(2,1)}, bf16[128,2048]{1,0:T(8,128)(2,1)S(1)}, u32[]{:S(2)}, u32[]{:S(2)}) collective-permute-start(bf16[128,2048]{1,0:T(8,128)(2,1)} %slice.271), channel_id=1, source_target_pairs={{0,24},{8,0},{16,8},{24,16},{1,25},{9,1},{17,9},{25,17},{2,26},{10... | collective-permute-start | bytes 1572872 | tf_op jit(solution)/shard_map/ppermute | solution.py:385
  313.4 50.7 %collective-permute-start.15 = (f32[128,2048]{1,0:T(8,128)S(1)}, f32[128,2048]{1,0:T(8,128)S(1)}, u32[]{:S(2)}, u32[]{:S(2)}) collective-permute-start(f32[128,2048]{1,0:T(8,128)S(1)} %get-tuple-element.119), channel_id=1, source_target_pairs={{0,8},{8,16},{16,24},{24,0},{1,9},{9,17},{17,25},{25,1},{2,10},{10... | collective-permute-start | bytes 3145736 | tf_op jit(solution)/shard_map/ppermute | solution.py:382
  313.4 51.3 %collective-permute-start.17 = (f32[128,2048]{1,0:T(8,128)}, f32[128,2048]{1,0:T(8,128)}, u32[]{:S(2)}, u32[]{:S(2)}) collective-permute-start(f32[128,2048]{1,0:T(8,128)} %get-tuple-element.120), channel_id=1, source_target_pairs={{0,24},{8,0},{16,8},{24,16},{1,25},{9,1},{17,9},{25,17},{2,26},{10... | collective-permute-start | bytes 3145736 | tf_op jit(solution)/shard_map/ppermute | solution.py:385
  360.8 35.8 %collective-permute-start.23 = (f32[128,2048]{1,0:T(8,128)}, f32[128,2048]{1,0:T(8,128)}, u32[]{:S(2)}, u32[]{:S(2)}) collective-permute-start(f32[128,2048]{1,0:T(8,128)} %get-tuple-element.125), channel_id=1, source_target_pairs={{0,8},{8,16},{16,24},{24,0},{1,9},{9,17},{17,25},{25,1},{2,10},{10... | collective-permute-start | bytes 3145736 | tf_op jit(solution)/shard_map/ppermute | solution.py:382
  360.8 40.7 %collective-permute-start.30 = (f32[128,2048]{1,0:T(8,128)}, f32[128,2048]{1,0:T(8,128)S(1)}, u32[]{:S(2)}, u32[]{:S(2)}) collective-permute-start(f32[128,2048]{1,0:T(8,128)} %get-tuple-element.126), channel_id=1, source_target_pairs={{0,24},{8,0},{16,8},{24,16},{1,25},{9,1},{17,9},{25,17},{2,26},{10... | collective-permute-start | bytes 3145736 | tf_op jit(solution)/shard_map/ppermute | solution.py:385
  364.5 68.7 %collective-permute-start.16 = (f32[256,2048]{1,0:T(8,128)S(1)}, f32[256,2048]{1,0:T(8,128)S(1)}, u32[]{:S(2)}, u32[]{:S(2)}) collective-permute-start(f32[256,2048]{1,0:T(8,128)S(1)} %pad_maximum_fusion.1), channel_id=1, source_target_pairs={{0,8},{8,16},{16,24},{24,0},{1,9},{9,17},{17,25},{25,1},{2,10},{10... | collective-permute-start | bytes 6291464 | tf_op jit(solution)/shard_map/ppermute | solution.py:382
  369.0 64.2 %collective-permute-start.18 = (f32[256,2048]{1,0:T(8,128)}, f32[256,2048]{1,0:T(8,128)}, u32[]{:S(2)}, u32[]{:S(2)}) collective-permute-start(f32[256,2048]{1,0:T(8,128)} %pad_maximum_fusion.2), channel_id=1, source_target_pairs={{0,24},{8,0},{16,8},{24,16},{1,25},{9,1},{17,9},{25,17},{2,26},{10... | collective-permute-start | bytes 6291464 | tf_op jit(solution)/shard_map/ppermute | solution.py:385
  401.1 125.0 %collective-permute-start.29 = (f32[256,2048]{1,0:T(8,128)}, f32[256,2048]{1,0:T(8,128)}, u32[]{:S(2)}, u32[]{:S(2)}) collective-permute-start(f32[256,2048]{1,0:T(8,128)} %pad_maximum_fusion.3), channel_id=1, source_target_pairs={{0,8},{8,16},{16,24},{24,0},{1,9},{9,17},{17,25},{25,1},{2,10},{10... | collective-permute-start | bytes 6291464 | tf_op jit(solution)/shard_map/ppermute | solution.py:382
  403.7 122.5 %collective-permute-start.31 = (f32[256,2048]{1,0:T(8,128)}, f32[256,2048]{1,0:T(8,128)}, u32[]{:S(2)}, u32[]{:S(2)}) collective-permute-start(f32[256,2048]{1,0:T(8,128)} %pad_maximum_fusion.4), channel_id=1, source_target_pairs={{0,24},{8,0},{16,8},{24,16},{1,25},{9,1},{17,9},{25,17},{2,26},{10... | collective-permute-start | bytes 6291464 | tf_op jit(solution)/shard_map/ppermute | solution.py:385
  445.0 39.2 %copy-start.42 = (bf16[4,256,256]{2,1,0:T(8,128)(2,1)}, bf16[4,256,256]{2,1,0:T(8,128)(2,1)S(1)}, u32[]{:S(2)}) copy-start(bf16[4,256,256]{2,1,0:T(8,128)(2,1)S(1)} %get-tuple-element.74.own_ref) | copy-start | bytes 1572868
  445.0 38.5 %collective-permute-start.24 = (bf16[4,256,256]{2,1,0:T(8,128)(2,1)S(1)}, bf16[4,256,256]{2,1,0:T(8,128)(2,1)S(1)}, u32[]{:S(2)}, u32[]{:S(2)}) collective-permute-start(bf16[4,256,256]{2,1,0:T(8,128)(2,1)S(1)} %get-tuple-element.74.own_ref), channel_id=1, source_target_pairs={{0,8},{8,16},{16,24},{24,0},{1,9},{9,17},{17,25},{25,1},{2,10},{10... | collective-permute-start | bytes 1572872 | tf_op jit(solution)/shard_map/ppermute | solution.py:382
  445.0 39.2 %collective-permute-start.25 = (bf16[4,256,256]{2,1,0:T(8,128)(2,1)S(1)}, bf16[4,256,256]{2,1,0:T(8,128)(2,1)S(1)}, u32[]{:S(2)}, u32[]{:S(2)}) collective-permute-start(bf16[4,256,256]{2,1,0:T(8,128)(2,1)S(1)} %get-tuple-element.74.own_ref), channel_id=1, source_target_pairs={{0,24},{8,0},{16,8},{24,16},{1,25},{9,1},{17,9},{25,17},{2,26},{10... | collective-permute-start | bytes 1572872 | tf_op jit(solution)/shard_map/ppermute | solution.py:385
  484.2 7.9 collective-permute-start.26
  484.9 7.4 collective-permute-start.27
  522.2 25.2 %collective-permute-start.28 = (bf16[256,2048]{1,0:T(8,128)(2,1)S(1)}, bf16[256,2048]{1,0:T(8,128)(2,1)S(1)}, u32[]{:S(2)}, u32[]{:S(2)}) collective-permute-start(bf16[256,2048]{1,0:T(8,128)(2,1)S(1)} %get-tuple-element.78.refs_0_), channel_id=1, source_target_pairs={{0,8},{8,16},{16,24},{24,0},{1,9},{9,17},{17,25},{25,1},{2,10},{10... | collective-permute-start | bytes 3145736 | tf_op jit(solution)/shard_map/ppermute | solution.py:382
  522.3 25.2 %collective-permute-start.33 = (bf16[256,2048]{1,0:T(8,128)(2,1)S(1)}, bf16[256,2048]{1,0:T(8,128)(2,1)S(1)}, u32[]{:S(2)}, u32[]{:S(2)}) collective-permute-start(bf16[256,2048]{1,0:T(8,128)(2,1)S(1)} %get-tuple-element.78.refs_0_), channel_id=1, source_target_pairs={{0,24},{8,0},{16,8},{24,16},{1,25},{9,1},{17,9},{25,17},{2,26},{10... | collective-permute-start | bytes 3145736 | tf_op jit(solution)/shard_map/ppermute | solution.py:385
  538.1 20.6 %collective-permute-start.35 = (bf16[4,256,256]{2,1,0:T(8,128)(2,1)S(1)}, bf16[4,256,256]{2,1,0:T(8,128)(2,1)S(1)}, u32[]{:S(2)}, u32[]{:S(2)}) collective-permute-start(bf16[4,256,256]{2,1,0:T(8,128)(2,1)S(1)} %get-tuple-element.83.own_ref), channel_id=1, source_target_pairs={{0,8},{8,16},{16,24},{24,0},{1,9},{9,17},{17,25},{25,1},{2,10},{10... | collective-permute-start | bytes 1572872 | tf_op jit(solution)/shard_map/ppermute | solution.py:382
  538.1 21.3 %collective-permute-start.36 = (bf16[4,256,256]{2,1,0:T(8,128)(2,1)S(1)}, bf16[4,256,256]{2,1,0:T(8,128)(2,1)S(1)}, u32[]{:S(2)}, u32[]{:S(2)}) collective-permute-start(bf16[4,256,256]{2,1,0:T(8,128)(2,1)S(1)} %get-tuple-element.83.own_ref), channel_id=1, source_target_pairs={{0,24},{8,0},{16,8},{24,16},{1,25},{9,1},{17,9},{25,17},{2,26},{10... | collective-permute-start | bytes 1572872 | tf_op jit(solution)/shard_map/ppermute | solution.py:385
  547.4 17.5 %collective-permute-start.32 = (bf16[128,2048]{1,0:T(8,128)(2,1)S(1)}, bf16[128,2048]{1,0:T(8,128)(2,1)S(1)}, u32[]{:S(2)}, u32[]{:S(2)}) collective-permute-start(bf16[128,2048]{1,0:T(8,128)(2,1)S(1)} %slice.276), channel_id=1, source_target_pairs={{0,8},{8,16},{16,24},{24,0},{1,9},{9,17},{17,25},{25,1},{2,10},{10... | collective-permute-start | bytes 1572872 | tf_op jit(solution)/shard_map/ppermute | solution.py:382
  548.6 16.3 %collective-permute-start.34 = (bf16[128,2048]{1,0:T(8,128)(2,1)}, bf16[128,2048]{1,0:T(8,128)(2,1)S(1)}, u32[]{:S(2)}, u32[]{:S(2)}) collective-permute-start(bf16[128,2048]{1,0:T(8,128)(2,1)} %slice.277), channel_id=1, source_target_pairs={{0,24},{8,0},{16,8},{24,16},{1,25},{9,1},{17,9},{25,17},{2,26},{10... | collective-permute-start | bytes 1572872 | tf_op jit(solution)/shard_map/ppermute | solution.py:385
  559.4 21.2 %collective-permute-start.37 = (bf16[2,256,256]{2,1,0:T(8,128)(2,1)}, bf16[2,256,256]{2,1,0:T(8,128)(2,1)S(1)}, u32[]{:S(2)}, u32[]{:S(2)}) collective-permute-start(bf16[2,256,256]{2,1,0:T(8,128)(2,1)} %slice.278), channel_id=1, source_target_pairs={{0,8},{8,16},{16,24},{24,0},{1,9},{9,17},{17,25},{25,1},{2,10},{10... | collective-permute-start | bytes 786440 | tf_op jit(solution)/shard_map/ppermute | solution.py:382
  560.2 20.4 %collective-permute-start.38 = (bf16[2,256,256]{2,1,0:T(8,128)(2,1)}, bf16[2,256,256]{2,1,0:T(8,128)(2,1)}, u32[]{:S(2)}, u32[]{:S(2)}) collective-permute-start(bf16[2,256,256]{2,1,0:T(8,128)(2,1)} %slice.279), channel_id=1, source_target_pairs={{0,24},{8,0},{16,8},{24,16},{1,25},{9,1},{17,9},{25,17},{2,26},{10... | collective-permute-start | bytes 786440 | tf_op jit(solution)/shard_map/ppermute | solution.py:385
  580.6 33.8 %copy-start.21 = (bf16[256,2048]{1,0:T(8,128)(2,1)S(1)}, bf16[256,2048]{1,0:T(8,128)(2,1)}, u32[]{:S(2)}) copy-start(bf16[256,2048]{1,0:T(8,128)(2,1)} %copy-done.20) | copy-start | bytes 3145732
  580.6 33.8 %copy-start.31 = (bf16[256,2048]{1,0:T(8,128)(2,1)S(1)}, bf16[256,2048]{1,0:T(8,128)(2,1)}, u32[]{:S(2)}) copy-start(bf16[256,2048]{1,0:T(8,128)(2,1)} %copy-done.30) | copy-start | bytes 3145732
  607.8 45.7 %collective-permute-start.43 = (bf16[256,2048]{1,0:T(8,128)(2,1)S(1)}, bf16[256,2048]{1,0:T(8,128)(2,1)S(1)}, u32[]{:S(2)}, u32[]{:S(2)}) collective-permute-start(bf16[256,2048]{1,0:T(8,128)(2,1)S(1)} %get-tuple-element.86.refs_0_), channel_id=1, source_target_pairs={{0,8},{8,16},{16,24},{24,0},{1,9},{9,17},{17,25},{25,1},{2,10},{10... | collective-permute-start | bytes 3145736 | tf_op jit(solution)/shard_map/ppermute | solution.py:382
  609.0 46.7 %collective-permute-start.45 = (bf16[256,2048]{1,0:T(8,128)(2,1)S(1)}, bf16[256,2048]{1,0:T(8,128)(2,1)S(1)}, u32[]{:S(2)}, u32[]{:S(2)}) collective-permute-start(bf16[256,2048]{1,0:T(8,128)(2,1)S(1)} %get-tuple-element.86.refs_0_), channel_id=1, source_target_pairs={{0,24},{8,0},{16,8},{24,16},{1,25},{9,1},{17,9},{25,17},{2,26},{10... | collective-permute-start | bytes 3145736 | tf_op jit(solution)/shard_map/ppermute | solution.py:385
  611.1 39.1 %collective-permute-start.39 = (f32[128,2048]{1,0:T(8,128)}, f32[128,2048]{1,0:T(8,128)S(1)}, u32[]{:S(2)}, u32[]{:S(2)}) collective-permute-start(f32[128,2048]{1,0:T(8,128)} %get-tuple-element.101), channel_id=1, source_target_pairs={{0,8},{8,16},{16,24},{24,0},{1,9},{9,17},{17,25},{25,1},{2,10},{10... | collective-permute-start | bytes 3145736 | tf_op jit(solution)/shard_map/ppermute | solution.py:382
  611.1 45.9 %collective-permute-start.41 = (f32[128,2048]{1,0:T(8,128)}, f32[128,2048]{1,0:T(8,128)S(1)}, u32[]{:S(2)}, u32[]{:S(2)}) collective-permute-start(f32[128,2048]{1,0:T(8,128)} %get-tuple-element.102), channel_id=1, source_target_pairs={{0,24},{8,0},{16,8},{24,16},{1,25},{9,1},{17,9},{25,17},{2,26},{10... | collective-permute-start | bytes 3145736 | tf_op jit(solution)/shard_map/ppermute | solution.py:385
  653.5 99.0 %collective-permute-start.40 = (f32[256,2048]{1,0:T(8,128)}, f32[256,2048]{1,0:T(8,128)S(1)}, u32[]{:S(2)}, u32[]{:S(2)}) collective-permute-start(f32[256,2048]{1,0:T(8,128)} %pad_maximum_fusion.5), channel_id=1, source_target_pairs={{0,8},{8,16},{16,24},{24,0},{1,9},{9,17},{17,25},{25,1},{2,10},{10... | collective-permute-start | bytes 6291464 | tf_op jit(solution)/shard_map/ppermute | solution.py:382
  653.5 48.8 %collective-permute-start.44 = (bf16[128,2048]{1,0:T(8,128)(2,1)S(1)}, bf16[128,2048]{1,0:T(8,128)(2,1)S(1)}, u32[]{:S(2)}, u32[]{:S(2)}) collective-permute-start(bf16[128,2048]{1,0:T(8,128)(2,1)S(1)} %slice.282), channel_id=1, source_target_pairs={{0,8},{8,16},{16,24},{24,0},{1,9},{9,17},{17,25},{25,1},{2,10},{10... | collective-permute-start | bytes 1572872 | tf_op jit(solution)/shard_map/ppermute | solution.py:382
  655.7 46.6 %collective-permute-start.46 = (bf16[128,2048]{1,0:T(8,128)(2,1)S(1)}, bf16[128,2048]{1,0:T(8,128)(2,1)S(1)}, u32[]{:S(2)}, u32[]{:S(2)}) collective-permute-start(bf16[128,2048]{1,0:T(8,128)(2,1)S(1)} %slice.283), channel_id=1, source_target_pairs={{0,24},{8,0},{16,8},{24,16},{1,25},{9,1},{17,9},{25,17},{2,26},{10... | collective-permute-start | bytes 1572872 | tf_op jit(solution)/shard_map/ppermute | solution.py:385
  658.9 93.6 %collective-permute-start.42 = (f32[256,2048]{1,0:T(8,128)}, f32[256,2048]{1,0:T(8,128)}, u32[]{:S(2)}, u32[]{:S(2)}) collective-permute-start(f32[256,2048]{1,0:T(8,128)} %pad_maximum_fusion.6), channel_id=1, source_target_pairs={{0,24},{8,0},{16,8},{24,16},{1,25},{9,1},{17,9},{25,17},{2,26},{10... | collective-permute-start | bytes 6291464 | tf_op jit(solution)/shard_map/ppermute | solution.py:385
  717.6 29.0 %collective-permute-start.47 = (f32[128,2048]{1,0:T(8,128)}, f32[128,2048]{1,0:T(8,128)S(1)}, u32[]{:S(2)}, u32[]{:S(2)}) collective-permute-start(f32[128,2048]{1,0:T(8,128)} %get-tuple-element.107), channel_id=1, source_target_pairs={{0,8},{8,16},{16,24},{24,0},{1,9},{9,17},{17,25},{25,1},{2,10},{10... | collective-permute-start | bytes 3145736 | tf_op jit(solution)/shard_map/ppermute | solution.py:382
  717.6 31.1 %collective-permute-start.49 = (f32[128,2048]{1,0:T(8,128)S(1)}, f32[128,2048]{1,0:T(8,128)S(1)}, u32[]{:S(2)}, u32[]{:S(2)}) collective-permute-start(f32[128,2048]{1,0:T(8,128)S(1)} %get-tuple-element.108), channel_id=1, source_target_pairs={{0,24},{8,0},{16,8},{24,16},{1,25},{9,1},{17,9},{25,17},{2,26},{10... | collective-permute-start | bytes 3145736 | tf_op jit(solution)/shard_map/ppermute | solution.py:385
  748.6 36.1 %collective-permute-start.48 = (f32[256,2048]{1,0:T(8,128)S(1)}, f32[256,2048]{1,0:T(8,128)S(1)}, u32[]{:S(2)}, u32[]{:S(2)}) collective-permute-start(f32[256,2048]{1,0:T(8,128)S(1)} %pad_maximum_fusion.7), channel_id=1, source_target_pairs={{0,8},{8,16},{16,24},{24,0},{1,9},{9,17},{17,25},{25,1},{2,10},{10... | collective-permute-start | bytes 6291464 | tf_op jit(solution)/shard_map/ppermute | solution.py:382
  750.4 34.9 %collective-permute-start.50 = (f32[256,2048]{1,0:T(8,128)S(1)}, f32[256,2048]{1,0:T(8,128)S(1)}, u32[]{:S(2)}, u32[]{:S(2)}) collective-permute-start(f32[256,2048]{1,0:T(8,128)S(1)} %pad_maximum_fusion.8), channel_id=1, source_target_pairs={{0,24},{8,0},{16,8},{24,16},{1,25},{9,1},{17,9},{25,17},{2,26},{10... | collective-permute-start | bytes 6291464 | tf_op jit(solution)/shard_map/ppermute | solution.py:385
  (52 other events, 311.9 us)
Sparse Core Ops, SparseCore 0:
  10.0 70.5 all-gather.17
  82.2 47.0 all-gather.19
  131.0 51.7 all-gather.21
  184.7 81.0 all-gather.23
  267.7 61.9 all-gather.15
  331.2 46.0 all-gather.25
  379.0 47.2 all-gather.27
  427.9 51.7 all-gather.29

commit v2 on v1

--- a/solution.py
+++ b/solution.py
@@ -390,7 +390,7 @@
         return [value, from_left, from_right,
                 to_right(from_left[:half]), to_left(from_right[half:])]
 
-    def device_fn(x_in, seg_ids, g_attn, w_q, w_k, w_v, w_o, g_mlp, w_gate, w_up, w_down):
+    def body(x_in, seg_ids, g_attn, w_q, w_k, w_v, w_o, g_mlp, w_gate, w_up, w_down):
         micro_n, rows, _ = x_in.shape
         layers = w_q.shape[0]
         head_dim = w_q.shape[3]
@@ -398,22 +398,6 @@
 
         seg_parts = [seg_ids, to_right(seg_ids), to_left(seg_ids)]
         seg_parts.append(to_right(seg_parts[1]))
-        weights = []
-        for l in range(layers):
-            w_qkv = jnp.concatenate([w[l].reshape(e_part, -1) for w in (w_q, w_k, w_v)], axis=1)
-            w_o_l = w_o[l].reshape(-1, w_o.shape[3])
-            if l == 0:
-                w_qkv_all, w_o_all = gather_call([w_qkv, w_o_l], mp_n, tok_n)
-            else:
-                w_qkv_all = lax.all_gather(w_qkv, ('mp', 'tok'), axis=0)
-                w_o_all = lax.all_gather(w_o_l, ('mp', 'tok'), axis=0).reshape((mp_n, tok_n) + w_o_l.shape)
-            weights.append((
-                w_qkv_all.reshape(mp_n, tok_n * e_part, -1), w_o_all,
-                lax.all_gather(w_gate[l], 'tok', axis=0, tiled=True),
-                lax.all_gather(w_up[l], 'tok', axis=0, tiled=True),
-                lax.all_gather(w_down[l], 'tok', axis=1, tiled=True),
-            ))
-
         me = lax.axis_index('mp')
         seg_ring = jnp.concatenate(seg_parts, axis=1)
         ring_at = [lax.rem(me + c + mp_n, mp_n) * rows for c in (0, -1, 1, 2)]
@@ -428,6 +412,28 @@
             streams.append(dict(name='ab'[b], cos=cos_w, sin=sin_w, bound=jnp.where(ok, jnp.inf, -jnp.inf),
                                 resid=x_in[b].astype(jnp.float32)))
 
+        def gathered(value, axis_name, **how):
+            return lax.all_gather(value, axis_name, **how)
+
+        weights = []
+        for l in range(layers):
+            w_qkv = jnp.concatenate([w[l].reshape(e_part, -1) for w in (w_q, w_k, w_v)], axis=1)
+            w_o_l = w_o[l].reshape(-1, w_o.shape[3])
+            if l == 0:
+                w_qkv, w_o_l, *_ = lax.optimization_barrier(
+                    (w_qkv, w_o_l, *[st[k] for st in streams for k in ('cos', 'sin')]))
+                w_qkv_all, w_o_all = gather_call([w_qkv, w_o_l], mp_n, tok_n)
+                w_qkv_all = w_qkv_all.reshape(mp_n, tok_n * e_part, -1)
+            else:
+                w_qkv_all = gathered(gathered(w_qkv, 'mp', axis=0), 'tok', axis=1, tiled=True)
+                w_o_all = gathered(gathered(w_o_l, 'mp', axis=0), 'tok', axis=1)
+            weights.append((
+                w_qkv_all, w_o_all,
+                gathered(w_gate[l], 'tok', axis=0, tiled=True),
+                gathered(w_up[l], 'tok', axis=0, tiled=True),
+                gathered(w_down[l], 'tok', axis=1, tiled=True),
+            ))
+
         half = rows // 2
         last = [None]
 
@@ -481,7 +487,7 @@
                 opp_step(a, l)
                 near_step(a, l)
             else:
-                attn_step(a, l, b['relay'])
+                attn_step(a, l)
                 share_step(a)
                 qkv_step(b, l)
                 opp_step(a, l)
@@ -494,7 +500,7 @@
 
 
     return jax.shard_map(
-        device_fn,
+        body,
         mesh=mesh,
         in_specs=(act_spec, seg_spec, gain_spec, head_in, head_in, head_in, head_out, gain_spec, ffn_in, ffn_in, ffn_out),
         out_specs=act_spec,

time: 805 us -> 835 us (1.037)
  waiting for transfers between devices: 220 us -> 252 us
    all_gather x8 -> x10, waiting for transfers between devices: 0.08 us -> 42.5 us  [gathered(): return lax.all_gather(value, axis_name, **how)]
    ppermute x26, waiting for transfers between devices: 216 us -> 207 us  [to_right(): return lax.ppermute(value, 'mp', fwd)]
    unnamed x117 -> x113, local copies, waits for them, and re-layouts: 21.2 us -> 21.1 us
  transfers between devices with their start and end apart: 59 -> 61, of which waited for: 16 -> 16; matrix products, arithmetic and copies ran while one was open for 7% -> 7% of each run, Pallas kernels for 46% -> 44%
where the time goes in v2:
time: 835 us; the launch traced here: 825 us
  Pallas kernels  391 us (47%)
  waiting for transfers between devices  252 us (30%)
  starting transfers between devices  80.9 us (10%)
  local copies, waits for them, and re-layouts  49.3 us (6%)
  other arithmetic  36.9 us (4%)
  between operations  15 us (2%)
    ppermute x26, waiting for transfers between devices, to_right(): return lax.ppermute(value, 'mp', fwd)  207 us
    pallas_call x8, Pallas kernels, mlp_call(): pl.pallas_call(functools.partial(mlp_kernel, len(pieces), n_out, n_act),...  161 us
    pallas_call x4, Pallas kernels, attn_call(): pl.pallas_call(functools.partial(attn_kernel, LOG2_E * head_dim ** (-0.5)...  105 us
    pallas_call x1, Pallas kernels, gather_call(): pl.pallas_call(functools.partial(gather_kernel, mp_n, tok_n // 2, n), nam...  93 us
    ppermute x25, starting transfers between devices, to_left(): return lax.ppermute(value, 'mp', bwd)  70.7 us
    all_gather x10, waiting for transfers between devices, gathered(): return lax.all_gather(value, axis_name, **how)  42.5 us
    pallas_call x4, Pallas kernels, qkv_call(): pl.pallas_call(functools.partial(qkv_kernel, q_w, kv_w), name='qkv', grid...  32.4 us
    unnamed x113, local copies, waits for them, and re-layouts  21.1 us
  transfers between devices with their start and end apart: 61, of which 16 were waited for; matrix products, arithmetic and copies ran while one was open for 7% of the time, Pallas kernels for 44%

profile of v2, /device:TPU:98, one launch (start us, length us, event | category | flops | bytes accessed | tf_op | source)
XLA Modules:
  0.0 825.0 jit_solution(13489279448642048764)
XLA Ops:
  16.4 3.3 fusion.11
  21.5 19.4 %all-gather.29.cloned.1.call-done = bf16[1024,768]{1,0:T(8,128)(2,1)} async-done(((bf16[256,768]{1,0:T(8,128)(2,1)}), bf16[1024,768]{1,0:T(8,128)(2,1)}) %all-gather.29.cloned.1.call-update) | async-done | bytes 1572880 | tf_op jit(solution)/shard_map/all_gather | solution.py:416
  41.0 23.0 %all-gather.21.cloned.1.call-done = bf16[4,512,256]{2,1,0:T(8,128)(2,1)} async-done(((bf16[1,512,256]{2,1,0:T(8,128)(2,1)}), bf16[4,512,256]{2,1,0:T(8,128)(2,1)}) %all-gather.21.cloned.1.call-update) | async-done | bytes 1048592 | tf_op jit(solution)/shard_map/all_gather | solution.py:416
  65.4 2.9 collective-permute-start.1
  69.8 3.4 bitcast_convert_fusion
  73.3 4.7 collective-permute-done.2
  80.2 93.0 %gather_weights.1 = (bf16[4,8,256,768]{3,2,1,0:T(8,128)(2,1)}, bf16[4,8,512,256]{3,2,1,0:T(8,128)(2,1)}) custom-call(bf16[256,768]{1,0:T(8,128)(2,1)} %pad_maximum_fusion.9.refs_0_, bf16[512,256]{1,0:T(8,128)(2,1)} %bitcast.65), custom_call_target="tpu_custom_call" | custom-call | flops 99999997952 | bytes 20971520 | tf_op jit(solution)/shard_map/gather_weights/pallas_call | solution.py:356
  174.8 7.9 qkv.4
  182.7 2.7 collective-permute-start.3
  186.8 8.3 %qkv.5 = (bf16[4,256,512]{2,1,0:T(8,128)(2,1)S(1)}, bf16[4,256,256]{2,1,0:T(8,128)(2,1)S(1)}) custom-call(f32[256,2048]{1,0:T(8,128)S(1)} %get-tuple-element.58.resid_ref, bf16[1,2048]{1,0:T(2,128)(2,1)S(1)} %get-tuple-element.145.gain_ref, f32[256,128]{1,0:T(8,128)S(1)} %pad_maximum_fusion.13.cos_ref, f32[256,128]{1,0:T(8,128)S(1)} %pad_maximum_fusion.14.sin_ref, ...), custom_call_target="tpu_custom_call" | custom-call | flops 3221225472 | bytes 12582912 | tf_op jit(solution)/shard_map/qkv/pallas_call | solution.py:63
  196.7 2.7 collective-permute-start.10
  200.3 2.5 collective-permute-start.6
  204.3 7.8 collective-permute-done.9.left_ref
  214.3 3.4 collective-permute-start.12
  217.8 27.0 %attn.4 = (f32[256,2048]{1,0:T(8,128)S(1)}, bf16[256,2048]{1,0:T(8,128)(2,1)}) custom-call(bf16[4,256,512]{2,1,0:T(8,128)(2,1)S(1)} %get-tuple-element.60.q_ref, bf16[4,256,256]{2,1,0:T(8,128)(2,1)S(1)} %get-tuple-element.57.own_ref, bf16[4,256,256]{2,1,0:T(8,128)(2,1)S(1)} %collective-permute-done.3.left_ref, ...), custom_call_target="tpu_custom_call" | custom-call | flops 10737418240 | bytes 8388608 | tf_op jit(solution)/shard_map/attn/pallas_call | solution.py:164
  246.1 3.2 collective-permute-start.13
  254.0 25.3 %attn.5 = (f32[256,2048]{1,0:T(8,128)S(1)}, bf16[256,2048]{1,0:T(8,128)(2,1)S(1)}) custom-call(bf16[4,256,512]{2,1,0:T(8,128)(2,1)S(1)} %copy-done.33, bf16[4,256,256]{2,1,0:T(8,128)(2,1)S(1)} %copy-done.39, bf16[4,256,256]{2,1,0:T(8,128)(2,1)S(1)} %collective-permute-done.9.left_ref, bf16[4,256,256]{2,1,0:T(8,128)(2,1)S(1)} %copy-done.23, ...), custom_call_target="tpu_custom_call" | custom-call | flops 10737418240 | bytes 8388608 | tf_op jit(solution)/shard_map/attn/pallas_call | solution.py:164
  279.5 3.2 collective-permute-start.21
  286.0 3.3 collective-permute-start.14
  289.2 25.8 %collective-permute-done.8.refs_0_ = bf16[128,2048]{1,0:T(8,128)(2,1)S(1)} collective-permute-done((bf16[128,2048]{1,0:T(8,128)(2,1)S(1)}, bf16[128,2048]{1,0:T(8,128)(2,1)S(1)}, u32[]{:S(2)}, u32[]{:S(2)}) %collective-permute-start.8) | collective-permute-done | bytes 524320 | tf_op jit(solution)/shard_map/ppermute | solution.py:382
  316.3 3.1 collective-permute-start.22
  319.4 14.4 %mlp.8 = f32[256,2048]{1,0:T(8,128)S(1)} custom-call(bf16[128,2048]{1,0:T(8,128)(2,1)S(1)} %collective-permute-done.8.refs_0_, bf16[128,2048]{1,0:T(8,128)(2,1)S(1)} %collective-permute-done.14.refs_1_, bf16[2048,2048]{1,0:T(8,128)(2,1)} %bitcast.41, bf16[2048,2048]{1,0:T(8,128)(2,1)} %bitcast.45, bf16[2048,2048]{1,0:T(8,128)(2,1)} %bitcast.49), custom_call_target="tpu_custom_call" | custom-call | flops 6442450944 | bytes 25165824 | tf_op jit(solution)/shard_map/mlp/pallas_call | solution.py:235
  335.1 3.6 collective-permute-start.17
  338.8 27.4 %mlp.9 = (f32[256,2048]{1,0:T(8,128)S(1)}, f32[256,2048]{1,0:T(8,128)}, f32[256,2048]{1,0:T(8,128)}) custom-call(bf16[256,2048]{1,0:T(8,128)(2,1)} %get-tuple-element.63.refs_0_, bf16[256,2048]{1,0:T(8,128)(2,1)} %collective-permute-done.7.refs_1_, bf16[256,2048]{1,0:T(8,128)(2,1)} %collective-permute-done.13.refs_2_, bf16[2048,2048]{1,0:T(8,128)(2,1)} %bitcast.42, ...), custom_call_target="tpu_custom_call" | custom-call | flops 19327352832 | bytes 25165824 | tf_op jit(solution)/shard_map/mlp/pallas_call | solution.py:235
  366.2 14.3 %mlp.10 = f32[256,2048]{1,0:T(8,128)S(1)} custom-call(bf16[128,2048]{1,0:T(8,128)(2,1)S(1)} %collective-permute-done.20.refs_0_, bf16[128,2048]{1,0:T(8,128)(2,1)S(1)} %collective-permute-done.22.refs_1_, bf16[2048,2048]{1,0:T(8,128)(2,1)} %bitcast.43, bf16[2048,2048]{1,0:T(8,128)(2,1)} %bitcast.47, bf16[2048,2048]{1,0:T(8,128)(2,1)} %bitcast.51), custom_call_target="tpu_custom_call" | custom-call | flops 6442450944 | bytes 25165824 | tf_op jit(solution)/shard_map/mlp/pallas_call | solution.py:235
  382.0 3.2 collective-permute-start.30
  390.3 1.9 collective-permute-start.18
  392.2 25.9 %mlp.11 = (f32[256,2048]{1,0:T(8,128)S(1)}, f32[256,2048]{1,0:T(8,128)}, f32[256,2048]{1,0:T(8,128)}) custom-call(bf16[256,2048]{1,0:T(8,128)(2,1)S(1)} %copy-done.29, bf16[256,2048]{1,0:T(8,128)(2,1)S(1)} %copy-done.15, bf16[256,2048]{1,0:T(8,128)(2,1)S(1)} %copy-done.17, bf16[2048,2048]{1,0:T(8,128)(2,1)} %bitcast.44, bf16[2048,2048]{1,0:T(8,128)(2,1)} %bitcast.48, ...), custom_call_target="tpu_custom_call" | custom-call | flops 19327352832 | bytes 25165824 | tf_op jit(solution)/shard_map/mlp/pallas_call | solution.py:235
  418.1 2.9 slice_add_fusion.5
  425.1 2.6 collective-permute-start.31
  427.8 26.6 %collective-permute-done.16 = f32[256,2048]{1,0:T(8,128)S(1)} collective-permute-done((f32[256,2048]{1,0:T(8,128)S(1)}, f32[256,2048]{1,0:T(8,128)S(1)}, u32[]{:S(2)}, u32[]{:S(2)}) %collective-permute-start.16) | collective-permute-done | bytes 2097184 | tf_op jit(solution)/shard_map/ppermute | solution.py:382
  454.4 2.4 add_add_fusion.1.resid_ref
  456.9 8.3 %qkv.6 = (bf16[4,256,512]{2,1,0:T(8,128)(2,1)S(1)}, bf16[4,256,256]{2,1,0:T(8,128)(2,1)S(1)}) custom-call(f32[256,2048]{1,0:T(8,128)S(1)} %add_add_fusion.1.resid_ref, bf16[1,2048]{1,0:T(2,128)(2,1)S(1)} %get-tuple-element.144.gain_ref, f32[256,128]{1,0:T(8,128)S(1)} %pad_maximum_fusion.11.cos_ref, f32[256,128]{1,0:T(8,128)S(1)} %pad_maximum_fusion.12.sin_ref, ...), custom_call_target="tpu_custom_call" | custom-call | flops 3221225472 | bytes 12582912 | tf_op jit(solution)/shard_map/qkv/pallas_call | solution.py:63
  466.1 3.4 collective-permute-start.24
  469.5 36.6 %collective-permute-done.23.left_ref = bf16[4,256,256]{2,1,0:T(8,128)(2,1)S(1)} collective-permute-done((bf16[4,256,256]{2,1,0:T(8,128)(2,1)S(1)}, bf16[4,256,256]{2,1,0:T(8,128)(2,1)S(1)}, u32[]{:S(2)}, u32[]{:S(2)}) %collective-permute-start.23) | collective-permute-done | bytes 524320 | tf_op jit(solution)/shard_map/ppermute | solution.py:382
  507.6 3.2 collective-permute-start.26
  510.8 3.9 collective-permute-done.25.opp_lo_ref
  518.5 26.3 %attn.6 = (f32[256,2048]{1,0:T(8,128)S(1)}, bf16[256,2048]{1,0:T(8,128)(2,1)S(1)}) custom-call(bf16[4,256,512]{2,1,0:T(8,128)(2,1)S(1)} %copy-done.37, bf16[4,256,256]{2,1,0:T(8,128)(2,1)S(1)} %copy-done.43, bf16[4,256,256]{2,1,0:T(8,128)(2,1)S(1)} %collective-permute-done.23.left_ref, bf16[4,256,256]{2,1,0:T(8,128)(2,1)S(1)} %collective-permute-done.24.right_ref, ...), custom_call_target="tpu_custom_call" | custom-call | flops 10737418240 | bytes 8388608 | tf_op jit(solution)/shard_map/attn/pallas_call | solution.py:164
  545.0 3.8 collective-permute-start.33
  548.8 3.0 add_add_fusion.resid_ref
  551.8 7.9 qkv.7
  560.7 3.2 collective-permute-start.36
  564.8 7.9 collective-permute-done.27.refs_1_
  573.9 3.1 collective-permute-start.34
  577.0 6.9 collective-permute-done.35.left_ref
  585.4 3.4 collective-permute-start.38
  588.9 2.6 collective-permute-done.32.refs_0_
  591.5 14.0 %mlp.12 = f32[256,2048]{1,0:T(8,128)S(1)} custom-call(bf16[128,2048]{1,0:T(8,128)(2,1)S(1)} %collective-permute-done.32.refs_0_, bf16[128,2048]{1,0:T(8,128)(2,1)S(1)} %collective-permute-done.34.refs_1_, bf16[2048,2048]{1,0:T(8,128)(2,1)} %bitcast.33, bf16[2048,2048]{1,0:T(8,128)(2,1)} %bitcast.37, bf16[2048,2048]{1,0:T(8,128)(2,1)} %bitcast.53), custom_call_target="tpu_custom_call" | custom-call | flops 6442450944 | bytes 25165824 | tf_op jit(solution)/shard_map/mlp/pallas_call | solution.py:235
  608.2 26.1 %attn.7 = (f32[256,2048]{1,0:T(8,128)S(1)}, bf16[256,2048]{1,0:T(8,128)(2,1)S(1)}) custom-call(bf16[4,256,512]{2,1,0:T(8,128)(2,1)S(1)} %copy-done.35, bf16[4,256,256]{2,1,0:T(8,128)(2,1)S(1)} %copy-done.41, bf16[4,256,256]{2,1,0:T(8,128)(2,1)S(1)} %copy-done.25, bf16[4,256,256]{2,1,0:T(8,128)(2,1)S(1)} %copy-done.27, ...), custom_call_target="tpu_custom_call" | custom-call | flops 10737418240 | bytes 8388608 | tf_op jit(solution)/shard_map/attn/pallas_call | solution.py:164
  635.5 2.1 collective-permute-start.45
  637.7 3.2 collective-permute-start.41
  640.9 25.5 %mlp.13 = (f32[256,2048]{1,0:T(8,128)S(1)}, f32[256,2048]{1,0:T(8,128)}, f32[256,2048]{1,0:T(8,128)}) custom-call(bf16[256,2048]{1,0:T(8,128)(2,1)S(1)} %copy-done.31, bf16[256,2048]{1,0:T(8,128)(2,1)S(1)} %copy-done.19, bf16[256,2048]{1,0:T(8,128)(2,1)S(1)} %copy-done.21, bf16[2048,2048]{1,0:T(8,128)(2,1)} %bitcast.34, bf16[2048,2048]{1,0:T(8,128)(2,1)} %bitcast.38, ...), custom_call_target="tpu_custom_call" | custom-call | flops 19327352832 | bytes 25165824 | tf_op jit(solution)/shard_map/mlp/pallas_call | solution.py:235
  666.4 10.4 %collective-permute-done.39 = f32[128,2048]{1,0:T(8,128)S(1)} collective-permute-done((f32[128,2048]{1,0:T(8,128)}, f32[128,2048]{1,0:T(8,128)S(1)}, u32[]{:S(2)}, u32[]{:S(2)}) %collective-permute-start.39) | collective-permute-done | bytes 1048608 | tf_op jit(solution)/shard_map/ppermute | solution.py:382
  676.8 1.7 slice_add_fusion.3
  680.5 2.5 collective-permute-start.44
  687.4 42.8 %collective-permute-done.44.refs_0_ = bf16[128,2048]{1,0:T(8,128)(2,1)S(1)} collective-permute-done((bf16[128,2048]{1,0:T(8,128)(2,1)S(1)}, bf16[128,2048]{1,0:T(8,128)(2,1)S(1)}, u32[]{:S(2)}, u32[]{:S(2)}) %collective-permute-start.44) | collective-permute-done | bytes 524320 | tf_op jit(solution)/shard_map/ppermute | solution.py:382
  730.2 14.0 %mlp.14 = f32[256,2048]{1,0:T(8,128)S(1)} custom-call(bf16[128,2048]{1,0:T(8,128)(2,1)S(1)} %collective-permute-done.44.refs_0_, bf16[128,2048]{1,0:T(8,128)(2,1)S(1)} %collective-permute-done.46.refs_1_, bf16[2048,2048]{1,0:T(8,128)(2,1)} %bitcast.35, bf16[2048,2048]{1,0:T(8,128)(2,1)} %bitcast.39, bf16[2048,2048]{1,0:T(8,128)(2,1)} %bitcast.55), custom_call_target="tpu_custom_call" | custom-call | flops 6442450944 | bytes 25165824 | tf_op jit(solution)/shard_map/mlp/pallas_call | solution.py:235
  745.4 3.5 collective-permute-start.49
  748.9 25.5 %mlp.15 = (f32[256,2048]{1,0:T(8,128)S(1)}, f32[256,2048]{1,0:T(8,128)}, f32[256,2048]{1,0:T(8,128)}) custom-call(bf16[256,2048]{1,0:T(8,128)(2,1)S(1)} %get-tuple-element.89.refs_0_, bf16[256,2048]{1,0:T(8,128)(2,1)S(1)} %collective-permute-done.43.refs_1_, bf16[256,2048]{1,0:T(8,128)(2,1)S(1)} %collective-permute-done.45.refs_2_, ...), custom_call_target="tpu_custom_call" | custom-call | flops 19327352832 | bytes 25165824 | tf_op jit(solution)/shard_map/mlp/pallas_call | solution.py:235
  774.4 1.7 slice_add_fusion.1
  778.2 2.1 collective-permute-start.50
  780.2 2.4 add_bitcast_fusion.1
  782.7 31.1 %collective-permute-done.48 = f32[256,2048]{1,0:T(8,128)S(1)} collective-permute-done((f32[256,2048]{1,0:T(8,128)S(1)}, f32[256,2048]{1,0:T(8,128)S(1)}, u32[]{:S(2)}, u32[]{:S(2)}) %collective-permute-start.48) | collective-permute-done | bytes 2097184 | tf_op jit(solution)/shard_map/ppermute | solution.py:382
  815.2 2.5 pad_maximum_fusion
  (274 shorter events, 74.0 us)
Async XLA Ops:
  6.5 34.4 %all-gather.29.cloned.1.call-start = ((), (), s32[]{:S(2)}) async-start(), calls=%async_computation.5 | async-start | bytes 1966080 | tf_op jit(solution)/shard_map/all_gather | solution.py:416
  13.8 50.3 %all-gather.21.cloned.1.call-start = ((), (), s32[]{:S(2)}) async-start(), calls=%async_computation.1 | async-start | bytes 1310720 | tf_op jit(solution)/shard_map/all_gather | solution.py:416
  14.8 304.6 %all-gather.23.cloned.1.call-start = ((), (), s32[]{:S(2)}) async-start(), calls=%async_computation.2 | async-start | bytes 9437184 | tf_op jit(solution)/shard_map/all_gather | solution.py:416
  16.4 303.0 %all-gather.25.cloned.1.call-start = ((), (), s32[]{:S(2)}) async-start(), calls=%async_computation.3 | async-start | bytes 9437184 | tf_op jit(solution)/shard_map/all_gather | solution.py:416
  19.8 299.6 %all-gather.27.cloned.1.call-start = ((), (), s32[]{:S(2)}) async-start(), calls=%async_computation.4 | async-start | bytes 9437184 | tf_op jit(solution)/shard_map/all_gather | solution.py:416
  21.5 43.5 %copy-start.54 = (s32[2,256]{1,0:T(2,128)S(1)}, s32[2,256]{1,0:T(2,128)}, u32[]{:S(2)}) copy-start(s32[2,256]{1,0:T(2,128)} %param.12) | copy-start | bytes 6148
  21.5 435.4 %all-gather.19.cloned.1.call-start = ((), (), s32[]{:S(2)}) async-start(), calls=%async_computation | async-start | bytes 14155776 | tf_op jit(solution)/shard_map/all_gather | solution.py:416
  41.0 469.8 %all-gather.31.cloned.1.call-start = ((), (), s32[]{:S(2)}) async-start(), calls=%async_computation.6 | async-start | bytes 9437184 | tf_op jit(solution)/shard_map/all_gather | solution.py:416
  64.1 527.3 %all-gather.33.cloned.1.call-start = ((), (), s32[]{:S(2)}) async-start(), calls=%async_computation.7 | async-start | bytes 9437184 | tf_op jit(solution)/shard_map/all_gather | solution.py:416
  64.9 526.5 %all-gather.35.cloned.1.call-start = ((), (), s32[]{:S(2)}) async-start(), calls=%async_computation.8 | async-start | bytes 9437184 | tf_op jit(solution)/shard_map/all_gather | solution.py:416
  65.0 8.2 collective-permute-start
  65.4 7.9 collective-permute-start.1
  68.4 523.1 %all-gather.37.cloned.1.call-start = ((), (), s32[]{:S(2)}) async-start(), calls=%async_computation.9 | async-start | bytes 9437184 | tf_op jit(solution)/shard_map/all_gather | solution.py:416
  73.2 4.9 collective-permute-start.2
  182.7 16.6 %collective-permute-start.3 = (bf16[4,256,256]{2,1,0:T(8,128)(2,1)S(1)}, bf16[4,256,256]{2,1,0:T(8,128)(2,1)S(1)}, u32[]{:S(2)}, u32[]{:S(2)}) collective-permute-start(bf16[4,256,256]{2,1,0:T(8,128)(2,1)S(1)} %get-tuple-element.57.own_ref), channel_id=1, source_target_pairs={{0,8},{8,16},{16,24},{24,0},{1,9},{9,17},{17,25},{25,1},{2,10},{10... | collective-permute-start | bytes 1572872 | tf_op jit(solution)/shard_map/ppermute | solution.py:382
  185.4 14.9 %collective-permute-start.4 = (bf16[4,256,256]{2,1,0:T(8,128)(2,1)S(1)}, bf16[4,256,256]{2,1,0:T(8,128)(2,1)S(1)}, u32[]{:S(2)}, u32[]{:S(2)}) collective-permute-start(bf16[4,256,256]{2,1,0:T(8,128)(2,1)S(1)} %get-tuple-element.57.own_ref), channel_id=1, source_target_pairs={{0,24},{8,0},{16,8},{24,16},{1,25},{9,1},{17,9},{25,17},{2,26},{10... | collective-permute-start | bytes 1572872 | tf_op jit(solution)/shard_map/ppermute | solution.py:385
  196.1 16.0 %collective-permute-start.9 = (bf16[4,256,256]{2,1,0:T(8,128)(2,1)S(1)}, bf16[4,256,256]{2,1,0:T(8,128)(2,1)S(1)}, u32[]{:S(2)}, u32[]{:S(2)}) collective-permute-start(bf16[4,256,256]{2,1,0:T(8,128)(2,1)S(1)} %get-tuple-element.59.own_ref), channel_id=1, source_target_pairs={{0,8},{8,16},{16,24},{24,0},{1,9},{9,17},{17,25},{25,1},{2,10},{10... | collective-permute-start | bytes 1572872 | tf_op jit(solution)/shard_map/ppermute | solution.py:382
  196.7 16.1 %collective-permute-start.10 = (bf16[4,256,256]{2,1,0:T(8,128)(2,1)S(1)}, bf16[4,256,256]{2,1,0:T(8,128)(2,1)S(1)}, u32[]{:S(2)}, u32[]{:S(2)}) collective-permute-start(bf16[4,256,256]{2,1,0:T(8,128)(2,1)S(1)} %get-tuple-element.59.own_ref), channel_id=1, source_target_pairs={{0,24},{8,0},{16,8},{24,16},{1,25},{9,1},{17,9},{25,17},{2,26},{10... | collective-permute-start | bytes 1572872 | tf_op jit(solution)/shard_map/ppermute | solution.py:385
  199.4 18.4 %collective-permute-start.5 = (bf16[2,256,256]{2,1,0:T(8,128)(2,1)S(1)}, bf16[2,256,256]{2,1,0:T(8,128)(2,1)S(1)}, u32[]{:S(2)}, u32[]{:S(2)}) collective-permute-start(bf16[2,256,256]{2,1,0:T(8,128)(2,1)S(1)} %slice.262), channel_id=1, source_target_pairs={{0,8},{8,16},{16,24},{24,0},{1,9},{9,17},{17,25},{25,1},{2,10},{10... | collective-permute-start | bytes 786440 | tf_op jit(solution)/shard_map/ppermute | solution.py:382
  200.3 17.4 %collective-permute-start.6 = (bf16[2,256,256]{2,1,0:T(8,128)(2,1)S(1)}, bf16[2,256,256]{2,1,0:T(8,128)(2,1)S(1)}, u32[]{:S(2)}, u32[]{:S(2)}) collective-permute-start(bf16[2,256,256]{2,1,0:T(8,128)(2,1)S(1)} %slice.263), channel_id=1, source_target_pairs={{0,24},{8,0},{16,8},{24,16},{1,25},{9,1},{17,9},{25,17},{2,26},{10... | collective-permute-start | bytes 786440 | tf_op jit(solution)/shard_map/ppermute | solution.py:385
  204.3 40.5 %copy-start.12 = (f32[256,1024]{1,0:T(8,128)}, f32[256,1024]{1,0:T(8,128)S(1)}, u32[]{:S(2)}) copy-start(f32[256,1024]{1,0:T(8,128)S(1)} %get-tuple-element.149.bound_ref) | copy-start | bytes 3145732
  212.8 36.6 %collective-permute-start.11 = (bf16[2,256,256]{2,1,0:T(8,128)(2,1)}, bf16[2,256,256]{2,1,0:T(8,128)(2,1)S(1)}, u32[]{:S(2)}, u32[]{:S(2)}) collective-permute-start(bf16[2,256,256]{2,1,0:T(8,128)(2,1)} %slice.265), channel_id=1, source_target_pairs={{0,8},{8,16},{16,24},{24,0},{1,9},{9,17},{17,25},{25,1},{2,10},{10... | collective-permute-start | bytes 786440 | tf_op jit(solution)/shard_map/ppermute | solution.py:382
  214.3 35.1 %collective-permute-start.12 = (bf16[2,256,256]{2,1,0:T(8,128)(2,1)}, bf16[2,256,256]{2,1,0:T(8,128)(2,1)}, u32[]{:S(2)}, u32[]{:S(2)}) collective-permute-start(bf16[2,256,256]{2,1,0:T(8,128)(2,1)} %slice.266), channel_id=1, source_target_pairs={{0,24},{8,0},{16,8},{24,16},{1,25},{9,1},{17,9},{25,17},{2,26},{10... | collective-permute-start | bytes 786440 | tf_op jit(solution)/shard_map/ppermute | solution.py:385
  246.1 33.2 %collective-permute-start.7 = (bf16[256,2048]{1,0:T(8,128)(2,1)}, bf16[256,2048]{1,0:T(8,128)(2,1)}, u32[]{:S(2)}, u32[]{:S(2)}) collective-permute-start(bf16[256,2048]{1,0:T(8,128)(2,1)} %get-tuple-element.63.refs_0_), channel_id=1, source_target_pairs={{0,8},{8,16},{16,24},{24,0},{1,9},{9,17},{17,25},{25,1},{2,10},{10... | collective-permute-start | bytes 3145736 | tf_op jit(solution)/shard_map/ppermute | solution.py:382
  246.1 33.2 %collective-permute-start.13 = (bf16[256,2048]{1,0:T(8,128)(2,1)}, bf16[256,2048]{1,0:T(8,128)(2,1)}, u32[]{:S(2)}, u32[]{:S(2)}) collective-permute-start(bf16[256,2048]{1,0:T(8,128)(2,1)} %get-tuple-element.63.refs_0_), channel_id=1, source_target_pairs={{0,24},{8,0},{16,8},{24,16},{1,25},{9,1},{17,9},{25,17},{2,26},{10... | collective-permute-start | bytes 3145736 | tf_op jit(solution)/shard_map/ppermute | solution.py:385
  279.4 35.7 %collective-permute-start.19 = (bf16[256,2048]{1,0:T(8,128)(2,1)S(1)}, bf16[256,2048]{1,0:T(8,128)(2,1)S(1)}, u32[]{:S(2)}, u32[]{:S(2)}) collective-permute-start(bf16[256,2048]{1,0:T(8,128)(2,1)S(1)} %get-tuple-element.72.refs_0_), channel_id=1, source_target_pairs={{0,8},{8,16},{16,24},{24,0},{1,9},{9,17},{17,25},{25,1},{2,10},{10... | collective-permute-start | bytes 3145736 | tf_op jit(solution)/shard_map/ppermute | solution.py:382
  279.5 35.7 %collective-permute-start.21 = (bf16[256,2048]{1,0:T(8,128)(2,1)S(1)}, bf16[256,2048]{1,0:T(8,128)(2,1)S(1)}, u32[]{:S(2)}, u32[]{:S(2)}) collective-permute-start(bf16[256,2048]{1,0:T(8,128)(2,1)S(1)} %get-tuple-element.72.refs_0_), channel_id=1, source_target_pairs={{0,24},{8,0},{16,8},{24,16},{1,25},{9,1},{17,9},{25,17},{2,26},{10... | collective-permute-start | bytes 3145736 | tf_op jit(solution)/shard_map/ppermute | solution.py:385
  284.7 30.3 %collective-permute-start.8 = (bf16[128,2048]{1,0:T(8,128)(2,1)S(1)}, bf16[128,2048]{1,0:T(8,128)(2,1)S(1)}, u32[]{:S(2)}, u32[]{:S(2)}) collective-permute-start(bf16[128,2048]{1,0:T(8,128)(2,1)S(1)} %slice.264), channel_id=1, source_target_pairs={{0,8},{8,16},{16,24},{24,0},{1,9},{9,17},{17,25},{25,1},{2,10},{10... | collective-permute-start | bytes 1572872 | tf_op jit(solution)/shard_map/ppermute | solution.py:382
  286.0 33.4 %collective-permute-start.14 = (bf16[128,2048]{1,0:T(8,128)(2,1)S(1)}, bf16[128,2048]{1,0:T(8,128)(2,1)S(1)}, u32[]{:S(2)}, u32[]{:S(2)}) collective-permute-start(bf16[128,2048]{1,0:T(8,128)(2,1)S(1)} %slice.267), channel_id=1, source_target_pairs={{0,24},{8,0},{16,8},{24,16},{1,25},{9,1},{17,9},{25,17},{2,26},{10... | collective-permute-start | bytes 1572872 | tf_op jit(solution)/shard_map/ppermute | solution.py:385
  315.1 51.1 %collective-permute-start.20 = (bf16[128,2048]{1,0:T(8,128)(2,1)S(1)}, bf16[128,2048]{1,0:T(8,128)(2,1)S(1)}, u32[]{:S(2)}, u32[]{:S(2)}) collective-permute-start(bf16[128,2048]{1,0:T(8,128)(2,1)S(1)} %slice.270), channel_id=1, source_target_pairs={{0,8},{8,16},{16,24},{24,0},{1,9},{9,17},{17,25},{25,1},{2,10},{10... | collective-permute-start | bytes 1572872 | tf_op jit(solution)/shard_map/ppermute | solution.py:382
  316.3 49.9 %collective-permute-start.22 = (bf16[128,2048]{1,0:T(8,128)(2,1)}, bf16[128,2048]{1,0:T(8,128)(2,1)S(1)}, u32[]{:S(2)}, u32[]{:S(2)}) collective-permute-start(bf16[128,2048]{1,0:T(8,128)(2,1)} %slice.271), channel_id=1, source_target_pairs={{0,24},{8,0},{16,8},{24,16},{1,25},{9,1},{17,9},{25,17},{2,26},{10... | collective-permute-start | bytes 1572872 | tf_op jit(solution)/shard_map/ppermute | solution.py:385
  335.1 50.1 %collective-permute-start.15 = (f32[128,2048]{1,0:T(8,128)S(1)}, f32[128,2048]{1,0:T(8,128)S(1)}, u32[]{:S(2)}, u32[]{:S(2)}) collective-permute-start(f32[128,2048]{1,0:T(8,128)S(1)} %get-tuple-element.122), channel_id=1, source_target_pairs={{0,8},{8,16},{16,24},{24,0},{1,9},{9,17},{17,25},{25,1},{2,10},{10... | collective-permute-start | bytes 3145736 | tf_op jit(solution)/shard_map/ppermute | solution.py:382
  335.1 50.7 %collective-permute-start.17 = (f32[128,2048]{1,0:T(8,128)}, f32[128,2048]{1,0:T(8,128)}, u32[]{:S(2)}, u32[]{:S(2)}) collective-permute-start(f32[128,2048]{1,0:T(8,128)} %get-tuple-element.123), channel_id=1, source_target_pairs={{0,24},{8,0},{16,8},{24,16},{1,25},{9,1},{17,9},{25,17},{2,26},{10... | collective-permute-start | bytes 3145736 | tf_op jit(solution)/shard_map/ppermute | solution.py:385
  382.0 36.1 %collective-permute-start.28 = (f32[128,2048]{1,0:T(8,128)}, f32[128,2048]{1,0:T(8,128)}, u32[]{:S(2)}, u32[]{:S(2)}) collective-permute-start(f32[128,2048]{1,0:T(8,128)} %get-tuple-element.128), channel_id=1, source_target_pairs={{0,8},{8,16},{16,24},{24,0},{1,9},{9,17},{17,25},{25,1},{2,10},{10... | collective-permute-start | bytes 3145736 | tf_op jit(solution)/shard_map/ppermute | solution.py:382
  382.0 40.6 %collective-permute-start.30 = (f32[128,2048]{1,0:T(8,128)}, f32[128,2048]{1,0:T(8,128)S(1)}, u32[]{:S(2)}, u32[]{:S(2)}) collective-permute-start(f32[128,2048]{1,0:T(8,128)} %get-tuple-element.129), channel_id=1, source_target_pairs={{0,24},{8,0},{16,8},{24,16},{1,25},{9,1},{17,9},{25,17},{2,26},{10... | collective-permute-start | bytes 3145736 | tf_op jit(solution)/shard_map/ppermute | solution.py:385
  385.8 68.7 %collective-permute-start.16 = (f32[256,2048]{1,0:T(8,128)S(1)}, f32[256,2048]{1,0:T(8,128)S(1)}, u32[]{:S(2)}, u32[]{:S(2)}) collective-permute-start(f32[256,2048]{1,0:T(8,128)S(1)} %pad_maximum_fusion.1), channel_id=1, source_target_pairs={{0,8},{8,16},{16,24},{24,0},{1,9},{9,17},{17,25},{25,1},{2,10},{10... | collective-permute-start | bytes 6291464 | tf_op jit(solution)/shard_map/ppermute | solution.py:382
  390.3 64.2 %collective-permute-start.18 = (f32[256,2048]{1,0:T(8,128)}, f32[256,2048]{1,0:T(8,128)}, u32[]{:S(2)}, u32[]{:S(2)}) collective-permute-start(f32[256,2048]{1,0:T(8,128)} %pad_maximum_fusion.2), channel_id=1, source_target_pairs={{0,24},{8,0},{16,8},{24,16},{1,25},{9,1},{17,9},{25,17},{2,26},{10... | collective-permute-start | bytes 6291464 | tf_op jit(solution)/shard_map/ppermute | solution.py:385
  422.6 126.1 %collective-permute-start.29 = (f32[256,2048]{1,0:T(8,128)}, f32[256,2048]{1,0:T(8,128)}, u32[]{:S(2)}, u32[]{:S(2)}) collective-permute-start(f32[256,2048]{1,0:T(8,128)} %pad_maximum_fusion.3), channel_id=1, source_target_pairs={{0,8},{8,16},{16,24},{24,0},{1,9},{9,17},{17,25},{25,1},{2,10},{10... | collective-permute-start | bytes 6291464 | tf_op jit(solution)/shard_map/ppermute | solution.py:382
  425.1 123.6 %collective-permute-start.31 = (f32[256,2048]{1,0:T(8,128)}, f32[256,2048]{1,0:T(8,128)}, u32[]{:S(2)}, u32[]{:S(2)}) collective-permute-start(f32[256,2048]{1,0:T(8,128)} %pad_maximum_fusion.4), channel_id=1, source_target_pairs={{0,24},{8,0},{16,8},{24,16},{1,25},{9,1},{17,9},{25,17},{2,26},{10... | collective-permute-start | bytes 6291464 | tf_op jit(solution)/shard_map/ppermute | solution.py:385
  466.1 40.7 %copy-start.42 = (bf16[4,256,256]{2,1,0:T(8,128)(2,1)}, bf16[4,256,256]{2,1,0:T(8,128)(2,1)S(1)}, u32[]{:S(2)}) copy-start(bf16[4,256,256]{2,1,0:T(8,128)(2,1)S(1)} %get-tuple-element.78.own_ref) | copy-start | bytes 1572868
  466.1 40.0 %collective-permute-start.23 = (bf16[4,256,256]{2,1,0:T(8,128)(2,1)S(1)}, bf16[4,256,256]{2,1,0:T(8,128)(2,1)S(1)}, u32[]{:S(2)}, u32[]{:S(2)}) collective-permute-start(bf16[4,256,256]{2,1,0:T(8,128)(2,1)S(1)} %get-tuple-element.78.own_ref), channel_id=1, source_target_pairs={{0,8},{8,16},{16,24},{24,0},{1,9},{9,17},{17,25},{25,1},{2,10},{10... | collective-permute-start | bytes 1572872 | tf_op jit(solution)/shard_map/ppermute | solution.py:382
  466.1 40.7 %collective-permute-start.24 = (bf16[4,256,256]{2,1,0:T(8,128)(2,1)S(1)}, bf16[4,256,256]{2,1,0:T(8,128)(2,1)S(1)}, u32[]{:S(2)}, u32[]{:S(2)}) collective-permute-start(bf16[4,256,256]{2,1,0:T(8,128)(2,1)S(1)} %get-tuple-element.78.own_ref), channel_id=1, source_target_pairs={{0,24},{8,0},{16,8},{24,16},{1,25},{9,1},{17,9},{25,17},{2,26},{10... | collective-permute-start | bytes 1572872 | tf_op jit(solution)/shard_map/ppermute | solution.py:385
  506.8 7.9 collective-permute-start.25
  507.6 7.4 collective-permute-start.26
  544.9 27.8 %collective-permute-start.27 = (bf16[256,2048]{1,0:T(8,128)(2,1)S(1)}, bf16[256,2048]{1,0:T(8,128)(2,1)S(1)}, u32[]{:S(2)}, u32[]{:S(2)}) collective-permute-start(bf16[256,2048]{1,0:T(8,128)(2,1)S(1)} %get-tuple-element.80.refs_0_), channel_id=1, source_target_pairs={{0,8},{8,16},{16,24},{24,0},{1,9},{9,17},{17,25},{25,1},{2,10},{10... | collective-permute-start | bytes 3145736 | tf_op jit(solution)/shard_map/ppermute | solution.py:382
  545.0 27.9 %collective-permute-start.33 = (bf16[256,2048]{1,0:T(8,128)(2,1)S(1)}, bf16[256,2048]{1,0:T(8,128)(2,1)S(1)}, u32[]{:S(2)}, u32[]{:S(2)}) collective-permute-start(bf16[256,2048]{1,0:T(8,128)(2,1)S(1)} %get-tuple-element.80.refs_0_), channel_id=1, source_target_pairs={{0,24},{8,0},{16,8},{24,16},{1,25},{9,1},{17,9},{25,17},{2,26},{10... | collective-permute-start | bytes 3145736 | tf_op jit(solution)/shard_map/ppermute | solution.py:385
  560.7 23.2 %collective-permute-start.35 = (bf16[4,256,256]{2,1,0:T(8,128)(2,1)S(1)}, bf16[4,256,256]{2,1,0:T(8,128)(2,1)S(1)}, u32[]{:S(2)}, u32[]{:S(2)}) collective-permute-start(bf16[4,256,256]{2,1,0:T(8,128)(2,1)S(1)} %get-tuple-element.86.own_ref), channel_id=1, source_target_pairs={{0,8},{8,16},{16,24},{24,0},{1,9},{9,17},{17,25},{25,1},{2,10},{10... | collective-permute-start | bytes 1572872 | tf_op jit(solution)/shard_map/ppermute | solution.py:382
  560.7 24.0 %collective-permute-start.36 = (bf16[4,256,256]{2,1,0:T(8,128)(2,1)S(1)}, bf16[4,256,256]{2,1,0:T(8,128)(2,1)S(1)}, u32[]{:S(2)}, u32[]{:S(2)}) collective-permute-start(bf16[4,256,256]{2,1,0:T(8,128)(2,1)S(1)} %get-tuple-element.86.own_ref), channel_id=1, source_target_pairs={{0,24},{8,0},{16,8},{24,16},{1,25},{9,1},{17,9},{25,17},{2,26},{10... | collective-permute-start | bytes 1572872 | tf_op jit(solution)/shard_map/ppermute | solution.py:385
  572.7 18.7 %collective-permute-start.32 = (bf16[128,2048]{1,0:T(8,128)(2,1)S(1)}, bf16[128,2048]{1,0:T(8,128)(2,1)S(1)}, u32[]{:S(2)}, u32[]{:S(2)}) collective-permute-start(bf16[128,2048]{1,0:T(8,128)(2,1)S(1)} %slice.276), channel_id=1, source_target_pairs={{0,8},{8,16},{16,24},{24,0},{1,9},{9,17},{17,25},{25,1},{2,10},{10... | collective-permute-start | bytes 1572872 | tf_op jit(solution)/shard_map/ppermute | solution.py:382
  573.9 17.6 %collective-permute-start.34 = (bf16[128,2048]{1,0:T(8,128)(2,1)}, bf16[128,2048]{1,0:T(8,128)(2,1)S(1)}, u32[]{:S(2)}, u32[]{:S(2)}) collective-permute-start(bf16[128,2048]{1,0:T(8,128)(2,1)} %slice.277), channel_id=1, source_target_pairs={{0,24},{8,0},{16,8},{24,16},{1,25},{9,1},{17,9},{25,17},{2,26},{10... | collective-permute-start | bytes 1572872 | tf_op jit(solution)/shard_map/ppermute | solution.py:385
  584.7 22.5 %collective-permute-start.37 = (bf16[2,256,256]{2,1,0:T(8,128)(2,1)}, bf16[2,256,256]{2,1,0:T(8,128)(2,1)S(1)}, u32[]{:S(2)}, u32[]{:S(2)}) collective-permute-start(bf16[2,256,256]{2,1,0:T(8,128)(2,1)} %slice.278), channel_id=1, source_target_pairs={{0,8},{8,16},{16,24},{24,0},{1,9},{9,17},{17,25},{25,1},{2,10},{10... | collective-permute-start | bytes 786440 | tf_op jit(solution)/shard_map/ppermute | solution.py:382
  585.4 21.7 %collective-permute-start.38 = (bf16[2,256,256]{2,1,0:T(8,128)(2,1)}, bf16[2,256,256]{2,1,0:T(8,128)(2,1)}, u32[]{:S(2)}, u32[]{:S(2)}) collective-permute-start(bf16[2,256,256]{2,1,0:T(8,128)(2,1)} %slice.279), channel_id=1, source_target_pairs={{0,24},{8,0},{16,8},{24,16},{1,25},{9,1},{17,9},{25,17},{2,26},{10... | collective-permute-start | bytes 786440 | tf_op jit(solution)/shard_map/ppermute | solution.py:385
  634.3 46.2 %collective-permute-start.43 = (bf16[256,2048]{1,0:T(8,128)(2,1)S(1)}, bf16[256,2048]{1,0:T(8,128)(2,1)S(1)}, u32[]{:S(2)}, u32[]{:S(2)}) collective-permute-start(bf16[256,2048]{1,0:T(8,128)(2,1)S(1)} %get-tuple-element.89.refs_0_), channel_id=1, source_target_pairs={{0,8},{8,16},{16,24},{24,0},{1,9},{9,17},{17,25},{25,1},{2,10},{10... | collective-permute-start | bytes 3145736 | tf_op jit(solution)/shard_map/ppermute | solution.py:382
  635.5 47.5 %collective-permute-start.45 = (bf16[256,2048]{1,0:T(8,128)(2,1)S(1)}, bf16[256,2048]{1,0:T(8,128)(2,1)S(1)}, u32[]{:S(2)}, u32[]{:S(2)}) collective-permute-start(bf16[256,2048]{1,0:T(8,128)(2,1)S(1)} %get-tuple-element.89.refs_0_), channel_id=1, source_target_pairs={{0,24},{8,0},{16,8},{24,16},{1,25},{9,1},{17,9},{25,17},{2,26},{10... | collective-permute-start | bytes 3145736 | tf_op jit(solution)/shard_map/ppermute | solution.py:385
  637.7 39.1 %collective-permute-start.39 = (f32[128,2048]{1,0:T(8,128)}, f32[128,2048]{1,0:T(8,128)S(1)}, u32[]{:S(2)}, u32[]{:S(2)}) collective-permute-start(f32[128,2048]{1,0:T(8,128)} %get-tuple-element.104), channel_id=1, source_target_pairs={{0,8},{8,16},{16,24},{24,0},{1,9},{9,17},{17,25},{25,1},{2,10},{10... | collective-permute-start | bytes 3145736 | tf_op jit(solution)/shard_map/ppermute | solution.py:382
  637.7 46.3 %collective-permute-start.41 = (f32[128,2048]{1,0:T(8,128)}, f32[128,2048]{1,0:T(8,128)S(1)}, u32[]{:S(2)}, u32[]{:S(2)}) collective-permute-start(f32[128,2048]{1,0:T(8,128)} %get-tuple-element.105), channel_id=1, source_target_pairs={{0,24},{8,0},{16,8},{24,16},{1,25},{9,1},{17,9},{25,17},{2,26},{10... | collective-permute-start | bytes 3145736 | tf_op jit(solution)/shard_map/ppermute | solution.py:385
  680.0 100.2 %collective-permute-start.40 = (f32[256,2048]{1,0:T(8,128)}, f32[256,2048]{1,0:T(8,128)S(1)}, u32[]{:S(2)}, u32[]{:S(2)}) collective-permute-start(f32[256,2048]{1,0:T(8,128)} %pad_maximum_fusion.5), channel_id=1, source_target_pairs={{0,8},{8,16},{16,24},{24,0},{1,9},{9,17},{17,25},{25,1},{2,10},{10... | collective-permute-start | bytes 6291464 | tf_op jit(solution)/shard_map/ppermute | solution.py:382
  680.5 49.6 %collective-permute-start.44 = (bf16[128,2048]{1,0:T(8,128)(2,1)S(1)}, bf16[128,2048]{1,0:T(8,128)(2,1)S(1)}, u32[]{:S(2)}, u32[]{:S(2)}) collective-permute-start(bf16[128,2048]{1,0:T(8,128)(2,1)S(1)} %slice.282), channel_id=1, source_target_pairs={{0,8},{8,16},{16,24},{24,0},{1,9},{9,17},{17,25},{25,1},{2,10},{10... | collective-permute-start | bytes 1572872 | tf_op jit(solution)/shard_map/ppermute | solution.py:382
  683.1 47.1 %collective-permute-start.46 = (bf16[128,2048]{1,0:T(8,128)(2,1)S(1)}, bf16[128,2048]{1,0:T(8,128)(2,1)S(1)}, u32[]{:S(2)}, u32[]{:S(2)}) collective-permute-start(bf16[128,2048]{1,0:T(8,128)(2,1)S(1)} %slice.283), channel_id=1, source_target_pairs={{0,24},{8,0},{16,8},{24,16},{1,25},{9,1},{17,9},{25,17},{2,26},{10... | collective-permute-start | bytes 1572872 | tf_op jit(solution)/shard_map/ppermute | solution.py:385
  685.8 94.4 %collective-permute-start.42 = (f32[256,2048]{1,0:T(8,128)}, f32[256,2048]{1,0:T(8,128)}, u32[]{:S(2)}, u32[]{:S(2)}) collective-permute-start(f32[256,2048]{1,0:T(8,128)} %pad_maximum_fusion.6), channel_id=1, source_target_pairs={{0,24},{8,0},{16,8},{24,16},{1,25},{9,1},{17,9},{25,17},{2,26},{10... | collective-permute-start | bytes 6291464 | tf_op jit(solution)/shard_map/ppermute | solution.py:385
  745.4 29.0 %collective-permute-start.47 = (f32[128,2048]{1,0:T(8,128)}, f32[128,2048]{1,0:T(8,128)S(1)}, u32[]{:S(2)}, u32[]{:S(2)}) collective-permute-start(f32[128,2048]{1,0:T(8,128)} %get-tuple-element.110), channel_id=1, source_target_pairs={{0,8},{8,16},{16,24},{24,0},{1,9},{9,17},{17,25},{25,1},{2,10},{10... | collective-permute-start | bytes 3145736 | tf_op jit(solution)/shard_map/ppermute | solution.py:382
  745.4 31.1 %collective-permute-start.49 = (f32[128,2048]{1,0:T(8,128)S(1)}, f32[128,2048]{1,0:T(8,128)S(1)}, u32[]{:S(2)}, u32[]{:S(2)}) collective-permute-start(f32[128,2048]{1,0:T(8,128)S(1)} %get-tuple-element.111), channel_id=1, source_target_pairs={{0,24},{8,0},{16,8},{24,16},{1,25},{9,1},{17,9},{25,17},{2,26},{10... | collective-permute-start | bytes 3145736 | tf_op jit(solution)/shard_map/ppermute | solution.py:385
  776.3 37.4 %collective-permute-start.48 = (f32[256,2048]{1,0:T(8,128)S(1)}, f32[256,2048]{1,0:T(8,128)S(1)}, u32[]{:S(2)}, u32[]{:S(2)}) collective-permute-start(f32[256,2048]{1,0:T(8,128)S(1)} %pad_maximum_fusion.7), channel_id=1, source_target_pairs={{0,8},{8,16},{16,24},{24,0},{1,9},{9,17},{17,25},{25,1},{2,10},{10... | collective-permute-start | bytes 6291464 | tf_op jit(solution)/shard_map/ppermute | solution.py:382
  778.2 36.2 %collective-permute-start.50 = (f32[256,2048]{1,0:T(8,128)S(1)}, f32[256,2048]{1,0:T(8,128)S(1)}, u32[]{:S(2)}, u32[]{:S(2)}) collective-permute-start(f32[256,2048]{1,0:T(8,128)S(1)} %pad_maximum_fusion.8), channel_id=1, source_target_pairs={{0,24},{8,0},{16,8},{24,16},{1,25},{9,1},{17,9},{25,17},{2,26},{10... | collective-permute-start | bytes 6291464 | tf_op jit(solution)/shard_map/ppermute | solution.py:385
  (52 other events, 419.8 us)
Sparse Core Ops, SparseCore 0:
  13.9 26.9 all-gather.28
  42.5 21.5 all-gather.20
  65.7 67.6 all-gather.22
  134.9 47.3 all-gather.24
  183.7 51.7 all-gather.26
  237.0 65.0 all-gather.18
  303.7 47.2 all-gather.30
  352.6 47.2 all-gather.32
  401.6 47.2 all-gather.34
  450.3 51.7 all-gather.36

commit v3 on v2

--- a/solution.py
+++ b/solution.py
@@ -217,23 +217,23 @@
 
     @pl.when(step >= n_act)
     def _():
-        rows = outs[0].shape[0]
         blk = act_scr.shape[2]
         part = None
         for i in range(n_act):
             term = jnp.dot(act_scr[i], wd_ref[i * blk:(i + 1) * blk], preferred_element_type=jnp.float32)
             part = term if part is None else part + term
-        for i, ref in enumerate(outs):
-            ref[...] = part[i * rows:(i + 1) * rows]
-
-
-def mlp_call(pieces, n_out, w_g, w_u, w_d, blk=512, blk2=512):
+        at = 0
+        for ref in outs:
+            ref[...] = part[at:at + ref.shape[0]]
+            at += ref.shape[0]
+
+
+def mlp_call(pieces, out_rows, w_g, w_u, w_d, blk=512, blk2=512):
     embed, ffn = w_g.shape
     total = sum(p.shape[0] for p in pieces)
-    rows = total // n_out
     n_act = ffn // blk
     return pl.pallas_call(
-        functools.partial(mlp_kernel, len(pieces), n_out, n_act),
+        functools.partial(mlp_kernel, len(pieces), len(out_rows), n_act),
         name="mlp",
         grid=(n_act + embed // blk2,),
         in_specs=[pl.BlockSpec(p.shape, lambda f: (0, 0)) for p in pieces]
@@ -242,8 +242,8 @@
             pl.BlockSpec((embed, blk), lambda f: (0, jnp.minimum(f, n_act - 1))),
             pl.BlockSpec((ffn, blk2), lambda f: (0, jnp.maximum(f - n_act, 0))),
         ],
-        out_specs=[pl.BlockSpec((rows, blk2), lambda f: (0, jnp.maximum(f - n_act, 0)))] * n_out,
-        out_shape=[jax.ShapeDtypeStruct((rows, embed), jnp.float32)] * n_out,
+        out_specs=[pl.BlockSpec((r, blk2), lambda f: (0, jnp.maximum(f - n_act, 0))) for r in out_rows],
+        out_shape=[jax.ShapeDtypeStruct((r, embed), jnp.float32) for r in out_rows],
         scratch_shapes=[pltpu.VMEM((total, embed), jnp.bfloat16), pltpu.VMEM((n_act, total, blk), jnp.bfloat16)],
         compiler_params=pltpu.CompilerParams(dimension_semantics=("arbitrary",), vmem_limit_bytes=48 * 1024 * 1024),
         cost_estimate=pl.CostEstimate(
@@ -460,20 +460,21 @@
         def opp_step(st, l):
             lo, hi = st['hids'][3:]
             lo = in_turn(lo)
-            (p_opp,) = mlp_call([lo, hi], 1, *weights[l][2:])
-            st['opp_in'] = to_right(p_opp[:half]), to_left(p_opp[half:])
-            last[0] = p_opp
+            p_lo, p_hi = mlp_call([lo, hi], [half, half], *weights[l][2:])
+            st['opp_in'] = to_right(p_lo), to_left(p_hi)
+            last[0] = p_lo
 
         def near_step(st, l):
             own, left, right = st['hids'][:3]
             left = in_turn(left)
-            p_own, p_left, p_right = mlp_call([own, left, right], 3, *weights[l][2:])
+            p_own, left_lo, left_hi, right_lo, right_hi = mlp_call([own, left, right], [rows] + [half] * 4, *weights[l][2:])
             last[0] = p_own
             lo_in, hi_in = st['opp_in']
-            p_right = jnp.concatenate([p_right[:half] + lo_in, p_right[half:]], axis=0)
-            p_left = jnp.concatenate([p_left[:half], p_left[half:] + hi_in], axis=0)
-            st['relay'] = p_right
-            st['resid'] = st['resid'] + p_own + to_right(p_right) + to_left(p_left)
+            hi_sum = to_right(right_hi)
+            lo_sum = to_left(left_lo)
+            lo_sum = lo_sum + to_right(right_lo + lo_in)
+            hi_sum = hi_sum + to_left(left_hi + hi_in)
+            st['resid'] = st['resid'] + p_own + jnp.concatenate([lo_sum, hi_sum], axis=0)
 
         a, b = streams
         for l in range(layers):

time: 835 us -> 787 us (0.943)
  the two profiles are of different devices: /device:TPU:98 before, /device:TPU:96 now
where the time goes in v3:
time: 787 us; the launch traced here: 778 us
  Pallas kernels  396 us (50%)
  waiting for transfers between devices  212 us (27%)
  starting transfers between devices  93.2 us (12%)
  local copies, waits for them, and re-layouts  35.9 us (5%)
  other arithmetic  25.8 us (3%)
  between operations  15.2 us (2%)
    pallas_call x8, Pallas kernels, mlp_call(): pl.pallas_call(functools.partial(mlp_kernel, len(pieces), len(out_rows),...  165 us
    ppermute x30, waiting for transfers between devices, to_right(): return lax.ppermute(value, 'mp', fwd)  143 us
    pallas_call x4, Pallas kernels, attn_call(): pl.pallas_call(functools.partial(attn_kernel, LOG2_E * head_dim ** (-0.5)...  103 us
    pallas_call x1, Pallas kernels, gather_call(): pl.pallas_call(functools.partial(gather_kernel, mp_n, tok_n // 2, n), nam...  95.5 us
    ppermute x29, starting transfers between devices, to_left(): return lax.ppermute(value, 'mp', bwd)  79.6 us
    all_gather x10, waiting for transfers between devices, gathered(): return lax.all_gather(value, axis_name, **how)  42.1 us
    pallas_call x4, Pallas kernels, qkv_call(): pl.pallas_call(functools.partial(qkv_kernel, q_w, kv_w), name='qkv', grid...  32.3 us
    ppermute x29, waiting for transfers between devices, to_left(): return lax.ppermute(value, 'mp', bwd)  25.2 us
  transfers between devices with their start and end apart: 69, of which 22 were waited for; matrix products, arithmetic and copies ran while one was open for 4% of the time, Pallas kernels for 48%

profile of v3, /device:TPU:96, one launch (start us, length us, event | category | flops | bytes accessed | tf_op | source)
XLA Modules:
  0.0 778.3 jit_solution(4229702750948221314)
XLA Ops:
  16.5 3.2 fusion.9
  21.5 19.0 %all-gather.29.cloned.1.call-done = bf16[1024,768]{1,0:T(8,128)(2,1)} async-done(((bf16[256,768]{1,0:T(8,128)(2,1)}), bf16[1024,768]{1,0:T(8,128)(2,1)}) %all-gather.29.cloned.1.call-update) | async-done | bytes 1572880 | tf_op jit(solution)/shard_map/all_gather | solution.py:416
  40.6 23.0 %all-gather.21.cloned.1.call-done = bf16[4,512,256]{2,1,0:T(8,128)(2,1)} async-done(((bf16[1,512,256]{2,1,0:T(8,128)(2,1)}), bf16[4,512,256]{2,1,0:T(8,128)(2,1)}) %all-gather.21.cloned.1.call-update) | async-done | bytes 1048592 | tf_op jit(solution)/shard_map/all_gather | solution.py:416
  65.7 2.9 collective-permute-start.1
  69.2 3.4 bitcast_convert_fusion
  73.6 4.7 collective-permute-done.2
  80.5 95.5 %gather_weights.1 = (bf16[4,8,256,768]{3,2,1,0:T(8,128)(2,1)}, bf16[4,8,512,256]{3,2,1,0:T(8,128)(2,1)}) custom-call(bf16[256,768]{1,0:T(8,128)(2,1)} %pad_maximum_fusion.1.refs_0_, bf16[512,256]{1,0:T(8,128)(2,1)} %bitcast.65), custom_call_target="tpu_custom_call" | custom-call | flops 99999997952 | bytes 20971520 | tf_op jit(solution)/shard_map/gather_weights/pallas_call | solution.py:356
  177.6 7.9 %qkv.4 = (bf16[4,256,512]{2,1,0:T(8,128)(2,1)S(1)}, bf16[4,256,256]{2,1,0:T(8,128)(2,1)S(1)}) custom-call(f32[256,2048]{1,0:T(8,128)S(1)} %copy-done, bf16[1,2048]{1,0:T(2,128)(2,1)S(1)} %get-tuple-element.153.gain_ref, f32[256,128]{1,0:T(8,128)S(1)} %pad_maximum_fusion.3.cos_ref, f32[256,128]{1,0:T(8,128)S(1)} %pad_maximum_fusion.4.sin_ref, ...), custom_call_target="tpu_custom_call" | custom-call | flops 3221225472 | bytes 12582912 | tf_op jit(solution)/shard_map/qkv/pallas_call | solution.py:63
  185.5 2.8 collective-permute-start.3
  189.7 8.3 %qkv.5 = (bf16[4,256,512]{2,1,0:T(8,128)(2,1)S(1)}, bf16[4,256,256]{2,1,0:T(8,128)(2,1)S(1)}) custom-call(f32[256,2048]{1,0:T(8,128)S(1)} %get-tuple-element.74.resid_ref, bf16[1,2048]{1,0:T(2,128)(2,1)S(1)} %get-tuple-element.153.gain_ref, f32[256,128]{1,0:T(8,128)S(1)} %pad_maximum_fusion.5.cos_ref, f32[256,128]{1,0:T(8,128)S(1)} %pad_maximum_fusion.6.sin_ref, ...), custom_call_target="tpu_custom_call" | custom-call | flops 3221225472 | bytes 12582912 | tf_op jit(solution)/shard_map/qkv/pallas_call | solution.py:63
  198.7 2.6 collective-permute-start.10
  203.3 2.5 collective-permute-start.6
  206.3 7.8 %collective-permute-done.9.left_ref = bf16[4,256,256]{2,1,0:T(8,128)(2,1)S(1)} collective-permute-done((bf16[4,256,256]{2,1,0:T(8,128)(2,1)S(1)}, bf16[4,256,256]{2,1,0:T(8,128)(2,1)S(1)}, u32[]{:S(2)}, u32[]{:S(2)}) %collective-permute-start.9) | collective-permute-done | bytes 524320 | tf_op jit(solution)/shard_map/ppermute | solution.py:382
  214.5 3.3 collective-permute-start.12
  220.0 26.3 %attn.4 = (f32[256,2048]{1,0:T(8,128)S(1)}, bf16[256,2048]{1,0:T(8,128)(2,1)S(1)}) custom-call(bf16[4,256,512]{2,1,0:T(8,128)(2,1)S(1)} %get-tuple-element.76.q_ref, bf16[4,256,256]{2,1,0:T(8,128)(2,1)S(1)} %get-tuple-element.73.own_ref, bf16[4,256,256]{2,1,0:T(8,128)(2,1)S(1)} %collective-permute-done.3.left_ref, ...), custom_call_target="tpu_custom_call" | custom-call | flops 10737418240 | bytes 8388608 | tf_op jit(solution)/shard_map/attn/pallas_call | solution.py:164
  246.8 2.9 collective-permute-start.13
  249.7 25.9 %attn.5 = (f32[256,2048]{1,0:T(8,128)S(1)}, bf16[256,2048]{1,0:T(8,128)(2,1)S(1)}) custom-call(bf16[4,256,512]{2,1,0:T(8,128)(2,1)S(1)} %get-tuple-element.81.q_ref, bf16[4,256,256]{2,1,0:T(8,128)(2,1)S(1)} %get-tuple-element.75.own_ref, bf16[4,256,256]{2,1,0:T(8,128)(2,1)S(1)} %collective-permute-done.9.left_ref, ...), custom_call_target="tpu_custom_call" | custom-call | flops 10737418240 | bytes 8388608 | tf_op jit(solution)/shard_map/attn/pallas_call | solution.py:164
  275.8 3.2 collective-permute-start.23
  279.2 3.3 collective-permute-start.14
  282.5 29.1 %collective-permute-done.8.refs_0_ = bf16[128,2048]{1,0:T(8,128)(2,1)S(1)} collective-permute-done((bf16[128,2048]{1,0:T(8,128)(2,1)S(1)}, bf16[128,2048]{1,0:T(8,128)(2,1)S(1)}, u32[]{:S(2)}, u32[]{:S(2)}) %collective-permute-start.8) | collective-permute-done | bytes 524320 | tf_op jit(solution)/shard_map/ppermute | solution.py:382
  312.8 3.1 collective-permute-start.24
  316.0 14.4 %mlp.8 = (f32[128,2048]{1,0:T(8,128)S(1)}, f32[128,2048]{1,0:T(8,128)S(1)}) custom-call(bf16[128,2048]{1,0:T(8,128)(2,1)S(1)} %collective-permute-done.8.refs_0_, bf16[128,2048]{1,0:T(8,128)(2,1)S(1)} %collective-permute-done.14.refs_1_, bf16[2048,2048]{1,0:T(8,128)(2,1)} %bitcast.45, bf16[2048,2048]{1,0:T(8,128)(2,1)} %bitcast.49, bf16[2048,2048]{1,0:T(8,128)(2,1)} %bitcast.53), custom_call_target="tpu_custom_call" | custom-call | flops 6442450944 | bytes 25165824 | tf_op jit(solution)/shard_map/mlp/pallas_call | solution.py:235
  330.6 3.6 collective-permute-start.19
  334.2 26.9 %mlp.9 = (f32[256,2048]{1,0:T(8,128)}, f32[128,2048]{1,0:T(8,128)S(1)}, f32[128,2048]{1,0:T(8,128)S(1)}, f32[128,2048]{1,0:T(8,128)S(1)}, f32[128,2048]{1,0:T(8,128)S(1)}) custom-call(bf16[256,2048]{1,0:T(8,128)(2,1)S(1)} %copy-done.29, bf16[256,2048]{1,0:T(8,128)(2,1)} %copy-done.53, bf16[256,2048]{1,0:T(8,128)(2,1)} %copy-done.55, ...), custom_call_target="tpu_custom_call" | custom-call | flops 19327352832 | bytes 25165824 | tf_op jit(solution)/shard_map/mlp/pallas_call | solution.py:235
  363.1 15.2 %mlp.10 = (f32[128,2048]{1,0:T(8,128)}, f32[128,2048]{1,0:T(8,128)}) custom-call(bf16[128,2048]{1,0:T(8,128)(2,1)S(1)} %collective-permute-done.22.refs_0_, bf16[128,2048]{1,0:T(8,128)(2,1)S(1)} %collective-permute-done.24.refs_1_, bf16[2048,2048]{1,0:T(8,128)(2,1)} %bitcast.47, bf16[2048,2048]{1,0:T(8,128)(2,1)} %bitcast.51, bf16[2048,2048]{1,0:T(8,128)(2,1)} %bitcast.55), custom_call_target="tpu_custom_call" | custom-call | flops 6442450944 | bytes 25165824 | tf_op jit(solution)/shard_map/mlp/pallas_call | solution.py:235
  379.4 3.3 collective-permute-start.20
  382.6 27.0 %mlp.11 = (f32[256,2048]{1,0:T(8,128)}, f32[128,2048]{1,0:T(8,128)}, f32[128,2048]{1,0:T(8,128)S(1)}, f32[128,2048]{1,0:T(8,128)S(1)}, f32[128,2048]{1,0:T(8,128)}) custom-call(bf16[256,2048]{1,0:T(8,128)(2,1)S(1)} %copy-done.27, bf16[256,2048]{1,0:T(8,128)(2,1)} %copy-done.51, bf16[256,2048]{1,0:T(8,128)(2,1)} %copy-done.52, bf16[2048,2048]{1,0:T(8,128)(2,1)} %bitcast.48, ...), custom_call_target="tpu_custom_call" | custom-call | flops 19327352832 | bytes 25165824 | tf_op jit(solution)/shard_map/mlp/pallas_call | solution.py:235
  411.1 18.0 %collective-permute-done.17 = f32[128,2048]{1,0:T(8,128)S(1)} collective-permute-done((f32[128,2048]{1,0:T(8,128)S(1)}, f32[128,2048]{1,0:T(8,128)S(1)}, u32[]{:S(2)}, u32[]{:S(2)}) %collective-permute-start.17) | collective-permute-done | bytes 1048608 | tf_op jit(solution)/shard_map/ppermute | solution.py:382
  431.9 8.2 %qkv.6 = (bf16[4,256,512]{2,1,0:T(8,128)(2,1)S(1)}, bf16[4,256,256]{2,1,0:T(8,128)(2,1)S(1)}) custom-call(f32[256,2048]{1,0:T(8,128)S(1)} %maximum_add_fusion.resid_ref, bf16[1,2048]{1,0:T(2,128)(2,1)S(1)} %get-tuple-element.152.gain_ref, f32[256,128]{1,0:T(8,128)S(1)} %pad_maximum_fusion.3.cos_ref, f32[256,128]{1,0:T(8,128)S(1)} %pad_maximum_fusion.4.sin_ref, ...), custom_call_target="tpu_custom_call" | custom-call | flops 3221225472 | bytes 12582912 | tf_op jit(solution)/shard_map/qkv/pallas_call | solution.py:63
  441.6 2.7 collective-permute-start.26
  444.4 7.9 %collective-permute-done.25.left_ref = bf16[4,256,256]{2,1,0:T(8,128)(2,1)S(1)} collective-permute-done((bf16[4,256,256]{2,1,0:T(8,128)(2,1)S(1)}, bf16[4,256,256]{2,1,0:T(8,128)(2,1)S(1)}, u32[]{:S(2)}, u32[]{:S(2)}) %collective-permute-start.25) | collective-permute-done | bytes 524320 | tf_op jit(solution)/shard_map/ppermute | solution.py:382
  454.6 3.2 collective-permute-start.28
  457.9 2.0 collective-permute-start.33
  459.9 2.4 add.146
  462.5 2.4 add.148
  465.7 3.1 collective-permute-start.35
  474.0 25.8 %attn.6 = (f32[256,2048]{1,0:T(8,128)S(1)}, bf16[256,2048]{1,0:T(8,128)(2,1)S(1)}) custom-call(bf16[4,256,512]{2,1,0:T(8,128)(2,1)S(1)} %copy-done.33, bf16[4,256,256]{2,1,0:T(8,128)(2,1)S(1)} %copy-done.37, bf16[4,256,256]{2,1,0:T(8,128)(2,1)S(1)} %copy-done.21, bf16[4,256,256]{2,1,0:T(8,128)(2,1)S(1)} %copy-done.23, bf16[2,256,256]{2,1,0:T(8,128)(2,1)S(1)} %copy-done.39, ...), custom_call_target="tpu_custom_call" | custom-call | flops 10737418240 | bytes 8388608 | tf_op jit(solution)/shard_map/attn/pallas_call | solution.py:164
  500.0 3.2 collective-permute-start.37
  503.2 5.3 collective-permute-done.32
  513.2 7.9 %qkv.7 = (bf16[4,256,512]{2,1,0:T(8,128)(2,1)S(1)}, bf16[4,256,256]{2,1,0:T(8,128)(2,1)S(1)}) custom-call(f32[256,2048]{1,0:T(8,128)S(1)} %maximum_add_fusion.1.resid_ref, bf16[1,2048]{1,0:T(2,128)(2,1)S(1)} %get-tuple-element.152.gain_ref, f32[256,128]{1,0:T(8,128)S(1)} %pad_maximum_fusion.5.cos_ref, f32[256,128]{1,0:T(8,128)S(1)} %pad_maximum_fusion.6.sin_ref, ...), custom_call_target="tpu_custom_call" | custom-call | flops 3221225472 | bytes 12582912 | tf_op jit(solution)/shard_map/qkv/pallas_call | solution.py:63
  522.2 3.1 collective-permute-start.40
  525.3 5.6 collective-permute-done.29.refs_1_
  533.1 3.7 collective-permute-start.38
  536.7 5.4 collective-permute-done.39.left_ref
  544.2 3.9 collective-permute-start.42
  548.1 4.0 collective-permute-done.36.refs_0_
  552.2 14.2 %mlp.12 = (f32[128,2048]{1,0:T(8,128)S(1)}, f32[128,2048]{1,0:T(8,128)S(1)}) custom-call(bf16[128,2048]{1,0:T(8,128)(2,1)S(1)} %collective-permute-done.36.refs_0_, bf16[128,2048]{1,0:T(8,128)(2,1)S(1)} %collective-permute-done.38.refs_1_, bf16[2048,2048]{1,0:T(8,128)(2,1)} %bitcast.33, bf16[2048,2048]{1,0:T(8,128)(2,1)} %bitcast.37, bf16[2048,2048]{1,0:T(8,128)(2,1)} %bitcast.41), custom_call_target="tpu_custom_call" | custom-call | flops 6442450944 | bytes 25165824 | tf_op jit(solution)/shard_map/mlp/pallas_call | solution.py:235
  566.4 25.3 %attn.7 = (f32[256,2048]{1,0:T(8,128)S(1)}, bf16[256,2048]{1,0:T(8,128)(2,1)S(1)}) custom-call(bf16[4,256,512]{2,1,0:T(8,128)(2,1)S(1)} %copy-done.31, bf16[4,256,256]{2,1,0:T(8,128)(2,1)S(1)} %copy-done.35, bf16[4,256,256]{2,1,0:T(8,128)(2,1)S(1)} %copy-done.17, bf16[4,256,256]{2,1,0:T(8,128)(2,1)S(1)} %copy-done.19, ...), custom_call_target="tpu_custom_call" | custom-call | flops 10737418240 | bytes 8388608 | tf_op jit(solution)/shard_map/attn/pallas_call | solution.py:164
  591.9 3.2 collective-permute-start.51
  595.1 3.2 collective-permute-start.47
  598.3 20.8 %collective-permute-done.49.refs_1_ = bf16[256,2048]{1,0:T(8,128)(2,1)S(1)} collective-permute-done((bf16[256,2048]{1,0:T(8,128)(2,1)S(1)}, bf16[256,2048]{1,0:T(8,128)(2,1)S(1)}, u32[]{:S(2)}, u32[]{:S(2)}) %collective-permute-start.49) | collective-permute-done | bytes 1048608 | tf_op jit(solution)/shard_map/ppermute | solution.py:382
  620.5 3.0 collective-permute-start.52
  623.5 26.6 %mlp.13 = (f32[256,2048]{1,0:T(8,128)}, f32[128,2048]{1,0:T(8,128)S(1)}, f32[128,2048]{1,0:T(8,128)S(1)}, f32[128,2048]{1,0:T(8,128)S(1)}, f32[128,2048]{1,0:T(8,128)S(1)}) custom-call(bf16[256,2048]{1,0:T(8,128)(2,1)S(1)} %copy-done.25, bf16[256,2048]{1,0:T(8,128)(2,1)} %copy-done.49, bf16[256,2048]{1,0:T(8,128)(2,1)} %copy-done.50, ...), custom_call_target="tpu_custom_call" | custom-call | flops 19327352832 | bytes 25165824 | tf_op jit(solution)/shard_map/mlp/pallas_call | solution.py:235
  650.1 14.0 %mlp.14 = (f32[128,2048]{1,0:T(8,128)S(1)}, f32[128,2048]{1,0:T(8,128)S(1)}) custom-call(bf16[128,2048]{1,0:T(8,128)(2,1)S(1)} %collective-permute-done.50.refs_0_, bf16[128,2048]{1,0:T(8,128)(2,1)S(1)} %collective-permute-done.52.refs_1_, bf16[2048,2048]{1,0:T(8,128)(2,1)} %bitcast.35, bf16[2048,2048]{1,0:T(8,128)(2,1)} %bitcast.39, bf16[2048,2048]{1,0:T(8,128)(2,1)} %bitcast.43), custom_call_target="tpu_custom_call" | custom-call | flops 6442450944 | bytes 25165824 | tf_op jit(solution)/shard_map/mlp/pallas_call | solution.py:235
  664.3 3.2 collective-permute-start.43
  668.7 3.3 collective-permute-start.48
  672.1 19.4 %collective-permute-done.54 = f32[128,2048]{1,0:T(8,128)S(1)} collective-permute-done((f32[128,2048]{1,0:T(8,128)S(1)}, f32[128,2048]{1,0:T(8,128)S(1)}, u32[]{:S(2)}, u32[]{:S(2)}) %collective-permute-start.54) | collective-permute-done | bytes 1048608 | tf_op jit(solution)/shard_map/ppermute | solution.py:382
  692.8 26.7 %mlp.15 = (f32[256,2048]{1,0:T(8,128)}, f32[128,2048]{1,0:T(8,128)S(1)}, f32[128,2048]{1,0:T(8,128)S(1)}, f32[128,2048]{1,0:T(8,128)S(1)}, f32[128,2048]{1,0:T(8,128)S(1)}) custom-call(bf16[256,2048]{1,0:T(8,128)(2,1)S(1)} %get-tuple-element.114.refs_0_, bf16[256,2048]{1,0:T(8,128)(2,1)} %copy-done.54, bf16[256,2048]{1,0:T(8,128)(2,1)} %copy-done.56, ...), custom_call_target="tpu_custom_call" | custom-call | flops 19327352832 | bytes 25165824 | tf_op jit(solution)/shard_map/mlp/pallas_call | solution.py:235
  719.6 12.4 %collective-permute-done.57 = f32[128,2048]{1,0:T(8,128)} collective-permute-done((f32[128,2048]{1,0:T(8,128)S(1)}, f32[128,2048]{1,0:T(8,128)}, u32[]{:S(2)}, u32[]{:S(2)}) %collective-permute-start.57) | collective-permute-done | bytes 1048608 | tf_op jit(solution)/shard_map/ppermute | solution.py:385
  732.1 3.8 collective-permute-start.53
  737.5 3.2 collective-permute-start.58
  744.5 11.2 %collective-permute-done.53 = f32[128,2048]{1,0:T(8,128)S(1)} collective-permute-done((f32[128,2048]{1,0:T(8,128)S(1)}, f32[128,2048]{1,0:T(8,128)S(1)}, u32[]{:S(2)}, u32[]{:S(2)}) %collective-permute-start.53) | collective-permute-done | bytes 1048608 | tf_op jit(solution)/shard_map/ppermute | solution.py:385
  756.6 11.1 %collective-permute-done.56 = f32[128,2048]{1,0:T(8,128)S(1)} collective-permute-done((f32[128,2048]{1,0:T(8,128)S(1)}, f32[128,2048]{1,0:T(8,128)S(1)}, u32[]{:S(2)}, u32[]{:S(2)}) %collective-permute-start.56) | collective-permute-done | bytes 1048608 | tf_op jit(solution)/shard_map/ppermute | solution.py:382
  768.5 2.5 pad_maximum_fusion
  (296 shorter events, 66.9 us)
Async XLA Ops:
  6.5 33.9 %all-gather.29.cloned.1.call-start = ((), (), s32[]{:S(2)}) async-start(), calls=%async_computation.5 | async-start | bytes 1966080 | tf_op jit(solution)/shard_map/all_gather | solution.py:416
  13.8 49.8 %all-gather.21.cloned.1.call-start = ((), (), s32[]{:S(2)}) async-start(), calls=%async_computation.1 | async-start | bytes 1310720 | tf_op jit(solution)/shard_map/all_gather | solution.py:416
  14.7 301.2 %all-gather.23.cloned.1.call-start = ((), (), s32[]{:S(2)}) async-start(), calls=%async_computation.2 | async-start | bytes 9437184 | tf_op jit(solution)/shard_map/all_gather | solution.py:416
  16.4 299.5 %all-gather.25.cloned.1.call-start = ((), (), s32[]{:S(2)}) async-start(), calls=%async_computation.3 | async-start | bytes 9437184 | tf_op jit(solution)/shard_map/all_gather | solution.py:416
  19.8 296.2 %all-gather.27.cloned.1.call-start = ((), (), s32[]{:S(2)}) async-start(), calls=%async_computation.4 | async-start | bytes 9437184 | tf_op jit(solution)/shard_map/all_gather | solution.py:416
  21.4 410.5 %all-gather.19.cloned.1.call-start = ((), (), s32[]{:S(2)}) async-start(), calls=%async_computation | async-start | bytes 14155776 | tf_op jit(solution)/shard_map/all_gather | solution.py:416
  40.5 428.2 %all-gather.31.cloned.1.call-start = ((), (), s32[]{:S(2)}) async-start(), calls=%async_computation.6 | async-start | bytes 9437184 | tf_op jit(solution)/shard_map/all_gather | solution.py:416
  63.7 488.4 %all-gather.33.cloned.1.call-start = ((), (), s32[]{:S(2)}) async-start(), calls=%async_computation.7 | async-start | bytes 9437184 | tf_op jit(solution)/shard_map/all_gather | solution.py:416
  64.5 487.6 %all-gather.35.cloned.1.call-start = ((), (), s32[]{:S(2)}) async-start(), calls=%async_computation.8 | async-start | bytes 9437184 | tf_op jit(solution)/shard_map/all_gather | solution.py:416
  65.3 486.8 %all-gather.37.cloned.1.call-start = ((), (), s32[]{:S(2)}) async-start(), calls=%async_computation.9 | async-start | bytes 9437184 | tf_op jit(solution)/shard_map/all_gather | solution.py:416
  185.5 16.8 %collective-permute-start.3 = (bf16[4,256,256]{2,1,0:T(8,128)(2,1)S(1)}, bf16[4,256,256]{2,1,0:T(8,128)(2,1)S(1)}, u32[]{:S(2)}, u32[]{:S(2)}) collective-permute-start(bf16[4,256,256]{2,1,0:T(8,128)(2,1)S(1)} %get-tuple-element.73.own_ref), channel_id=1, source_target_pairs={{0,8},{8,16},{16,24},{24,0},{1,9},{9,17},{17,25},{25,1},{2,10},{10... | collective-permute-start | bytes 1572872 | tf_op jit(solution)/shard_map/ppermute | solution.py:382
  188.3 14.9 %collective-permute-start.4 = (bf16[4,256,256]{2,1,0:T(8,128)(2,1)S(1)}, bf16[4,256,256]{2,1,0:T(8,128)(2,1)S(1)}, u32[]{:S(2)}, u32[]{:S(2)}) collective-permute-start(bf16[4,256,256]{2,1,0:T(8,128)(2,1)S(1)} %get-tuple-element.73.own_ref), channel_id=1, source_target_pairs={{0,24},{8,0},{16,8},{24,16},{1,25},{9,1},{17,9},{25,17},{2,26},{10... | collective-permute-start | bytes 1572872 | tf_op jit(solution)/shard_map/ppermute | solution.py:385
  198.0 16.1 %collective-permute-start.9 = (bf16[4,256,256]{2,1,0:T(8,128)(2,1)S(1)}, bf16[4,256,256]{2,1,0:T(8,128)(2,1)S(1)}, u32[]{:S(2)}, u32[]{:S(2)}) collective-permute-start(bf16[4,256,256]{2,1,0:T(8,128)(2,1)S(1)} %get-tuple-element.75.own_ref), channel_id=1, source_target_pairs={{0,8},{8,16},{16,24},{24,0},{1,9},{9,17},{17,25},{25,1},{2,10},{10... | collective-permute-start | bytes 1572872 | tf_op jit(solution)/shard_map/ppermute | solution.py:382
  198.7 15.8 %collective-permute-start.10 = (bf16[4,256,256]{2,1,0:T(8,128)(2,1)S(1)}, bf16[4,256,256]{2,1,0:T(8,128)(2,1)S(1)}, u32[]{:S(2)}, u32[]{:S(2)}) collective-permute-start(bf16[4,256,256]{2,1,0:T(8,128)(2,1)S(1)} %get-tuple-element.75.own_ref), channel_id=1, source_target_pairs={{0,24},{8,0},{16,8},{24,16},{1,25},{9,1},{17,9},{25,17},{2,26},{10... | collective-permute-start | bytes 1572872 | tf_op jit(solution)/shard_map/ppermute | solution.py:385
  202.4 17.4 %collective-permute-start.5 = (bf16[2,256,256]{2,1,0:T(8,128)(2,1)S(1)}, bf16[2,256,256]{2,1,0:T(8,128)(2,1)S(1)}, u32[]{:S(2)}, u32[]{:S(2)}) collective-permute-start(bf16[2,256,256]{2,1,0:T(8,128)(2,1)S(1)} %slice.166), channel_id=1, source_target_pairs={{0,8},{8,16},{16,24},{24,0},{1,9},{9,17},{17,25},{25,1},{2,10},{10... | collective-permute-start | bytes 786440 | tf_op jit(solution)/shard_map/ppermute | solution.py:382
  203.3 16.7 %collective-permute-start.6 = (bf16[2,256,256]{2,1,0:T(8,128)(2,1)S(1)}, bf16[2,256,256]{2,1,0:T(8,128)(2,1)S(1)}, u32[]{:S(2)}, u32[]{:S(2)}) collective-permute-start(bf16[2,256,256]{2,1,0:T(8,128)(2,1)S(1)} %slice.167), channel_id=1, source_target_pairs={{0,24},{8,0},{16,8},{24,16},{1,25},{9,1},{17,9},{25,17},{2,26},{10... | collective-permute-start | bytes 786440 | tf_op jit(solution)/shard_map/ppermute | solution.py:385
  214.1 35.5 %collective-permute-start.11 = (bf16[2,256,256]{2,1,0:T(8,128)(2,1)S(1)}, bf16[2,256,256]{2,1,0:T(8,128)(2,1)S(1)}, u32[]{:S(2)}, u32[]{:S(2)}) collective-permute-start(bf16[2,256,256]{2,1,0:T(8,128)(2,1)S(1)} %slice.169), channel_id=1, source_target_pairs={{0,8},{8,16},{16,24},{24,0},{1,9},{9,17},{17,25},{25,1},{2,10},{10... | collective-permute-start | bytes 786440 | tf_op jit(solution)/shard_map/ppermute | solution.py:382
  214.5 35.1 %collective-permute-start.12 = (bf16[2,256,256]{2,1,0:T(8,128)(2,1)S(1)}, bf16[2,256,256]{2,1,0:T(8,128)(2,1)S(1)}, u32[]{:S(2)}, u32[]{:S(2)}) collective-permute-start(bf16[2,256,256]{2,1,0:T(8,128)(2,1)S(1)} %slice.170), channel_id=1, source_target_pairs={{0,24},{8,0},{16,8},{24,16},{1,25},{9,1},{17,9},{25,17},{2,26},{10... | collective-permute-start | bytes 786440 | tf_op jit(solution)/shard_map/ppermute | solution.py:385
  246.3 29.3 %collective-permute-start.7 = (bf16[256,2048]{1,0:T(8,128)(2,1)S(1)}, bf16[256,2048]{1,0:T(8,128)(2,1)S(1)}, u32[]{:S(2)}, u32[]{:S(2)}) collective-permute-start(bf16[256,2048]{1,0:T(8,128)(2,1)S(1)} %get-tuple-element.79.refs_0_), channel_id=1, source_target_pairs={{0,8},{8,16},{16,24},{24,0},{1,9},{9,17},{17,25},{25,1},{2,10},{10... | collective-permute-start | bytes 3145736 | tf_op jit(solution)/shard_map/ppermute | solution.py:382
  246.8 28.9 %collective-permute-start.13 = (bf16[256,2048]{1,0:T(8,128)(2,1)S(1)}, bf16[256,2048]{1,0:T(8,128)(2,1)S(1)}, u32[]{:S(2)}, u32[]{:S(2)}) collective-permute-start(bf16[256,2048]{1,0:T(8,128)(2,1)S(1)} %get-tuple-element.79.refs_0_), channel_id=1, source_target_pairs={{0,24},{8,0},{16,8},{24,16},{1,25},{9,1},{17,9},{25,17},{2,26},{10... | collective-permute-start | bytes 3145736 | tf_op jit(solution)/shard_map/ppermute | solution.py:385
  275.7 35.9 %collective-permute-start.21 = (bf16[256,2048]{1,0:T(8,128)(2,1)S(1)}, bf16[256,2048]{1,0:T(8,128)(2,1)S(1)}, u32[]{:S(2)}, u32[]{:S(2)}) collective-permute-start(bf16[256,2048]{1,0:T(8,128)(2,1)S(1)} %get-tuple-element.92.refs_0_), channel_id=1, source_target_pairs={{0,8},{8,16},{16,24},{24,0},{1,9},{9,17},{17,25},{25,1},{2,10},{10... | collective-permute-start | bytes 3145736 | tf_op jit(solution)/shard_map/ppermute | solution.py:382
  275.8 35.9 %collective-permute-start.23 = (bf16[256,2048]{1,0:T(8,128)(2,1)S(1)}, bf16[256,2048]{1,0:T(8,128)(2,1)S(1)}, u32[]{:S(2)}, u32[]{:S(2)}) collective-permute-start(bf16[256,2048]{1,0:T(8,128)(2,1)S(1)} %get-tuple-element.92.refs_0_), channel_id=1, source_target_pairs={{0,24},{8,0},{16,8},{24,16},{1,25},{9,1},{17,9},{25,17},{2,26},{10... | collective-permute-start | bytes 3145736 | tf_op jit(solution)/shard_map/ppermute | solution.py:385
  279.1 32.5 %collective-permute-start.8 = (bf16[128,2048]{1,0:T(8,128)(2,1)S(1)}, bf16[128,2048]{1,0:T(8,128)(2,1)S(1)}, u32[]{:S(2)}, u32[]{:S(2)}) collective-permute-start(bf16[128,2048]{1,0:T(8,128)(2,1)S(1)} %slice.168), channel_id=1, source_target_pairs={{0,8},{8,16},{16,24},{24,0},{1,9},{9,17},{17,25},{25,1},{2,10},{10... | collective-permute-start | bytes 1572872 | tf_op jit(solution)/shard_map/ppermute | solution.py:382
  279.2 36.7 %collective-permute-start.14 = (bf16[128,2048]{1,0:T(8,128)(2,1)S(1)}, bf16[128,2048]{1,0:T(8,128)(2,1)S(1)}, u32[]{:S(2)}, u32[]{:S(2)}) collective-permute-start(bf16[128,2048]{1,0:T(8,128)(2,1)S(1)} %slice.171), channel_id=1, source_target_pairs={{0,24},{8,0},{16,8},{24,16},{1,25},{9,1},{17,9},{25,17},{2,26},{10... | collective-permute-start | bytes 1572872 | tf_op jit(solution)/shard_map/ppermute | solution.py:385
  311.6 49.5 %collective-permute-start.22 = (bf16[128,2048]{1,0:T(8,128)(2,1)S(1)}, bf16[128,2048]{1,0:T(8,128)(2,1)S(1)}, u32[]{:S(2)}, u32[]{:S(2)}) collective-permute-start(bf16[128,2048]{1,0:T(8,128)(2,1)S(1)} %slice.172), channel_id=1, source_target_pairs={{0,8},{8,16},{16,24},{24,0},{1,9},{9,17},{17,25},{25,1},{2,10},{10... | collective-permute-start | bytes 1572872 | tf_op jit(solution)/shard_map/ppermute | solution.py:382
  312.8 50.3 %collective-permute-start.24 = (bf16[128,2048]{1,0:T(8,128)(2,1)}, bf16[128,2048]{1,0:T(8,128)(2,1)S(1)}, u32[]{:S(2)}, u32[]{:S(2)}) collective-permute-start(bf16[128,2048]{1,0:T(8,128)(2,1)} %slice.173), channel_id=1, source_target_pairs={{0,24},{8,0},{16,8},{24,16},{1,25},{9,1},{17,9},{25,17},{2,26},{10... | collective-permute-start | bytes 1572872 | tf_op jit(solution)/shard_map/ppermute | solution.py:385
  330.5 48.5 %collective-permute-start.16 = (f32[128,2048]{1,0:T(8,128)S(1)}, f32[128,2048]{1,0:T(8,128)S(1)}, u32[]{:S(2)}, u32[]{:S(2)}) collective-permute-start(f32[128,2048]{1,0:T(8,128)S(1)} %get-tuple-element.84), channel_id=1, source_target_pairs={{0,8},{8,16},{16,24},{24,0},{1,9},{9,17},{17,25},{25,1},{2,10},{10... | collective-permute-start | bytes 3145736 | tf_op jit(solution)/shard_map/ppermute | solution.py:382
  330.6 48.6 %collective-permute-start.19 = (f32[128,2048]{1,0:T(8,128)S(1)}, f32[128,2048]{1,0:T(8,128)S(1)}, u32[]{:S(2)}, u32[]{:S(2)}) collective-permute-start(f32[128,2048]{1,0:T(8,128)S(1)} %get-tuple-element.91), channel_id=1, source_target_pairs={{0,24},{8,0},{16,8},{24,16},{1,25},{9,1},{17,9},{25,17},{2,26},{10... | collective-permute-start | bytes 3145736 | tf_op jit(solution)/shard_map/ppermute | solution.py:385
  361.1 48.6 %collective-permute-start.15 = (f32[128,2048]{1,0:T(8,128)S(1)}, f32[128,2048]{1,0:T(8,128)S(1)}, u32[]{:S(2)}, u32[]{:S(2)}) collective-permute-start(f32[128,2048]{1,0:T(8,128)S(1)} %get-tuple-element.87), channel_id=1, source_target_pairs={{0,24},{8,0},{16,8},{24,16},{1,25},{9,1},{17,9},{25,17},{2,26},{10... | collective-permute-start | bytes 3145736 | tf_op jit(solution)/shard_map/ppermute | solution.py:385
  361.1 68.1 %collective-permute-start.18 = (f32[128,2048]{1,0:T(8,128)S(1)}, f32[128,2048]{1,0:T(8,128)S(1)}, u32[]{:S(2)}, u32[]{:S(2)}) collective-permute-start(f32[128,2048]{1,0:T(8,128)S(1)} %get-tuple-element.89), channel_id=1, source_target_pairs={{0,8},{8,16},{16,24},{24,0},{1,9},{9,17},{17,25},{25,1},{2,10},{10... | collective-permute-start | bytes 3145736 | tf_op jit(solution)/shard_map/ppermute | solution.py:382
  378.3 79.6 %collective-permute-start.31 = (f32[128,2048]{1,0:T(8,128)}, f32[128,2048]{1,0:T(8,128)}, u32[]{:S(2)}, u32[]{:S(2)}) collective-permute-start(f32[128,2048]{1,0:T(8,128)} %get-tuple-element.94), channel_id=1, source_target_pairs={{0,8},{8,16},{16,24},{24,0},{1,9},{9,17},{17,25},{25,1},{2,10},{10... | collective-permute-start | bytes 3145736 | tf_op jit(solution)/shard_map/ppermute | solution.py:382
  379.1 50.0 %collective-permute-start.17 = (f32[128,2048]{1,0:T(8,128)S(1)}, f32[128,2048]{1,0:T(8,128)S(1)}, u32[]{:S(2)}, u32[]{:S(2)}) collective-permute-start(f32[128,2048]{1,0:T(8,128)S(1)} %add.140), channel_id=1, source_target_pairs={{0,8},{8,16},{16,24},{24,0},{1,9},{9,17},{17,25},{25,1},{2,10},{10... | collective-permute-start | bytes 3145736 | tf_op jit(solution)/shard_map/ppermute | solution.py:382
  379.4 49.9 %collective-permute-start.20 = (f32[128,2048]{1,0:T(8,128)S(1)}, f32[128,2048]{1,0:T(8,128)S(1)}, u32[]{:S(2)}, u32[]{:S(2)}) collective-permute-start(f32[128,2048]{1,0:T(8,128)S(1)} %add.142), channel_id=1, source_target_pairs={{0,24},{8,0},{16,8},{24,16},{1,25},{9,1},{17,9},{25,17},{2,26},{10... | collective-permute-start | bytes 3145736 | tf_op jit(solution)/shard_map/ppermute | solution.py:385
  409.6 52.6 %collective-permute-start.34 = (f32[128,2048]{1,0:T(8,128)}, f32[128,2048]{1,0:T(8,128)}, u32[]{:S(2)}, u32[]{:S(2)}) collective-permute-start(f32[128,2048]{1,0:T(8,128)} %get-tuple-element.107), channel_id=1, source_target_pairs={{0,24},{8,0},{16,8},{24,16},{1,25},{9,1},{17,9},{25,17},{2,26},{10... | collective-permute-start | bytes 3145736 | tf_op jit(solution)/shard_map/ppermute | solution.py:385
  453.1 11.8 %collective-permute-start.27 = (bf16[2,256,256]{2,1,0:T(8,128)(2,1)S(1)}, bf16[2,256,256]{2,1,0:T(8,128)(2,1)S(1)}, u32[]{:S(2)}, u32[]{:S(2)}) collective-permute-start(bf16[2,256,256]{2,1,0:T(8,128)(2,1)S(1)} %slice.174), channel_id=1, source_target_pairs={{0,8},{8,16},{16,24},{24,0},{1,9},{9,17},{17,25},{25,1},{2,10},{10... | collective-permute-start | bytes 786440 | tf_op jit(solution)/shard_map/ppermute | solution.py:382
  454.6 14.1 %collective-permute-start.28 = (bf16[2,256,256]{2,1,0:T(8,128)(2,1)}, bf16[2,256,256]{2,1,0:T(8,128)(2,1)}, u32[]{:S(2)}, u32[]{:S(2)}) collective-permute-start(bf16[2,256,256]{2,1,0:T(8,128)(2,1)} %slice.175), channel_id=1, source_target_pairs={{0,24},{8,0},{16,8},{24,16},{1,25},{9,1},{17,9},{25,17},{2,26},{10... | collective-permute-start | bytes 786440 | tf_op jit(solution)/shard_map/ppermute | solution.py:385
  457.9 42.1 %collective-permute-start.30 = (f32[128,2048]{1,0:T(8,128)}, f32[128,2048]{1,0:T(8,128)}, u32[]{:S(2)}, u32[]{:S(2)}) collective-permute-start(f32[128,2048]{1,0:T(8,128)} %get-tuple-element.103), channel_id=1, source_target_pairs={{0,24},{8,0},{16,8},{24,16},{1,25},{9,1},{17,9},{25,17},{2,26},{10... | collective-permute-start | bytes 3145736 | tf_op jit(solution)/shard_map/ppermute | solution.py:385
  457.9 52.5 %collective-permute-start.33 = (f32[128,2048]{1,0:T(8,128)}, f32[128,2048]{1,0:T(8,128)}, u32[]{:S(2)}, u32[]{:S(2)}) collective-permute-start(f32[128,2048]{1,0:T(8,128)} %get-tuple-element.105), channel_id=1, source_target_pairs={{0,8},{8,16},{16,24},{24,0},{1,9},{9,17},{17,25},{25,1},{2,10},{10... | collective-permute-start | bytes 3145736 | tf_op jit(solution)/shard_map/ppermute | solution.py:382
  462.3 46.3 %collective-permute-start.32 = (f32[128,2048]{1,0:T(8,128)}, f32[128,2048]{1,0:T(8,128)}, u32[]{:S(2)}, u32[]{:S(2)}) collective-permute-start(f32[128,2048]{1,0:T(8,128)} %add.146), channel_id=1, source_target_pairs={{0,8},{8,16},{16,24},{24,0},{1,9},{9,17},{17,25},{25,1},{2,10},{10... | collective-permute-start | bytes 3145736 | tf_op jit(solution)/shard_map/ppermute | solution.py:382
  465.7 44.7 %collective-permute-start.35 = (f32[128,2048]{1,0:T(8,128)}, f32[128,2048]{1,0:T(8,128)}, u32[]{:S(2)}, u32[]{:S(2)}) collective-permute-start(f32[128,2048]{1,0:T(8,128)} %add.148), channel_id=1, source_target_pairs={{0,24},{8,0},{16,8},{24,16},{1,25},{9,1},{17,9},{25,17},{2,26},{10... | collective-permute-start | bytes 3145736 | tf_op jit(solution)/shard_map/ppermute | solution.py:385
  499.9 31.0 %collective-permute-start.29 = (bf16[256,2048]{1,0:T(8,128)(2,1)S(1)}, bf16[256,2048]{1,0:T(8,128)(2,1)S(1)}, u32[]{:S(2)}, u32[]{:S(2)}) collective-permute-start(bf16[256,2048]{1,0:T(8,128)(2,1)S(1)} %get-tuple-element.101.refs_0_), channel_id=1, source_target_pairs={{0,8},{8,16},{16,24},{24,0},{1,9},{9,17},{17,25},{25,1},{2,10},{10... | collective-permute-start | bytes 3145736 | tf_op jit(solution)/shard_map/ppermute | solution.py:382
  500.0 32.2 %collective-permute-start.37 = (bf16[256,2048]{1,0:T(8,128)(2,1)S(1)}, bf16[256,2048]{1,0:T(8,128)(2,1)S(1)}, u32[]{:S(2)}, u32[]{:S(2)}) collective-permute-start(bf16[256,2048]{1,0:T(8,128)(2,1)S(1)} %get-tuple-element.101.refs_0_), channel_id=1, source_target_pairs={{0,24},{8,0},{16,8},{24,16},{1,25},{9,1},{17,9},{25,17},{2,26},{10... | collective-permute-start | bytes 3145736 | tf_op jit(solution)/shard_map/ppermute | solution.py:385
  522.1 20.1 %collective-permute-start.39 = (bf16[4,256,256]{2,1,0:T(8,128)(2,1)S(1)}, bf16[4,256,256]{2,1,0:T(8,128)(2,1)S(1)}, u32[]{:S(2)}, u32[]{:S(2)}) collective-permute-start(bf16[4,256,256]{2,1,0:T(8,128)(2,1)S(1)} %get-tuple-element.110.own_ref), channel_id=1, source_target_pairs={{0,8},{8,16},{16,24},{24,0},{1,9},{9,17},{17,25},{25,1},{2,10},{10... | collective-permute-start | bytes 1572872 | tf_op jit(solution)/shard_map/ppermute | solution.py:382
  522.2 21.2 %collective-permute-start.40 = (bf16[4,256,256]{2,1,0:T(8,128)(2,1)S(1)}, bf16[4,256,256]{2,1,0:T(8,128)(2,1)S(1)}, u32[]{:S(2)}, u32[]{:S(2)}) collective-permute-start(bf16[4,256,256]{2,1,0:T(8,128)(2,1)S(1)} %get-tuple-element.110.own_ref), channel_id=1, source_target_pairs={{0,24},{8,0},{16,8},{24,16},{1,25},{9,1},{17,9},{25,17},{2,26},{10... | collective-permute-start | bytes 1572872 | tf_op jit(solution)/shard_map/ppermute | solution.py:385
  530.9 21.2 %collective-permute-start.36 = (bf16[128,2048]{1,0:T(8,128)(2,1)S(1)}, bf16[128,2048]{1,0:T(8,128)(2,1)S(1)}, u32[]{:S(2)}, u32[]{:S(2)}) collective-permute-start(bf16[128,2048]{1,0:T(8,128)(2,1)S(1)} %slice.176), channel_id=1, source_target_pairs={{0,8},{8,16},{16,24},{24,0},{1,9},{9,17},{17,25},{25,1},{2,10},{10... | collective-permute-start | bytes 1572872 | tf_op jit(solution)/shard_map/ppermute | solution.py:382
  533.1 19.1 %collective-permute-start.38 = (bf16[128,2048]{1,0:T(8,128)(2,1)}, bf16[128,2048]{1,0:T(8,128)(2,1)S(1)}, u32[]{:S(2)}, u32[]{:S(2)}) collective-permute-start(bf16[128,2048]{1,0:T(8,128)(2,1)} %slice.177), channel_id=1, source_target_pairs={{0,24},{8,0},{16,8},{24,16},{1,25},{9,1},{17,9},{25,17},{2,26},{10... | collective-permute-start | bytes 1572872 | tf_op jit(solution)/shard_map/ppermute | solution.py:385
  542.9 23.5 %collective-permute-start.41 = (bf16[2,256,256]{2,1,0:T(8,128)(2,1)}, bf16[2,256,256]{2,1,0:T(8,128)(2,1)S(1)}, u32[]{:S(2)}, u32[]{:S(2)}) collective-permute-start(bf16[2,256,256]{2,1,0:T(8,128)(2,1)} %slice.178), channel_id=1, source_target_pairs={{0,8},{8,16},{16,24},{24,0},{1,9},{9,17},{17,25},{25,1},{2,10},{10... | collective-permute-start | bytes 786440 | tf_op jit(solution)/shard_map/ppermute | solution.py:382
  544.2 22.2 %collective-permute-start.42 = (bf16[2,256,256]{2,1,0:T(8,128)(2,1)}, bf16[2,256,256]{2,1,0:T(8,128)(2,1)}, u32[]{:S(2)}, u32[]{:S(2)}) collective-permute-start(bf16[2,256,256]{2,1,0:T(8,128)(2,1)} %slice.179), channel_id=1, source_target_pairs={{0,24},{8,0},{16,8},{24,16},{1,25},{9,1},{17,9},{25,17},{2,26},{10... | collective-permute-start | bytes 786440 | tf_op jit(solution)/shard_map/ppermute | solution.py:385
  591.8 27.3 %collective-permute-start.49 = (bf16[256,2048]{1,0:T(8,128)(2,1)S(1)}, bf16[256,2048]{1,0:T(8,128)(2,1)S(1)}, u32[]{:S(2)}, u32[]{:S(2)}) collective-permute-start(bf16[256,2048]{1,0:T(8,128)(2,1)S(1)} %get-tuple-element.114.refs_0_), channel_id=1, source_target_pairs={{0,8},{8,16},{16,24},{24,0},{1,9},{9,17},{17,25},{25,1},{2,10},{10... | collective-permute-start | bytes 3145736 | tf_op jit(solution)/shard_map/ppermute | solution.py:382
  591.9 27.3 %collective-permute-start.51 = (bf16[256,2048]{1,0:T(8,128)(2,1)S(1)}, bf16[256,2048]{1,0:T(8,128)(2,1)S(1)}, u32[]{:S(2)}, u32[]{:S(2)}) collective-permute-start(bf16[256,2048]{1,0:T(8,128)(2,1)S(1)} %get-tuple-element.114.refs_0_), channel_id=1, source_target_pairs={{0,24},{8,0},{16,8},{24,16},{1,25},{9,1},{17,9},{25,17},{2,26},{10... | collective-permute-start | bytes 3145736 | tf_op jit(solution)/shard_map/ppermute | solution.py:385
  595.1 72.4 %collective-permute-start.44 = (f32[128,2048]{1,0:T(8,128)S(1)}, f32[128,2048]{1,0:T(8,128)S(1)}, u32[]{:S(2)}, u32[]{:S(2)}) collective-permute-start(f32[128,2048]{1,0:T(8,128)S(1)} %get-tuple-element.112), channel_id=1, source_target_pairs={{0,8},{8,16},{16,24},{24,0},{1,9},{9,17},{17,25},{25,1},{2,10},{10... | collective-permute-start | bytes 3145736 | tf_op jit(solution)/shard_map/ppermute | solution.py:382
  595.1 73.5 %collective-permute-start.47 = (f32[128,2048]{1,0:T(8,128)S(1)}, f32[128,2048]{1,0:T(8,128)S(1)}, u32[]{:S(2)}, u32[]{:S(2)}) collective-permute-start(f32[128,2048]{1,0:T(8,128)S(1)} %get-tuple-element.121), channel_id=1, source_target_pairs={{0,24},{8,0},{16,8},{24,16},{1,25},{9,1},{17,9},{25,17},{2,26},{10... | collective-permute-start | bytes 3145736 | tf_op jit(solution)/shard_map/ppermute | solution.py:385
  619.1 31.0 %collective-permute-start.50 = (bf16[128,2048]{1,0:T(8,128)(2,1)S(1)}, bf16[128,2048]{1,0:T(8,128)(2,1)S(1)}, u32[]{:S(2)}, u32[]{:S(2)}) collective-permute-start(bf16[128,2048]{1,0:T(8,128)(2,1)S(1)} %slice.180), channel_id=1, source_target_pairs={{0,8},{8,16},{16,24},{24,0},{1,9},{9,17},{17,25},{25,1},{2,10},{10... | collective-permute-start | bytes 1572872 | tf_op jit(solution)/shard_map/ppermute | solution.py:382
  620.5 29.6 %collective-permute-start.52 = (bf16[128,2048]{1,0:T(8,128)(2,1)S(1)}, bf16[128,2048]{1,0:T(8,128)(2,1)S(1)}, u32[]{:S(2)}, u32[]{:S(2)}) collective-permute-start(bf16[128,2048]{1,0:T(8,128)(2,1)S(1)} %slice.181), channel_id=1, source_target_pairs={{0,24},{8,0},{16,8},{24,16},{1,25},{9,1},{17,9},{25,17},{2,26},{10... | collective-permute-start | bytes 1572872 | tf_op jit(solution)/shard_map/ppermute | solution.py:385
  664.2 27.3 %collective-permute-start.54 = (f32[128,2048]{1,0:T(8,128)S(1)}, f32[128,2048]{1,0:T(8,128)S(1)}, u32[]{:S(2)}, u32[]{:S(2)}) collective-permute-start(f32[128,2048]{1,0:T(8,128)S(1)} %get-tuple-element.124), channel_id=1, source_target_pairs={{0,8},{8,16},{16,24},{24,0},{1,9},{9,17},{17,25},{25,1},{2,10},{10... | collective-permute-start | bytes 3145736 | tf_op jit(solution)/shard_map/ppermute | solution.py:382
  664.3 72.9 %collective-permute-start.43 = (f32[128,2048]{1,0:T(8,128)S(1)}, f32[128,2048]{1,0:T(8,128)}, u32[]{:S(2)}, u32[]{:S(2)}) collective-permute-start(f32[128,2048]{1,0:T(8,128)S(1)} %get-tuple-element.117), channel_id=1, source_target_pairs={{0,24},{8,0},{16,8},{24,16},{1,25},{9,1},{17,9},{25,17},{2,26},{10... | collective-permute-start | bytes 3145736 | tf_op jit(solution)/shard_map/ppermute | solution.py:385
  667.5 69.9 %collective-permute-start.46 = (f32[128,2048]{1,0:T(8,128)S(1)}, f32[128,2048]{1,0:T(8,128)S(1)}, u32[]{:S(2)}, u32[]{:S(2)}) collective-permute-start(f32[128,2048]{1,0:T(8,128)S(1)} %get-tuple-element.119), channel_id=1, source_target_pairs={{0,8},{8,16},{16,24},{24,0},{1,9},{9,17},{17,25},{25,1},{2,10},{10... | collective-permute-start | bytes 3145736 | tf_op jit(solution)/shard_map/ppermute | solution.py:382
  668.6 68.9 %collective-permute-start.45 = (f32[128,2048]{1,0:T(8,128)}, f32[128,2048]{1,0:T(8,128)S(1)}, u32[]{:S(2)}, u32[]{:S(2)}) collective-permute-start(f32[128,2048]{1,0:T(8,128)} %add.152), channel_id=1, source_target_pairs={{0,8},{8,16},{16,24},{24,0},{1,9},{9,17},{17,25},{25,1},{2,10},{10... | collective-permute-start | bytes 3145736 | tf_op jit(solution)/shard_map/ppermute | solution.py:382
  668.7 73.5 %collective-permute-start.48 = (f32[128,2048]{1,0:T(8,128)S(1)}, f32[128,2048]{1,0:T(8,128)S(1)}, u32[]{:S(2)}, u32[]{:S(2)}) collective-permute-start(f32[128,2048]{1,0:T(8,128)S(1)} %add.154), channel_id=1, source_target_pairs={{0,24},{8,0},{16,8},{24,16},{1,25},{9,1},{17,9},{25,17},{2,26},{10... | collective-permute-start | bytes 3145736 | tf_op jit(solution)/shard_map/ppermute | solution.py:385
  692.5 39.5 %collective-permute-start.57 = (f32[128,2048]{1,0:T(8,128)S(1)}, f32[128,2048]{1,0:T(8,128)}, u32[]{:S(2)}, u32[]{:S(2)}) collective-permute-start(f32[128,2048]{1,0:T(8,128)S(1)} %get-tuple-element.131), channel_id=1, source_target_pairs={{0,24},{8,0},{16,8},{24,16},{1,25},{9,1},{17,9},{25,17},{2,26},{10... | collective-permute-start | bytes 3145736 | tf_op jit(solution)/shard_map/ppermute | solution.py:385
  732.1 23.6 %collective-permute-start.53 = (f32[128,2048]{1,0:T(8,128)S(1)}, f32[128,2048]{1,0:T(8,128)S(1)}, u32[]{:S(2)}, u32[]{:S(2)}) collective-permute-start(f32[128,2048]{1,0:T(8,128)S(1)} %get-tuple-element.127), channel_id=1, source_target_pairs={{0,24},{8,0},{16,8},{24,16},{1,25},{9,1},{17,9},{25,17},{2,26},{10... | collective-permute-start | bytes 3145736 | tf_op jit(solution)/shard_map/ppermute | solution.py:385
  737.2 19.2 %collective-permute-start.55 = (f32[128,2048]{1,0:T(8,128)S(1)}, f32[128,2048]{1,0:T(8,128)S(1)}, u32[]{:S(2)}, u32[]{:S(2)}) collective-permute-start(f32[128,2048]{1,0:T(8,128)S(1)} %add.158), channel_id=1, source_target_pairs={{0,8},{8,16},{16,24},{24,0},{1,9},{9,17},{17,25},{25,1},{2,10},{10... | collective-permute-start | bytes 3145736 | tf_op jit(solution)/shard_map/ppermute | solution.py:382
  737.4 30.3 %collective-permute-start.56 = (f32[128,2048]{1,0:T(8,128)S(1)}, f32[128,2048]{1,0:T(8,128)S(1)}, u32[]{:S(2)}, u32[]{:S(2)}) collective-permute-start(f32[128,2048]{1,0:T(8,128)S(1)} %get-tuple-element.129), channel_id=1, source_target_pairs={{0,8},{8,16},{16,24},{24,0},{1,9},{9,17},{17,25},{25,1},{2,10},{10... | collective-permute-start | bytes 3145736 | tf_op jit(solution)/shard_map/ppermute | solution.py:382
  737.5 30.2 %collective-permute-start.58 = (f32[128,2048]{1,0:T(8,128)S(1)}, f32[128,2048]{1,0:T(8,128)S(1)}, u32[]{:S(2)}, u32[]{:S(2)}) collective-permute-start(f32[128,2048]{1,0:T(8,128)S(1)} %add.160), channel_id=1, source_target_pairs={{0,24},{8,0},{16,8},{24,16},{1,25},{9,1},{17,9},{25,17},{2,26},{10... | collective-permute-start | bytes 3145736 | tf_op jit(solution)/shard_map/ppermute | solution.py:385
  (65 other events, 820.6 us)
Sparse Core Ops, SparseCore 0:
  13.9 26.5 all-gather.28
  42.0 21.5 all-gather.20
  65.2 68.8 all-gather.22
  135.6 46.8 all-gather.24
  183.9 51.0 all-gather.26
  236.4 65.8 all-gather.18
  303.9 47.4 all-gather.30
  353.1 47.2 all-gather.32
  402.0 47.2 all-gather.34
  450.7 51.0 all-gather.36
